TPU v7x, 32 devices: a whole 2x2x4 slice. The times are simulated.
32 devices in a mesh: gx: 4 (over z), gy: 4 (over x, core), gz: 2 (over y).
Axes of the slice: x: 2, y: 2, z: 4, core: 2. Of those that a mesh axis runs over, the one named last changes fastest.
Arguments:
- positions: float32 [3, 4, 4, 2, 128], P(None, 'gx', 'gy', 'gz'), may hold values from 0 to 24, as said below
- occupancy: int32 [4, 4, 2, 128], P('gx', 'gy', 'gz'), may hold values from 0 to 1
- neighbours: int32 [56, 4, 4, 2, 128], P(None, 'gx', 'gy', 'gz'), may hold values from 0 to 639, as said below
- keep: int32 [56, 4, 4, 2, 128], P(None, 'gx', 'gy', 'gz'), may hold values from 0 to 1, as said below
- face_x: int32 [4, 4, 2, 2, 64], P('gx', 'gy', 'gz'), may hold values from 0 to 127, as said below
- face_y: int32 [4, 4, 2, 2, 128], P('gx', 'gy', 'gz'), may hold values from 0 to 255, as said below
- face_z: int32 [4, 4, 2, 128], P('gx', 'gy', 'gz'), may hold values from 0 to 511, as said below
- radial_one: float32 [8, 128], replicated, may hold values from -2 to 2
- mix_one: bfloat16 [384, 128], replicated, may hold values from -0.3125 to 0.3125
- embed: float32 [128], replicated, may hold values from -3 to 3
- radial_two: float32 [8, 128], replicated, may hold values from -3 to 3
- mix_two: bfloat16 [384, 128], replicated, may hold values from -0.3125 to 0.3125
- read_one: float32 [128], replicated, may hold values from -0.4375 to 0.4375
- read_hidden: float32 [128, 16], replicated, may hold values from -0.5 to 0.5
- read_out: float32 [16], replicated, may hold values from -1.5 to 1.5
Outputs:
- energies: float32 [4, 4, 2, 128], P('gx', 'gy', 'gz')
- forces: float32 [3, 4, 4, 2, 128], P(None, 'gx', 'gy', 'gz')
Inputs may be any that keep to these rules, and one draw needn't show every extreme that they name: `positions`: coordinates in angstrom in the box's own frame; any two atoms named by one list entry lie at least 1.4 apart, counted with the periodic images along gx and gy. `neighbours`: Where the neighbour would lie outside the slab, the entry names the atom at the opposite offset and keep is 0. `keep`: 0 where the atom's slot or the neighbour's slot is empty, or the entry is a pad. `face_x`: distinct own slots; entry 0 lists the slots seen by the lower box, entry 1 by the higher box. `face_y`: distinct rows of the own and x-ghost part of the list; entry 0 for the lower box along gy, entry 1 for the higher. `face_z`: distinct rows of the own, x- and y-ghost part of the list, seen by the other box along gz.
All inputs are finite; a program needn't handle non-finite values.
Results may differ from a plain program's by a relative error of at most 0.01.
Values may be sent and summed in bfloat16 or wider, within the bound.
No kernel may reach another device: no remote copies, remote signals or barrier semaphores. Data moves between devices by JAX's collectives and lax.ppermute only.
A program may use at most 128 MiB of HBM per device.

v0:
```python
import math

import jax
import jax.numpy as jnp
from jax import lax
from jax.sharding import PartitionSpec as P

NB = 8
LX = 4
LY = 4
LZ = 8


SPACING = 1.8
CUTOFF = 5.0
SPREAD = 0.4
HIGHEST = lax.Precision.HIGHEST


def extended(block, sides, width):
    for axis, dim in sides:
        count = lax.axis_size(axis)
        forward = [(i, i + 1) for i in range(count - 1)]
        forward.append((count - 1, 0))
        backward = [(target, source) for source, target in forward]
        low = lax.ppermute(
            lax.slice_in_dim(block, block.shape[dim] - width, None, axis=dim), axis, forward
        )
        high = lax.ppermute(lax.slice_in_dim(block, 0, width, axis=dim), axis, backward)
        block = jnp.concatenate([low, block, high], axis=dim)
    return block


def partner(x, axis, stride):
    return lax.ppermute(x, axis, [(i, i ^ 1 << stride) for i in range(lax.axis_size(axis))])


def harmonics(unit_vec):
    unit_x, unit_y, unit_z = (unit_vec[0], unit_vec[1], unit_vec[2])
    root_three = 3.0**0.5
    root_fifteen = 15.0**0.5
    root_five = 5.0**0.5
    return jnp.stack(
        [
            jnp.ones_like(unit_x),
            root_three * unit_x,
            root_three * unit_y,
            root_three * unit_z,
            root_fifteen * unit_x * unit_y,
            root_fifteen * unit_y * unit_z,
            0.5 * root_five * (3.0 * unit_z * unit_z - 1.0),
            root_fifteen * unit_x * unit_z,
            0.5 * root_fifteen * (unit_x * unit_x - unit_y * unit_y),
        ]
    )


def radial_basis(distance):
    orders = jnp.arange(1, NB + 1).astype(jnp.float32)[:, None, None]
    scaled = distance / CUTOFF
    envelope = jnp.where(scaled < 1.0, (1.0 - scaled * scaled) ** 2, 0.0)
    return (2.0 / CUTOFF) ** 0.5 * jnp.sin(orders * jnp.pi * scaled) / distance * envelope


def edge_frame(source, centre, nbr_slots, edge_weight):
    offset_vec = source[:, nbr_slots] - centre[:, None, :]
    distance = jnp.sqrt(jnp.sum(offset_vec * offset_vec, axis=0))
    return (radial_basis(distance) * edge_weight, harmonics(offset_vec / distance))


def moments_one(source, centre, nbr_slots, edge_weight):
    basis, angular = edge_frame(source, centre, nbr_slots, edge_weight)
    return jnp.einsum("kja,mja->kma", basis, angular, precision=HIGHEST)


def invariants(amplitude):
    return jnp.concatenate(
        [
            amplitude[:, 0, :],
            jnp.sum(amplitude[:, 1:4, :] ** 2, axis=1),
            jnp.sum(amplitude[:, 4:9, :] ** 2, axis=1),
        ],
        axis=1,
    )


def layer_one_tail(moments, radial_one, mix_one, embed):
    amplitude = SPREAD * jnp.einsum("kma,kc->amc", moments, radial_one, precision=HIGHEST)
    mixed_in = invariants(amplitude).astype(jnp.bfloat16)
    return jnp.dot(mixed_in, mix_one, preferred_element_type=jnp.float32) + embed


def pick_block(total_rows):
    block_size = min(total_rows, 1152)
    while total_rows % block_size:
        block_size = block_size - 1
    return block_size


def layer_two(
    source,
    features,
    nbr_slots,
    edge_weight,
    occupied,
    radial_two,
    mix_two,
    read_one,
    read_hidden,
    read_out,
):
    edge_count, atom_count = nbr_slots.shape
    block_size = pick_block(atom_count)
    groups = atom_count // block_size
    widened = features.astype(jnp.float32)

    def per_block(pieces):
        block_slots, block_weight, centre, block_occupied, base_rows = pieces
        basis, angular = edge_frame(source, centre, block_slots, block_weight)
        radial = jnp.einsum("kja,kc->jac", basis, radial_two, precision=HIGHEST)
        message = radial * widened[block_slots]
        amplitude = SPREAD * jnp.einsum("mja,jac->amc", angular, message, precision=HIGHEST)
        mixed_rows = (
            jnp.dot(
                invariants(amplitude).astype(jnp.bfloat16),
                mix_two,
                preferred_element_type=jnp.float32,
            )
            + base_rows
        )
        hidden = jax.nn.silu(jnp.dot(mixed_rows, read_hidden, precision=HIGHEST))
        return block_occupied * (
            jnp.dot(base_rows, read_one, precision=HIGHEST)
            + jnp.dot(hidden, read_out, precision=HIGHEST)
        )

    pieces = (
        nbr_slots.reshape(edge_count, groups, block_size).transpose(1, 0, 2),
        edge_weight.reshape(edge_count, groups, block_size).transpose(1, 0, 2),
        source[:, :atom_count].reshape(3, groups, block_size).transpose(1, 0, 2),
        occupied.reshape(groups, block_size),
        widened[:atom_count].reshape(groups, block_size, widened.shape[1]),
    )
    return lax.map(per_block, pieces).reshape(atom_count)


def spread_positions(own_coords, lists_x, lists_y, list_z, upward):
    step_x = jnp.array([LX * SPACING, 0.0, 0.0], jnp.float32)[:, None]
    step_y = jnp.array([0.0, LY * SPACING, 0.0], jnp.float32)[:, None]
    step_z = jnp.array([0.0, 0.0, LZ * SPACING], jnp.float32)[:, None]
    padded = extended(own_coords[:, lists_x], (("gx", 1),), 1)
    widened = jnp.concatenate([own_coords, padded[:, 0] - step_x, padded[:, 3] + step_x], axis=1)
    padded = extended(widened[:, lists_y], (("gy", 1),), 1)
    widened = jnp.concatenate([widened, padded[:, 0] - step_y, padded[:, 3] + step_y], axis=1)
    arrived = partner(widened[:, list_z], "gz", 0)
    return jnp.concatenate([widened, arrived + upward * step_z], axis=1)


def spread_features(own_rows, lists_x, lists_y, list_z):
    padded = extended(own_rows[lists_x], (("gx", 0),), 1)
    widened = jnp.concatenate([own_rows, padded[0], padded[3]], axis=0)
    padded = extended(widened[lists_y], (("gy", 0),), 1)
    widened = jnp.concatenate([widened, padded[0], padded[3]], axis=0)
    arrived = partner(widened[list_z], "gz", 0)
    return jnp.concatenate([widened, arrived], axis=0)


def take_part(values, start, length, atom_axis):
    return lax.slice_in_dim(values, start, start + length, axis=atom_axis)


def add_part(values, slot_list, update, atom_axis):
    if atom_axis == 0:
        return values.at[slot_list].add(update)
    return values.at[:, slot_list].add(update)


def join_flat(parts, lead_dims):
    return jnp.concatenate(
        [part.reshape(part.shape[:lead_dims] + (-1,)) for part in parts], axis=lead_dims
    )


def split_flat(joined, shapes):
    pieces = []
    start = 0
    for shape in shapes:
        length = math.prod(shape)
        pieces.append(joined.reshape(joined.shape[:-1] + tuple(shape)))
        start = start + length
    return pieces


def fold_back(items, own_count, lists_x, lists_y, list_z):
    x_len = lists_x.shape[1]
    y_len = lists_y.shape[1]
    z_len = list_z.shape[0]
    first_end = own_count + 2 * x_len
    second_end = first_end + 2 * y_len
    axes_of = [atom_axis for values, atom_axis in items]
    inner_rows = [take_part(values, 0, second_end, atom_axis) for values, atom_axis in items]
    outgoing = [take_part(values, second_end, z_len, atom_axis) for values, atom_axis in items]
    arrived = split_flat(
        partner(join_flat(outgoing, 0).astype(jnp.bfloat16), "gz", 0).astype(jnp.float32),
        [part.shape for part in outgoing],
    )
    inner_rows = [
        add_part(rows, list_z, extra, atom_axis)
        for rows, extra, atom_axis in zip(inner_rows, arrived, axes_of)
    ]
    side_rows = [
        jnp.stack(
            [
                take_part(rows, first_end, y_len, atom_axis),
                take_part(rows, first_end + y_len, y_len, atom_axis),
            ]
        )
        for rows, atom_axis in zip(inner_rows, axes_of)
    ]
    padded = extended(join_flat(side_rows, 1).astype(jnp.bfloat16), (("gy", 0),), 1).astype(
        jnp.float32
    )
    shapes = [part.shape[1:] for part in side_rows]
    lower = split_flat(padded[0], shapes)
    upper = split_flat(padded[3], shapes)
    inner_rows = [
        add_part(
            add_part(take_part(rows, 0, first_end, atom_axis), lists_y[0], low_part, atom_axis),
            lists_y[1],
            high_part,
            atom_axis,
        )
        for rows, low_part, high_part, atom_axis in zip(inner_rows, lower, upper, axes_of)
    ]
    side_rows = [
        jnp.stack(
            [
                take_part(rows, own_count, x_len, atom_axis),
                take_part(rows, own_count + x_len, x_len, atom_axis),
            ]
        )
        for rows, atom_axis in zip(inner_rows, axes_of)
    ]
    padded = extended(join_flat(side_rows, 1).astype(jnp.bfloat16), (("gx", 0),), 1).astype(
        jnp.float32
    )
    shapes = [part.shape[1:] for part in side_rows]
    lower = split_flat(padded[0], shapes)
    upper = split_flat(padded[3], shapes)
    return [
        add_part(
            add_part(take_part(rows, 0, own_count, atom_axis), lists_x[0], low_part, atom_axis),
            lists_x[1],
            high_part,
            atom_axis,
        )
        for rows, low_part, high_part, atom_axis in zip(inner_rows, lower, upper, axes_of)
    ]


def per_device(
    positions,
    occupancy,
    neighbours,
    keep,
    face_x,
    face_y,
    face_z,
    radial_one,
    mix_one,
    embed,
    radial_two,
    mix_two,
    read_one,
    read_hidden,
    read_out,
):
    atom_count = positions.shape[-1]
    own_coords = positions.reshape(3, atom_count)
    nbr_slots = neighbours.reshape(neighbours.shape[0], atom_count)
    edge_weight = keep.reshape(nbr_slots.shape).astype(jnp.float32)
    occupied = occupancy.reshape(atom_count).astype(jnp.float32)
    lists_x = face_x.reshape(2, face_x.shape[-1])
    lists_y = face_y.reshape(2, face_y.shape[-1])
    list_z = face_z.reshape(face_z.shape[-1])
    upward = jnp.where(lax.axis_index("gz") == 0, 1.0, -1.0).astype(jnp.float32)
    source = spread_positions(own_coords, lists_x, lists_y, list_z, upward)
    moments, pull_all = jax.vjp(
        lambda coords: moments_one(coords, coords[:, :atom_count], nbr_slots, edge_weight), source
    )
    first_rows, pull_tail = jax.vjp(
        lambda moment_sum: layer_one_tail(moment_sum, radial_one, mix_one, embed), moments
    )
    features = spread_features(first_rows.astype(jnp.bfloat16), lists_x, lists_y, list_z)
    energies, pull_two = jax.vjp(
        lambda coords, feature_rows: layer_two(
            coords,
            feature_rows,
            nbr_slots,
            edge_weight,
            occupied,
            radial_two,
            mix_two,
            read_one,
            read_hidden,
            read_out,
        ),
        source,
        features,
    )
    grad_source, grad_rows = pull_two(jnp.ones_like(energies))
    grad_rows = grad_rows.astype(jnp.float32)
    (grad_moments,) = pull_tail(grad_rows[:atom_count])
    remote_rows = jnp.concatenate(
        [jnp.zeros_like(grad_rows[:atom_count]), grad_rows[atom_count:]], axis=0
    )
    (folded_rows,) = fold_back([(remote_rows, 0)], atom_count, lists_x, lists_y, list_z)
    grad_layer = grad_source
    (extra_grad,) = pull_tail(folded_rows)
    grad_moments = grad_moments + extra_grad
    (from_all,) = pull_all(grad_moments)
    grad_layer = grad_layer + from_all
    (folded_one,) = fold_back([(grad_layer, 1)], atom_count, lists_x, lists_y, list_z)
    forces = -folded_one
    return (energies.reshape(occupancy.shape), forces.reshape(positions.shape))


def solution(mesh):
    return jax.shard_map(
        per_device,
        mesh=mesh,
        in_specs=(
            P(None, "gx", "gy", "gz", None),
            P("gx", "gy", "gz", None),
            P(None, "gx", "gy", "gz", None),
            P(None, "gx", "gy", "gz", None),
            P("gx", "gy", "gz", None, None),
            P("gx", "gy", "gz", None, None),
            P("gx", "gy", "gz", None),
            P(),
            P(),
            P(),
            P(),
            P(),
            P(),
            P(),
            P(),
        ),
        out_specs=(P("gx", "gy", "gz", None), P(None, "gx", "gy", "gz", None)),
        check_vma=False,
    )
```

profile of v0, /device:TPU:0, one launch (start us, length us, event | category | flops | bytes accessed | tf_op | source)
XLA Modules:
  0.0 326.9 jit_solution(15675707168307534303)
XLA Ops:
  3.6 3.1 collective-permute-start
  6.7 2.1 collective-permute-start.1
  17.5 1.9 collective-permute-done.2
  24.0 2.3 collective-permute-done.4
  26.3 24.3 %gather_fusion.3 = f32[7168,3]{1,0:T(8,128)} fusion(f32[3,640]{0,1:T(8,128)S(1)} %add_dynamic-update-slice_fusion, s32[7168]{0:T(1024)S(1)} %broadcast_clamp_fusion), kind=kCustom, calls=%fused_computation.3 | custom fusion | bytes 200704 | tf_op jit(solution)/shard_map/jvp()/gather | solution.py:66
  50.6 2.9 copy.358
  55.7 1.8 convolution_bitcast_fusion
  59.5 3.8 %collective-permute-start.6 = (bf16[1,64,128]{2,1,0:T(8,128)(2,1)S(1)}, bf16[1,64,128]{2,1,0:T(8,128)(2,1)S(1)}, u32[]{:S(2)}, u32[]{:S(2)}) collective-permute-start(bf16[1,64,128]{2,1,0:T(8,128)(2,1)S(1)} %get-tuple-element.515), channel_id=1, source_target_pairs={{8,0},{16,8},{24,16},{0,24},{9,1},{17,9},{25,17},{1,25},{10,2},{18... | collective-permute-start | bytes 49160 | tf_op jit(solution)/shard_map/ppermute | solution.py:29
  66.0 2.2 collective-permute-start.8
  70.5 1.8 collective-permute-start.9
  74.7 24.3 %gather_fusion.7 = f32[7168,128]{1,0:T(8,128)} fusion(f32[640,128]{1,0:T(8,128)S(1)} %convert_element_type.109, s32[7168]{0:T(1024)S(1)} %broadcast_clamp_fusion), kind=kCustom, calls=%fused_computation.7 | custom fusion | bytes 7368704 | tf_op jit(solution)/shard_map/jvp()/while/body/eval_jaxpr/gather | solution.py:121
  99.0 9.4 %fusion.136 = (f32[56,128,128]{2,1,0:T(8,128)S(1)}, f32[56,128,128]{2,1,0:T(8,128)}) fusion(f32[56,128,128]{2,1,0:T(8,128)} %bitcast.278, f32[8,128]{1,0:T(8,128)S(1)} %copy-done.19, f32[56,128]{1,0:T(8,128)S(1)} %bitcast.292, f32[56,128]{1,0:T(8,128)S(1)} %copy.306, f32[56,128]{1,0:T(8,128)S(1)} %copy.303, f32[56,128]{1,0:T(8,128)S(1)} %copy.304, ...), kind=kOutput, calls=%fused_computation.321 | convolution fusion | flops 89284608 | bytes 11128864 | tf_op jit(solution)/shard_map/jvp()/while/body/eval_jaxpr/kja,kc->jac/dot_general | solution.py:120
  108.5 1.8 copy-done.2
  110.3 6.1 %fusion.4 = f32[128,9,128]{2,1,0:T(8,128)} fusion(f32[9,56,128]{1,0,2:T(8,128)S(1)} %copy.307, f32[56,128,128]{2,1,0:T(8,128)S(1)} %get-tuple-element.526), kind=kOutput, calls=%fused_computation.27 | convolution fusion | flops 99090432 | bytes 4517888 | tf_op jit(solution)/shard_map/jvp()/while/body/eval_jaxpr/mja,jac->amc/dot_general | solution.py:122
  116.5 2.3 copy.312
  124.1 10.4 %fusion.2 = f32[128,9,56]{2,1,0:T(8,128)} fusion(f32[128,9,128]{2,1,0:T(8,128)S(1)} %copy.314, f32[56,128,128]{2,1,0:T(8,128)} %copy-done.2), kind=kOutput, calls=%fused_computation.25 | convolution fusion | flops 99090432 | bytes 4517888 | tf_op jit(solution)/shard_map/transpose(jvp())/while/body/eval_jaxpr/mja,jac->amc/dot_general | solution.py:122
  134.5 6.1 %fusion.137 = f32[128,128,56]{1,2,0:T(8,128)S(1)} fusion(f32[128,9,128]{2,1,0:T(8,128)S(1)} %copy.314, f32[9,56,128]{1,0,2:T(8,128)S(1)} %copy.307), kind=kOutput, calls=%fused_computation.322 | convolution fusion | flops 99090432 | bytes 4517888 | tf_op jit(solution)/shard_map/transpose(jvp())/while/body/eval_jaxpr/mja,jac->amc/dot_general | solution.py:122
  140.7 3.0 bitcast_multiply_fusion
  143.7 39.3 %scatter_fusion.1 = f32[640,128]{1,0:T(8,128)S(1)} fusion(f32[640,128]{1,0:T(8,128)S(1)} %pad.69, s32[7168]{0:T(1024)S(1)} %copy-done.9, f32[7168,128]{1,0:T(8,128)} %bitcast.280), kind=kCustom, calls=%fused_computation.9 | custom fusion | flops 917504 | bytes 11038720 | tf_op jit(solution)/shard_map/transpose(jvp())/while/body/eval_jaxpr/scatter-add | solution.py:121
  183.2 2.0 collective-permute-start.10
  185.3 1.9 collective-permute-done.10
  188.9 1.8 collective-permute-start.12
  196.3 3.9 %collective-permute-start.14 = (bf16[1,8192]{1,0:T(2,128)(2,1)S(1)}, bf16[1,8192]{1,0:T(2,128)(2,1)S(1)}, u32[]{:S(2)}, u32[]{:S(2)}) collective-permute-start(bf16[1,8192]{1,0:T(2,128)(2,1)S(1)} %bitcast.307), channel_id=1, source_target_pairs={{8,0},{16,8},{24,16},{0,24},{9,1},{17,9},{25,17},{1,25},{10,2},{18... | collective-permute-start | bytes 49160 | tf_op jit(solution)/shard_map/ppermute | solution.py:29
  208.3 1.8 fusion.138
  213.7 7.5 %fusion.44 = (f32[56,128]{1,0:T(8,128)S(1)}, f32[56,128]{1,0:T(8,128)S(1)}, f32[56,128]{1,0:T(8,128)S(1)}, f32[56,128]{1,0:T(8,128)S(1)}, f32[56,128]{1,0:T(8,128)S(1)}, /*index=5*/f32[56,128]{1,0:T(8,128)S(1)}) fusion(f32[56,128]{1,0:T(8,128)} %copy.317, f32[56,128]{1,0:T(8,128)} %copy-done.13, f32[56,128]{1,0:T(8,128)S(1)} %copy-done.12, ...), kind=kOutput, calls=%fused_computation.85 | convolution fusion | flops 90503168 | bytes 7888928 | tf_op jit(solution)/shard_map/transpose(jvp())/while/body/eval_jaxpr/kja,kc->jac/dot_general | solution.py:120
  222.2 2.5 copy.360
  224.9 2.5 copy.359
  227.6 39.1 %scatter_fusion.6 = f32[3,640]{0,1:T(8,128)S(1)} fusion(f32[3,640]{0,1:T(8,128)S(1)} %pad.79, s32[7168]{0:T(1024)S(1)} %copy-done.10, f32[7168,3]{1,0:T(8,128)} %bitcast.282), kind=kCustom, calls=%fused_computation.15 | custom fusion | flops 21504 | bytes 286720 | tf_op jit(solution)/shard_map/transpose(jvp())/scatter-add | solution.py:66
  266.7 39.4 %scatter_fusion = f32[3,640]{0,1:T(8,128)S(1)} fusion(f32[3,640]{0,1:T(8,128)S(1)} %pad.68, s32[7168]{0:T(1024)S(1)} %copy-done.10, f32[7168,3]{1,0:T(8,128)} %bitcast.283), kind=kCustom, calls=%fused_computation.8 | custom fusion | flops 21504 | bytes 286720 | tf_op jit(solution)/shard_map/transpose(jvp())/while/body/eval_jaxpr/scatter-add | solution.py:66
  306.1 2.1 collective-permute-start.15
  311.5 1.8 collective-permute-start.17
  319.5 2.5 collective-permute-start.19
  (282 shorter events, 66.7 us)
Async XLA Ops:
  0.6 57.9 %copy-start = (bf16[384,128]{1,0:T(8,128)(2,1)S(1)}, bf16[384,128]{1,0:T(8,128)(2,1)}, u32[]{:S(2)}) copy-start(bf16[384,128]{1,0:T(8,128)(2,1)} %param.26) | copy-start | bytes 294916
  3.6 10.0 %collective-permute-start = (f32[3,1,64]{0,2,1:T(8,128)S(1)}, f32[3,1,64]{0,2,1:T(8,128)S(1)}, u32[]{:S(2)}, u32[]{:S(2)}) collective-permute-start(f32[3,1,64]{0,2,1:T(8,128)S(1)} %get-tuple-element.502), channel_id=1, source_target_pairs={{0,8},{8,16},{16,24},{24,0},{1,9},{9,17},{17,25},{25,1},{2,10},{10... | collective-permute-start | bytes 2312 | tf_op jit(solution)/shard_map/ppermute | solution.py:26
  6.7 7.5 %collective-permute-start.1 = (f32[3,1,64]{0,2,1:T(8,128)S(1)}, f32[3,1,64]{0,2,1:T(8,128)S(1)}, u32[]{:S(2)}, u32[]{:S(2)}) collective-permute-start(f32[3,1,64]{0,2,1:T(8,128)S(1)} %get-tuple-element.501), channel_id=1, source_target_pairs={{8,0},{16,8},{24,16},{0,24},{9,1},{17,9},{25,17},{1,25},{10,2},{18... | collective-permute-start | bytes 2312 | tf_op jit(solution)/shard_map/ppermute | solution.py:29
  15.7 3.7 %collective-permute-start.2 = (f32[3,1,128]{0,2,1:T(8,128)S(1)}, f32[3,1,128]{0,2,1:T(8,128)S(1)}, u32[]{:S(2)}, u32[]{:S(2)}) collective-permute-start(f32[3,1,128]{0,2,1:T(8,128)S(1)} %get-tuple-element.478), channel_id=1, source_target_pairs={{0,2},{2,4},{4,6},{6,0},{1,3},{3,5},{5,7},{7,1},{8,10},{10,12},{12... | collective-permute-start | bytes 4616 | tf_op jit(solution)/shard_map/ppermute | solution.py:26
  15.7 4.3 %collective-permute-start.3 = (f32[3,1,128]{0,2,1:T(8,128)S(1)}, f32[3,1,128]{0,2,1:T(8,128)S(1)}, u32[]{:S(2)}, u32[]{:S(2)}) collective-permute-start(f32[3,1,128]{0,2,1:T(8,128)S(1)} %get-tuple-element.477), channel_id=1, source_target_pairs={{2,0},{4,2},{6,4},{0,6},{3,1},{5,3},{7,5},{1,7},{10,8},{12,10},{14... | collective-permute-start | bytes 4616 | tf_op jit(solution)/shard_map/ppermute | solution.py:29
  21.4 4.9 %collective-permute-start.4 = (f32[3,128]{0,1:T(8,128)S(1)}, f32[3,128]{0,1:T(8,128)S(1)}, u32[]{:S(2)}, u32[]{:S(2)}) collective-permute-start(f32[3,128]{0,1:T(8,128)S(1)} %bitcast.325), channel_id=1, source_target_pairs={{0,1},{1,0},{2,3},{3,2},{4,5},{5,4},{6,7},{7,6},{8,9},{9,8},{10,11... | collective-permute-start | bytes 4616 | tf_op jit(solution)/shard_map/ppermute | solution.py:35
  23.1 75.9 %copy-start.29 = (f32[8]{0:T(128)}, f32[8]{0:T(128)S(1)}, u32[]{:S(2)}) copy-start(f32[8]{0:T(128)S(1)} %convert_multiply_fusion) | copy-start | bytes 100
  24.0 75.0 %copy-start.5 = (f32[56,1,1,1,128]{4,3,2,1,0:T(1,128)}, f32[56,1,1,1,128]{4,3,2,1,0:T(1,128)S(1)}, u32[]{:S(2)}) copy-start(f32[56,1,1,1,128]{4,3,2,1,0:T(1,128)S(1)} %convert_element_type.106) | copy-start | bytes 86020
  53.8 45.2 %copy-start.11 = (f32[56,128]{1,0:T(8,128)}, f32[56,128]{1,0:T(8,128)S(1)}, u32[]{:S(2)}) copy-start(f32[56,128]{1,0:T(8,128)S(1)} %copy.304) | copy-start | bytes 86020
  59.5 5.6 %collective-permute-start.5 = (bf16[1,64,128]{2,1,0:T(8,128)(2,1)S(1)}, bf16[1,64,128]{2,1,0:T(8,128)(2,1)S(1)}, u32[]{:S(2)}, u32[]{:S(2)}) collective-permute-start(bf16[1,64,128]{2,1,0:T(8,128)(2,1)S(1)} %get-tuple-element.516), channel_id=1, source_target_pairs={{0,8},{8,16},{16,24},{24,0},{1,9},{9,17},{17,25},{25,1},{2,10},{10... | collective-permute-start | bytes 49160 | tf_op jit(solution)/shard_map/ppermute | solution.py:26
  59.5 5.5 %collective-permute-start.6 = (bf16[1,64,128]{2,1,0:T(8,128)(2,1)S(1)}, bf16[1,64,128]{2,1,0:T(8,128)(2,1)S(1)}, u32[]{:S(2)}, u32[]{:S(2)}) collective-permute-start(bf16[1,64,128]{2,1,0:T(8,128)(2,1)S(1)} %get-tuple-element.515), channel_id=1, source_target_pairs={{8,0},{16,8},{24,16},{0,24},{9,1},{17,9},{25,17},{1,25},{10,2},{18... | collective-permute-start | bytes 49160 | tf_op jit(solution)/shard_map/ppermute | solution.py:29
  65.9 3.4 %collective-permute-start.7 = (bf16[1,128,128]{2,1,0:T(8,128)(2,1)S(1)}, bf16[1,128,128]{2,1,0:T(8,128)(2,1)S(1)}, u32[]{:S(2)}, u32[]{:S(2)}) collective-permute-start(bf16[1,128,128]{2,1,0:T(8,128)(2,1)S(1)} %get-tuple-element.498), channel_id=1, source_target_pairs={{0,2},{2,4},{4,6},{6,0},{1,3},{3,5},{5,7},{7,1},{8,10},{10,12},{12... | collective-permute-start | bytes 98312 | tf_op jit(solution)/shard_map/ppermute | solution.py:26
  66.0 3.8 %collective-permute-start.8 = (bf16[1,128,128]{2,1,0:T(8,128)(2,1)S(1)}, bf16[1,128,128]{2,1,0:T(8,128)(2,1)S(1)}, u32[]{:S(2)}, u32[]{:S(2)}) collective-permute-start(bf16[1,128,128]{2,1,0:T(8,128)(2,1)S(1)} %get-tuple-element.497), channel_id=1, source_target_pairs={{2,0},{4,2},{6,4},{0,6},{3,1},{5,3},{7,5},{1,7},{10,8},{12,10},{14... | collective-permute-start | bytes 98312 | tf_op jit(solution)/shard_map/ppermute | solution.py:29
  70.5 4.1 %collective-permute-start.9 = (bf16[128,128]{1,0:T(8,128)(2,1)S(1)}, bf16[128,128]{1,0:T(8,128)(2,1)S(1)}, u32[]{:S(2)}, u32[]{:S(2)}) collective-permute-start(bf16[128,128]{1,0:T(8,128)(2,1)S(1)} %gather_fusion.6), channel_id=1, source_target_pairs={{0,1},{1,0},{2,3},{3,2},{4,5},{5,4},{6,7},{7,6},{8,9},{9,8},{10,11... | collective-permute-start | bytes 98312 | tf_op jit(solution)/shard_map/ppermute | solution.py:35
  183.2 4.0 %collective-permute-start.10 = (bf16[16384]{0:T(1024)(128)(2,1)S(1)}, bf16[16384]{0:T(1024)(128)(2,1)S(1)}, u32[]{:S(2)}, u32[]{:S(2)}) collective-permute-start(bf16[16384]{0:T(1024)(128)(2,1)S(1)} %slice_bitcast_fusion.5), channel_id=1, source_target_pairs={{0,1},{1,0},{2,3},{3,2},{4,5},{5,4},{6,7},{7,6},{8,9},{9,8},{10,11... | collective-permute-start | bytes 98312 | tf_op jit(solution)/shard_map/ppermute | solution.py:35
  188.8 4.1 %collective-permute-start.11 = (bf16[1,16384]{1,0:T(2,128)(2,1)S(1)}, bf16[1,16384]{1,0:T(2,128)(2,1)S(1)}, u32[]{:S(2)}, u32[]{:S(2)}) collective-permute-start(bf16[1,16384]{1,0:T(2,128)(2,1)S(1)} %bitcast.298), channel_id=1, source_target_pairs={{0,2},{2,4},{4,6},{6,0},{1,3},{3,5},{5,7},{7,1},{8,10},{10,12},{12... | collective-permute-start | bytes 98312 | tf_op jit(solution)/shard_map/ppermute | solution.py:26
  188.9 3.9 %collective-permute-start.12 = (bf16[1,16384]{1,0:T(2,128)(2,1)S(1)}, bf16[1,16384]{1,0:T(2,128)(2,1)S(1)}, u32[]{:S(2)}, u32[]{:S(2)}) collective-permute-start(bf16[1,16384]{1,0:T(2,128)(2,1)S(1)} %bitcast.300), channel_id=1, source_target_pairs={{2,0},{4,2},{6,4},{0,6},{3,1},{5,3},{7,5},{1,7},{10,8},{12,10},{14... | collective-permute-start | bytes 98312 | tf_op jit(solution)/shard_map/ppermute | solution.py:29
  196.2 5.8 %collective-permute-start.13 = (bf16[1,8192]{1,0:T(2,128)(2,1)S(1)}, bf16[1,8192]{1,0:T(2,128)(2,1)S(1)}, u32[]{:S(2)}, u32[]{:S(2)}) collective-permute-start(bf16[1,8192]{1,0:T(2,128)(2,1)S(1)} %bitcast.305), channel_id=1, source_target_pairs={{0,8},{8,16},{16,24},{24,0},{1,9},{9,17},{17,25},{25,1},{2,10},{10... | collective-permute-start | bytes 49160 | tf_op jit(solution)/shard_map/ppermute | solution.py:26
  196.3 5.7 %collective-permute-start.14 = (bf16[1,8192]{1,0:T(2,128)(2,1)S(1)}, bf16[1,8192]{1,0:T(2,128)(2,1)S(1)}, u32[]{:S(2)}, u32[]{:S(2)}) collective-permute-start(bf16[1,8192]{1,0:T(2,128)(2,1)S(1)} %bitcast.307), channel_id=1, source_target_pairs={{8,0},{16,8},{24,16},{0,24},{9,1},{17,9},{25,17},{1,25},{10,2},{18... | collective-permute-start | bytes 49160 | tf_op jit(solution)/shard_map/ppermute | solution.py:29
  224.9 85.0 %copy-start.36 = (s32[128]{0:T(128)S(1)}, s32[128]{0:T(128)}, u32[]{:S(2)}) copy-start(s32[128]{0:T(128)} %copy-done.35) | copy-start | bytes 1540
  227.4 85.9 %copy-start.34 = (f32[128]{0:T(128)S(1)}, f32[128]{0:T(128)}, u32[]{:S(2)}) copy-start(f32[128]{0:T(128)} %param.30) | copy-start | bytes 1540
  227.4 87.5 %copy-start.24 = (s32[128]{0:T(128)S(1)}, s32[128]{0:T(128)}, u32[]{:S(2)}) copy-start(s32[128]{0:T(128)} %get-tuple-element.524) | copy-start | bytes 1540
  227.4 88.8 %copy-start.22 = (s32[128]{0:T(128)S(1)}, s32[128]{0:T(128)}, u32[]{:S(2)}) copy-start(s32[128]{0:T(128)} %get-tuple-element.523) | copy-start | bytes 1540
  227.4 94.7 %copy-start.38 = (f32[16]{0:T(128)S(1)}, f32[16]{0:T(128)}, u32[]{:S(2)}) copy-start(f32[16]{0:T(128)} %param.32) | copy-start | bytes 196
  227.4 94.7 %copy-start.41 = (s32[1,1,1,128]{3,2,1,0:T(1,128)S(1)}, s32[1,1,1,128]{3,2,1,0:T(1,128)}, u32[]{:S(2)}) copy-start(s32[1,1,1,128]{3,2,1,0:T(1,128)} %param.19) | copy-start | bytes 1540
  227.4 96.4 %copy-start.28 = (s32[64]{0:T(128)S(1)}, s32[64]{0:T(128)}, u32[]{:S(2)}) copy-start(s32[64]{0:T(128)} %get-tuple-element.522) | copy-start | bytes 772
  227.4 97.4 %copy-start.26 = (s32[64]{0:T(128)S(1)}, s32[64]{0:T(128)}, u32[]{:S(2)}) copy-start(s32[64]{0:T(128)} %get-tuple-element.521) | copy-start | bytes 772
  306.1 3.6 %collective-permute-start.15 = (bf16[384]{0:T(512)(128)(2,1)S(1)}, bf16[384]{0:T(512)(128)(2,1)S(1)}, u32[]{:S(2)}, u32[]{:S(2)}) collective-permute-start(bf16[384]{0:T(512)(128)(2,1)S(1)} %bitcast.324), channel_id=1, source_target_pairs={{0,1},{1,0},{2,3},{3,2},{4,5},{5,4},{6,7},{7,6},{8,9},{9,8},{10,11... | collective-permute-start | bytes 2312 | tf_op jit(solution)/shard_map/ppermute | solution.py:35
  311.4 3.0 collective-permute-start.16
  311.5 3.1 collective-permute-start.17
  317.7 5.7 %collective-permute-start.18 = (bf16[1,192]{1,0:T(2,128)(2,1)S(1)}, bf16[1,192]{1,0:T(2,128)(2,1)S(1)}, u32[]{:S(2)}, u32[]{:S(2)}) collective-permute-start(bf16[1,192]{1,0:T(2,128)(2,1)S(1)} %stack.67), channel_id=1, source_target_pairs={{0,8},{8,16},{16,24},{24,0},{1,9},{9,17},{17,25},{25,1},{2,10},{10... | collective-permute-start | bytes 1160 | tf_op jit(solution)/shard_map/ppermute | solution.py:26
  319.5 3.9 %collective-permute-start.19 = (bf16[1,192]{1,0:T(2,128)(2,1)S(1)}, bf16[1,192]{1,0:T(2,128)(2,1)S(1)}, u32[]{:S(2)}, u32[]{:S(2)}) collective-permute-start(bf16[1,192]{1,0:T(2,128)(2,1)S(1)} %stack.68), channel_id=1, source_target_pairs={{8,0},{16,8},{24,16},{0,24},{9,1},{17,9},{25,17},{1,25},{10,2},{18... | collective-permute-start | bytes 1160 | tf_op jit(solution)/shard_map/ppermute | solution.py:29
  (30 other events, 320.9 us)
where the time goes:
time: 333 us; the launch traced here: 327 us
  other arithmetic  151 us (45%)
  local copies, waits for them, and re-layouts  75.4 us (23%)
  matrix products  50.1 us (15%)
  starting transfers between devices  32.5 us (10%)
  waiting for transfers between devices  15 us (5%)
    scatter-add x2, other arithmetic, edge_frame(): offset_vec = source[:, nbr_slots] - centre[:, None, :]  78.4 us
    scatter-add x1, other arithmetic, per_block(): message = radial * widened[block_slots]  39.3 us
    gather x2, local copies, waits for them, and re-layouts, edge_frame(): offset_vec = source[:, nbr_slots] - centre[:, None, :]  27.2 us
    gather x1, local copies, waits for them, and re-layouts, per_block(): message = radial * widened[block_slots]  24.3 us
    dot_general x3, matrix products, per_block(): jnp.einsum('mja,jac->amc', angular, message, precision=HIGHEST)  22.6 us
    ppermute x8, starting transfers between devices, extended(): lax.ppermute(lax.slice_in_dim(block, 0, width, axis=dim), axis, backward)  19.8 us
    dot_general x2, matrix products, per_block(): radial = jnp.einsum('kja,kc->jac', basis, radial_two, precision=HIGHEST)  16.9 us
    ppermute x4, starting transfers between devices, partner(): lax.ppermute(x, axis, [(i, i ^ 1 << stride) for i in range(lax.axis_size(...  7.6 us
  transfers between devices with their start and end apart: 20, of which 12 were waited for; matrix products, arithmetic and copies ran while one was open for 4% of the time, Pallas kernels for 0%

commit v1 on v0

v1 whole, which is shorter than its diff:
```python
import functools
import math

import jax
import jax.numpy as jnp
from jax import lax
from jax.experimental import pallas as pl
from jax.experimental.pallas import tpu as pltpu
from jax.sharding import PartitionSpec as P

NB = 8
LX = 4
LY = 4
LZ = 8

SPACING = 1.8
CUTOFF = 5.0
SPREAD = 0.4
HIGHEST = lax.Precision.HIGHEST
F32 = jnp.float32
BF16 = jnp.bfloat16

ROOT3 = 3.0**0.5
ROOT5 = 5.0**0.5
ROOT15 = 15.0**0.5
GROUP = 4


def dot(a, b, ca=1, cb=0, precision=None):
    return lax.dot_general(
        a, b, (((ca,), (cb,)), ((), ())), precision=precision, preferred_element_type=F32
    )


def split2(x):
    hi = x.astype(BF16)
    lo = (x - hi.astype(F32)).astype(BF16)
    return hi, lo


def dot_split(a, b, ca=1, cb=0):
    hi, lo = split2(b)
    return dot(a, hi, ca, cb) + dot(a, lo, ca, cb)


def onehot(row, size):
    count = row.shape[-1]
    ids = lax.broadcasted_iota(jnp.int32, (size, count), 0)
    return jnp.where(ids == row, 1.0, 0.0).astype(BF16)


def lane_pick(blocks, rows):
    width = blocks[0].shape[-1]
    shift = width.bit_length() - 1
    lane = rows & (width - 1)
    block = rows >> shift
    out = jnp.take_along_axis(blocks[0], lane, axis=1)
    for index in range(1, len(blocks)):
        part = jnp.take_along_axis(blocks[index], lane, axis=1)
        out = jnp.where(block == index, part, out)
    return out


def spread_rows(row, count):
    return jnp.broadcast_to(row, (count, row.shape[-1]))


def padded_coords(pos_ref):
    rows = [pos_ref[i : i + 1, :] for i in range(3)]
    return jnp.concatenate(rows + [jnp.zeros_like(rows[0])] * 5, axis=0)


def face_row(fx_ref):
    return jnp.concatenate([fx_ref[1:2, :], fx_ref[0:1, :]], axis=1)


def low_lanes(shape):
    return lax.broadcasted_iota(jnp.int32, shape, 1) < shape[1] // 2


def shift_rows(shape, axis, amount):
    ids = lax.broadcasted_iota(jnp.int32, shape, 0)
    return jnp.where(ids == axis, amount, 0.0)


def pos_x_kernel(pos_ref, fx_ref, out_ref):
    coords = padded_coords(pos_ref)
    out_ref[...] = lane_pick([coords], spread_rows(face_row(fx_ref), 8))


def pos_y_kernel(pos_ref, lo_ref, hi_ref, fy_ref, p1_ref, up_ref, down_ref):
    coords = padded_coords(pos_ref)
    shape = coords.shape
    low = lo_ref[...] - shift_rows(shape, 0, LX * SPACING)
    high = hi_ref[...] + shift_rows(shape, 0, LX * SPACING)
    ghost = jnp.where(low_lanes(shape), low, high)
    p1_ref[...] = ghost
    up_ref[...] = lane_pick([coords, ghost], spread_rows(fy_ref[1:2, :], 8))
    down_ref[...] = lane_pick([coords, ghost], spread_rows(fy_ref[0:1, :], 8))


def pos_z_kernel(pos_ref, p1_ref, lo_ref, hi_ref, fz_ref, p2_ref, p3_ref, out_ref):
    coords = padded_coords(pos_ref)
    shape = coords.shape
    low = lo_ref[...] - shift_rows(shape, 1, LY * SPACING)
    high = hi_ref[...] + shift_rows(shape, 1, LY * SPACING)
    p2_ref[...] = low
    p3_ref[...] = high
    out_ref[...] = lane_pick([coords, p1_ref[...], low, high], spread_rows(fz_ref[...], 8))


def layer_one_kernel(
    pos_ref,
    p1_ref,
    p2_ref,
    p3_ref,
    pz_ref,
    zs_ref,
    nbr_ref,
    keep_ref,
    fx_ref,
    radial_ref,
    mix_ref,
    embed_ref,
    unit_ref,
    rinv_ref,
    basis_ref,
    slope_ref,
    amp_ref,
    h0_ref,
    send_ref,
    mom_ref,
):
    entries, atoms = nbr_ref.shape
    nbr = nbr_ref[...]
    lane = nbr & (atoms - 1)
    block = nbr >> (atoms.bit_length() - 1)
    last = pz_ref[...] + shift_rows(pz_ref.shape, 2, zs_ref[0])
    tables = [padded_coords(pos_ref), p1_ref[...], p2_ref[...], p3_ref[...], last]
    vec = []
    for axis in range(3):
        got = None
        for index, table in enumerate(tables):
            spread = spread_rows(table[axis : axis + 1, :], entries)
            part = jnp.take_along_axis(spread, lane, axis=1)
            got = part if index == 0 else jnp.where(block == index, part, got)
        vec.append(got - pos_ref[axis : axis + 1, :])
    r_sq = vec[0] * vec[0] + vec[1] * vec[1] + vec[2] * vec[2]
    dist = jnp.sqrt(r_sq)
    rinv = 1.0 / dist
    ux, uy, uz = (v * rinv for v in vec)
    rinv_ref[...] = rinv
    unit_ref[0:entries, :] = ux
    unit_ref[entries : 2 * entries, :] = uy
    unit_ref[2 * entries : 3 * entries, :] = uz
    scaled = jnp.minimum(dist * (1.0 / CUTOFF), 1.0)
    phase = scaled * math.pi
    sine = jnp.sin(phase)
    cosine = jnp.cos(phase)
    inner = 1.0 - scaled * scaled
    weight = keep_ref[...].astype(F32) * (2.0 / CUTOFF) ** 0.5
    env = weight * inner * inner * rinv
    env_slope = -env * rinv - weight * rinv * (4.0 / CUTOFF) * scaled * inner
    twice = 2.0 * cosine
    s_prev, s_now = jnp.zeros_like(sine), sine
    c_prev, c_now = jnp.ones_like(cosine), cosine
    basis = []
    for k in range(NB):
        bk = s_now * env
        basis.append(bk)
        basis_ref[k * entries : (k + 1) * entries, :] = bk
        slope_ref[k * entries : (k + 1) * entries, :] = (
            c_now * env * ((k + 1) * math.pi / CUTOFF) + s_now * env_slope
        )
        s_prev, s_now = s_now, twice * s_now - s_prev
        c_prev, c_now = c_now, twice * c_now - c_prev
    angular = harmonics(ux, uy, uz)
    for m in range(9):
        for k in range(NB):
            prod = basis[k] if m == 0 else basis[k] * angular[m]
            mom_ref[k : k + 1, m * atoms : (m + 1) * atoms] = jnp.sum(prod, axis=0, keepdims=True)
    amp = SPREAD * dot(radial_ref[...], mom_ref[...], 0, 0, HIGHEST)
    amp_ref[...] = amp
    inv = invariants([amp[:, m * atoms : (m + 1) * atoms] for m in range(9)])
    h1 = dot(mix_ref[...], inv, 0, 0)
    h1 = h1 + dot(embed_ref[...], jnp.ones((1, atoms), F32), 0, 0, HIGHEST)
    h1b = h1.astype(BF16)
    h0_ref[...] = h1b
    send_ref[...] = dot(h1b, onehot(face_row(fx_ref), atoms)).astype(BF16)


def harmonics(ux, uy, uz):
    return [
        None,
        ROOT3 * ux,
        ROOT3 * uy,
        ROOT3 * uz,
        ROOT15 * ux * uy,
        ROOT15 * uy * uz,
        0.5 * ROOT5 * (3.0 * uz * uz - 1.0),
        ROOT15 * ux * uz,
        0.5 * ROOT15 * (ux * ux - uy * uy),
    ]


def invariants(amp):
    first = amp[1] * amp[1] + amp[2] * amp[2] + amp[3] * amp[3]
    second = amp[4] * amp[4] + amp[5] * amp[5] + amp[6] * amp[6]
    second = second + amp[7] * amp[7] + amp[8] * amp[8]
    return jnp.concatenate([amp[0], first, second], axis=0).astype(BF16)


def feat_y_kernel(h0_ref, lo_ref, hi_ref, fy_ref, h1_ref, up_ref, down_ref):
    low = lo_ref[...]
    ghost = jnp.where(low_lanes(low.shape), low.astype(F32), hi_ref[...].astype(F32)).astype(BF16)
    h1_ref[...] = ghost
    table = jnp.concatenate([h0_ref[...], ghost], axis=1)
    size = table.shape[1]
    up_ref[...] = dot(table, onehot(fy_ref[1:2, :], size)).astype(BF16)
    down_ref[...] = dot(table, onehot(fy_ref[0:1, :], size)).astype(BF16)


def feat_z_kernel(h0_ref, h1_ref, h2_ref, h3_ref, fz_ref, out_ref):
    table = jnp.concatenate([h0_ref[...], h1_ref[...], h2_ref[...], h3_ref[...]], axis=1)
    out_ref[...] = dot(table, onehot(fz_ref[...], table.shape[1])).astype(BF16)


def stack3(hi, lo):
    return jnp.concatenate([hi, lo, hi], axis=0).astype(BF16)


def layer_two_kernel(
    h0_ref,
    h1_ref,
    h2_ref,
    h3_ref,
    h4_ref,
    nbr_ref,
    occ_ref,
    unit_ref,
    rinv_ref,
    basis_ref,
    slope_ref,
    radial_ref,
    mix_ref,
    rone_ref,
    rhid_ref,
    rout_ref,
    en_ref,
    gin_ref,
    gz_ref,
    grad_ref,
    oh_ref,
    hg_ref,
    rad_ref,
    slo_ref,
    rq_ref,
    acc_ref,
    d_ref,
    dh_ref,
    rts_ref,
    y_ref,
    table_ref,
):
    entries, atoms = nbr_ref.shape
    channels = h0_ref.shape[0]
    total = 5 * atoms
    steps = entries // GROUP
    width = GROUP * atoms
    blocks = channels // 8
    for index, ref in enumerate((h0_ref, h1_ref, h2_ref, h3_ref, h4_ref)):
        table_ref[:, index * atoms : (index + 1) * atoms] = ref[...]
    rt = radial_ref[...]
    hi = rt.astype(BF16).astype(F32)
    lo = rt - hi
    pad = jnp.zeros((channels - 3 * NB, channels), F32)
    rts_ref[...] = jnp.transpose(jnp.concatenate([hi, hi, lo, pad], axis=0)).astype(BF16)
    ux = unit_ref[0:entries, :]
    uy = unit_ref[entries : 2 * entries, :]
    uz = unit_ref[2 * entries : 3 * entries, :]
    for m, val in enumerate(harmonics(ux, uy, uz)):
        if m:
            y_ref[(m - 1) * entries : m * entries, :] = val
    acc_ref[...] = jnp.zeros_like(acc_ref)

    def radial_cols(ref, first):
        cols = [ref[pl.ds(first + jj, NB, stride=entries), :] for jj in range(GROUP)]
        value = jnp.concatenate(cols, axis=1)
        top = value.astype(BF16).astype(F32)
        return stack3(top, value - top)

    def prepare(step):
        first = step * GROUP
        rows = [nbr_ref[pl.ds(first + jj, 1), :] for jj in range(GROUP)]
        hot = onehot(jnp.concatenate(rows, axis=1), total)
        oh_ref[step] = hot
        hg_ref[step] = dot(table_ref[...], hot)
        rts = rts_ref[:, 0 : 3 * NB]
        rad_ref[step] = dot(rts, radial_cols(basis_ref, first))
        slo_ref[step] = dot(rts, radial_cols(slope_ref, first))

    def accumulate(step):
        first = step * GROUP
        for cb in range(blocks):
            rows = slice(cb * 8, cb * 8 + 8)
            msgs = []
            for jj in range(GROUP):
                cols = slice(jj * atoms, (jj + 1) * atoms)
                msgs.append(hg_ref[step, rows, cols] * rad_ref[step, rows, cols])
            for m in range(9):
                value = acc_ref[m, rows, :]
                for jj in range(GROUP):
                    if m == 0:
                        value = value + msgs[jj]
                    else:
                        yv = y_ref[pl.ds((m - 1) * entries + first + jj, 1), :]
                        value = value + msgs[jj] * yv
                acc_ref[m, rows, :] = value

    prepare(0)

    def forward_body(step, carry):
        accumulate(step - 1)
        prepare(step)
        return carry

    lax.fori_loop(1, steps, forward_body, 0)
    accumulate(steps - 1)

    occ = occ_ref[...].astype(F32)
    ones = jnp.ones((1, atoms), F32)
    amp = [SPREAD * acc_ref[m] for m in range(9)]
    own = h0_ref[...].astype(F32)
    h2 = dot(mix_ref[...], invariants(amp), 0, 0) + own
    pre = dot(rhid_ref[...], h2, 0, 0, HIGHEST)
    sig = 1.0 / (1.0 + jnp.exp(-pre))
    rout = dot(rout_ref[...], ones, 0, 0, HIGHEST)
    rone = dot(rone_ref[...], ones, 0, 0, HIGHEST)
    energy = jnp.sum(own * rone, axis=0, keepdims=True)
    energy = energy + jnp.sum(rout * pre * sig, axis=0, keepdims=True)
    en_ref[...] = occ * energy
    dpre = occ * rout * sig * (1.0 + pre * (1.0 - sig))
    dh2 = dot(rhid_ref[...], dpre, 1, 0, HIGHEST)
    dinv = dot_split(mix_ref[...], dh2)
    low = dinv[channels : 2 * channels]
    top = dinv[2 * channels :]
    own_extra = dh2 + occ * rone
    twice = 2.0 * SPREAD
    d6 = twice * amp[6] * top
    d_ref[0] = SPREAD * dinv[0:channels] - 0.5 * ROOT5 * d6
    for m in range(1, 4):
        d_ref[m] = (twice * ROOT3) * amp[m] * low
    for m in (4, 5, 7, 8):
        d_ref[m] = (twice * 0.5 * ROOT15) * amp[m] * top
    d_ref[6] = (1.5 * ROOT5) * d6
    dh_ref[...] = jnp.zeros_like(dh_ref)

    def reverse(step):
        first = step * GROUP
        units = []
        for jj in range(GROUP):
            units.append([unit_ref[pl.ds(i * entries + first + jj, 1), :] for i in range(3)])
        sums = [[None] * 4 for _ in range(GROUP)]
        for cb in range(blocks):
            rows = slice(cb * 8, cb * 8 + 8)
            d = [d_ref[m, rows, :] for m in range(9)]
            for jj in range(GROUP):
                cols = slice(jj * atoms, (jj + 1) * atoms)
                vx, vy, vz = units[jj]
                hg = hg_ref[step, rows, cols]
                rad = rad_ref[step, rows, cols]
                cx = vy * d[4] + vz * d[7] + vx * d[8]
                cy = vx * d[4] + vz * d[5] - vy * d[8]
                cz = vy * d[5] + vx * d[7] + vz * d[6]
                ex, ey, ez = d[1] + cx, d[2] + cy, d[3] + cz
                q = d[0] + vx * ex + vy * ey + vz * ez
                rq_ref[rows, cols] = rad * q
                msg = hg * rad
                parts = [
                    msg * (ex + cx),
                    msg * (ey + cy),
                    msg * (ez + cz),
                    hg * q * slo_ref[step, rows, cols],
                ]
                for i in range(4):
                    prior = sums[jj][i]
                    sums[jj][i] = parts[i] if prior is None else prior + parts[i]
        for jj in range(GROUP):
            for i in range(4):
                row = pl.ds(i * entries + first + jj, 1)
                grad_ref[row, :] = jnp.sum(sums[jj][i], axis=0, keepdims=True)
        dh_ref[...] += dot(oh_ref[step], rq_ref[...].astype(BF16), 1, 1)

    def reverse_body(step, carry):
        reverse(step)
        return carry

    lax.fori_loop(0, steps, reverse_body, 0)

    inner = 4 * atoms
    gin_ref[0:atoms, :] = (dh_ref[0:atoms, :] + jnp.transpose(own_extra)).astype(BF16)
    gin_ref[atoms:inner, :] = dh_ref[atoms:inner, :].astype(BF16)
    gz_ref[...] = dh_ref[inner:, :].astype(BF16)


def fold_z_kernel(gin_ref, az_ref, fz_ref, acc_ref, low_ref, high_ref):
    size = gin_ref.shape[0]
    half = size // 2
    quarter = half // 2
    rows = gin_ref[...].astype(F32) + dot(onehot(fz_ref[...], size), az_ref[...])
    acc_ref[...] = rows[0:half]
    low_ref[...] = rows[half : half + quarter].astype(BF16)
    high_ref[...] = rows[half + quarter :].astype(BF16)


def fold_y_kernel(acc_ref, a0_ref, a1_ref, fy_ref, own_ref, low_ref, high_ref):
    size = acc_ref.shape[0]
    half = size // 2
    quarter = half // 2
    rows = acc_ref[...]
    rows = rows + dot(onehot(fy_ref[0:1, :], size), a0_ref[...])
    rows = rows + dot(onehot(fy_ref[1:2, :], size), a1_ref[...])
    own_ref[...] = rows[0:half]
    low_ref[...] = rows[half : half + quarter].astype(BF16)
    high_ref[...] = rows[half + quarter :].astype(BF16)


def layer_one_reverse_kernel(
    own_ref,
    a0_ref,
    a1_ref,
    fx_ref,
    amp_ref,
    nbr_ref,
    unit_ref,
    rinv_ref,
    basis_ref,
    slope_ref,
    grad_ref,
    radial_ref,
    mix_ref,
    f0_ref,
    f1_ref,
    f2_ref,
    f3_ref,
    f4_ref,
    dv_ref,
    sc_ref,
):
    entries, atoms = nbr_ref.shape
    channels = own_ref.shape[1]
    rows = own_ref[...]
    rows = rows + dot(onehot(fx_ref[0:1, :], atoms), a0_ref[...])
    rows = rows + dot(onehot(fx_ref[1:2, :], atoms), a1_ref[...])
    cot = jnp.transpose(rows)
    dinv = dot_split(mix_ref[...], cot)
    low = dinv[channels : 2 * channels]
    top = dinv[2 * channels :]
    pieces = [dinv[0:channels]]
    for m in range(1, 9):
        amp = amp_ref[:, m * atoms : (m + 1) * atoms]
        pieces.append(2.0 * amp * (low if m < 4 else top))
    dmom = SPREAD * dot(radial_ref[...], jnp.concatenate(pieces, axis=1), 1, 0, HIGHEST)
    ux = unit_ref[0:entries, :]
    uy = unit_ref[entries : 2 * entries, :]
    uz = unit_ref[2 * entries : 3 * entries, :]
    basis = [basis_ref[k * entries : (k + 1) * entries, :] for k in range(NB)]
    slope = [slope_ref[k * entries : (k + 1) * entries, :] for k in range(NB)]
    angular = harmonics(ux, uy, uz)
    dr = grad_ref[3 * entries : 4 * entries, :]
    dy = []
    for m in range(9):
        part = None
        sl = None
        for k in range(NB):
            row = dmom[k : k + 1, m * atoms : (m + 1) * atoms]
            sl = slope[k] * row if sl is None else sl + slope[k] * row
            if m:
                part = basis[k] * row if part is None else part + basis[k] * row
        dr = dr + (sl if m == 0 else sl * angular[m])
        dy.append(part)
    wx = grad_ref[0:entries, :] + ROOT3 * dy[1]
    wx = wx + ROOT15 * (uy * dy[4] + uz * dy[7] + ux * dy[8])
    wy = grad_ref[entries : 2 * entries, :] + ROOT3 * dy[2]
    wy = wy + ROOT15 * (ux * dy[4] + uz * dy[5] - uy * dy[8])
    wz = grad_ref[2 * entries : 3 * entries, :] + ROOT3 * dy[3]
    wz = wz + ROOT15 * (uy * dy[5] + ux * dy[7]) + (3.0 * ROOT5) * uz * dy[6]
    rinv = rinv_ref[...]
    along = dr - rinv * (ux * wx + uy * wy + uz * wz)
    grads = [wx * rinv + along * ux, wy * rinv + along * uy, wz * rinv + along * uz]
    centre = []
    for i in range(3):
        centre.append(jnp.sum(grads[i], axis=0, keepdims=True))
        top16 = grads[i].astype(BF16).astype(F32)
        dv_ref[i * entries : (i + 1) * entries, :] = top16
        dv_ref[(3 + i) * entries : (4 + i) * entries, :] = grads[i] - top16
    shift = atoms.bit_length() - 1
    sc_ref[...] = jnp.zeros_like(sc_ref)

    def body(step, carry):
        first = step * GROUP
        row = jnp.concatenate([nbr_ref[pl.ds(first + jj, 1), :] for jj in range(GROUP)], axis=1)
        hot = onehot(row & (atoms - 1), atoms)
        block = row >> shift
        cols = [dv_ref[pl.ds(first + jj, 6, stride=entries), :] for jj in range(GROUP)]
        value = jnp.concatenate(cols, axis=1)
        value = jnp.concatenate([value, jnp.zeros_like(value[0:2])], axis=0)
        parts = [jnp.where(block == index, value, 0.0) for index in range(5)]
        sc_ref[...] += dot(jnp.concatenate(parts, axis=0).astype(BF16), hot, 1, 1)
        return carry

    lax.fori_loop(0, entries // GROUP, body, 0)
    zero = jnp.zeros((5, atoms), F32)
    own = jnp.concatenate(centre + [zero], axis=0)
    for index, ref in enumerate((f0_ref, f1_ref, f2_ref, f3_ref, f4_ref)):
        base = index * 8
        value = sc_ref[base : base + 3, :] + sc_ref[base + 3 : base + 6, :]
        value = jnp.concatenate([value, zero], axis=0)
        ref[...] = value - own if index == 0 else value


def scatter_lanes(values, row, size):
    return dot(values, onehot(row, size).astype(F32), 1, 1, HIGHEST)


def force_z_kernel(f0_ref, f1_ref, f2_ref, f3_ref, az_ref, fz_ref, out_ref, low_ref, high_ref):
    atoms = f0_ref.shape[1]
    add = scatter_lanes(az_ref[...], fz_ref[...], 4 * atoms)
    out_ref[:, 0:atoms] = f0_ref[...] + add[:, 0:atoms]
    out_ref[:, atoms : 2 * atoms] = f1_ref[...] + add[:, atoms : 2 * atoms]
    low_ref[...] = f2_ref[...] + add[:, 2 * atoms : 3 * atoms]
    high_ref[...] = f3_ref[...] + add[:, 3 * atoms :]


def force_y_kernel(acc_ref, a0_ref, a1_ref, fy_ref, own_ref, ghost_ref):
    size = acc_ref.shape[1]
    rows = acc_ref[...]
    rows = rows + scatter_lanes(a0_ref[...], fy_ref[0:1, :], size)
    rows = rows + scatter_lanes(a1_ref[...], fy_ref[1:2, :], size)
    own_ref[...] = rows[:, 0 : size // 2]
    ghost_ref[...] = rows[:, size // 2 :]


def force_x_kernel(own_ref, a0_ref, a1_ref, fx_ref, out_ref):
    size = own_ref.shape[1]
    from_low = a0_ref[...][:, size // 2 :]
    from_high = a1_ref[...][:, 0 : size // 2]
    rows = own_ref[...]
    rows = rows + scatter_lanes(from_low, fx_ref[0:1, :], size)
    rows = rows + scatter_lanes(from_high, fx_ref[1:2, :], size)
    out_ref[...] = -rows[0:3]


def call(kernel, outs, *args, scratch=(), vmem=8, scalars=()):
    specs = []
    for index in range(len(args)):
        space = pltpu.SMEM if index in scalars else pltpu.VMEM
        specs.append(pl.BlockSpec(memory_space=space))
    single = not isinstance(outs, (list, tuple))
    shapes = [outs] if single else list(outs)
    result = pl.pallas_call(
        kernel,
        out_shape=shapes,
        in_specs=specs,
        out_specs=[pl.BlockSpec(memory_space=pltpu.VMEM)] * len(shapes),
        scratch_shapes=list(scratch),
        compiler_params=pltpu.CompilerParams(vmem_limit_bytes=vmem * 1024 * 1024),
    )(*args)
    return result[0] if single else result


def moved(x, axis, step):
    count = lax.axis_size(axis)
    return lax.ppermute(x, axis, [(i, (i + step) % count) for i in range(count)])


def partner(x, axis):
    return lax.ppermute(x, axis, [(i, i ^ 1) for i in range(lax.axis_size(axis))])


def per_device(
    positions,
    occupancy,
    neighbours,
    keep,
    face_x,
    face_y,
    face_z,
    radial_one,
    mix_one,
    embed,
    radial_two,
    mix_two,
    read_one,
    read_hidden,
    read_out,
):
    atoms = positions.shape[-1]
    entries = neighbours.shape[0]
    channels = radial_one.shape[1]
    pos = positions.reshape(3, atoms)
    nbr = neighbours.reshape(entries, atoms)
    kept = keep.reshape(entries, atoms)
    occ = occupancy.reshape(1, atoms)
    fx = face_x.reshape(2, face_x.shape[-1])
    fy = face_y.reshape(2, face_y.shape[-1])
    fz = face_z.reshape(1, face_z.shape[-1])
    zshift = jnp.where(lax.axis_index("gz") == 0, LZ * SPACING, -LZ * SPACING)
    zshift = zshift.astype(F32).reshape(1)
    embed = embed.reshape(1, channels)
    read_one = read_one.reshape(1, channels)
    read_out = read_out.reshape(1, read_out.shape[0])

    def f32(*shape):
        return jax.ShapeDtypeStruct(shape, F32)

    def b16(*shape):
        return jax.ShapeDtypeStruct(shape, BF16)

    small = f32(8, atoms)
    sent = call(pos_x_kernel, small, pos, fx)
    lo, hi = moved(sent, "gx", 1), moved(sent, "gx", -1)
    p1, up, down = call(pos_y_kernel, [small] * 3, pos, lo, hi, fy)
    lo, hi = moved(up, "gy", 1), moved(down, "gy", -1)
    p2, p3, sent = call(pos_z_kernel, [small] * 3, pos, p1, lo, hi, fz)
    pz = partner(sent, "gz")

    square = b16(channels, atoms)
    unit, rinv, basis, slope, amp, h0, sent = call(
        layer_one_kernel,
        [
            f32(3 * entries, atoms),
            f32(entries, atoms),
            f32(NB * entries, atoms),
            f32(NB * entries, atoms),
            f32(channels, 9 * atoms),
            square,
            square,
        ],
        pos,
        p1,
        p2,
        p3,
        pz,
        zshift,
        nbr,
        kept,
        fx,
        radial_one,
        mix_one,
        embed,
        scratch=[pltpu.VMEM((NB, 9 * atoms), F32)],
        scalars=(5,),
    )
    lo, hi = moved(sent, "gx", 1), moved(sent, "gx", -1)
    h1, up, down = call(feat_y_kernel, [square] * 3, h0, lo, hi, fy)
    h2, h3 = moved(up, "gy", 1), moved(down, "gy", -1)
    sent = call(feat_z_kernel, square, h0, h1, h2, h3, fz)
    h4 = partner(sent, "gz")

    steps = entries // GROUP
    width = GROUP * atoms
    energies, gin, gz, grad = call(
        layer_two_kernel,
        [f32(1, atoms), b16(4 * atoms, channels), b16(atoms, channels), f32(4 * entries, atoms)],
        h0,
        h1,
        h2,
        h3,
        h4,
        nbr,
        occ,
        unit,
        rinv,
        basis,
        slope,
        radial_two,
        mix_two,
        read_one,
        read_hidden,
        read_out,
        scratch=[
            pltpu.VMEM((steps, 5 * atoms, width), BF16),
            pltpu.VMEM((steps, channels, width), F32),
            pltpu.VMEM((steps, channels, width), F32),
            pltpu.VMEM((steps, channels, width), F32),
            pltpu.VMEM((channels, width), F32),
            pltpu.VMEM((9, channels, atoms), F32),
            pltpu.VMEM((9, channels, atoms), F32),
            pltpu.VMEM((5 * atoms, channels), F32),
            pltpu.VMEM((channels, channels), BF16),
            pltpu.VMEM((8 * entries, atoms), F32),
            pltpu.VMEM((channels, 5 * atoms), BF16),
        ],
        vmem=40,
    )
    az = partner(gz, "gz")
    acc, low, high = call(
        fold_z_kernel,
        [f32(2 * atoms, channels), b16(atoms, channels), b16(atoms, channels)],
        gin,
        az,
        fz,
    )
    a0, a1 = moved(high, "gy", 1), moved(low, "gy", -1)
    half = atoms // 2
    own, low, high = call(
        fold_y_kernel,
        [f32(atoms, channels), b16(half, channels), b16(half, channels)],
        acc,
        a0,
        a1,
        fy,
    )
    a0, a1 = moved(high, "gx", 1), moved(low, "gx", -1)
    f0, f1, f2, f3, f4 = call(
        layer_one_reverse_kernel,
        [small] * 5,
        own,
        a0,
        a1,
        fx,
        amp,
        nbr,
        unit,
        rinv,
        basis,
        slope,
        grad,
        radial_one,
        mix_one,
        scratch=[pltpu.VMEM((6 * entries, atoms), F32), pltpu.VMEM((40, atoms), F32)],
    )
    az = partner(f4, "gz")
    acc, low, high = call(
        force_z_kernel, [f32(8, 2 * atoms), small, small], f0, f1, f2, f3, az, fz
    )
    a0, a1 = moved(high, "gy", 1), moved(low, "gy", -1)
    own, ghost = call(force_y_kernel, [small, small], acc, a0, a1, fy)
    a0, a1 = moved(ghost, "gx", 1), moved(ghost, "gx", -1)
    forces = call(force_x_kernel, f32(3, atoms), own, a0, a1, fx)
    return (energies.reshape(occupancy.shape), forces.reshape(positions.shape))


def solution(mesh):
    return jax.shard_map(
        per_device,
        mesh=mesh,
        in_specs=(
            P(None, "gx", "gy", "gz", None),
            P("gx", "gy", "gz", None),
            P(None, "gx", "gy", "gz", None),
            P(None, "gx", "gy", "gz", None),
            P("gx", "gy", "gz", None, None),
            P("gx", "gy", "gz", None, None),
            P("gx", "gy", "gz", None),
            P(),
            P(),
            P(),
            P(),
            P(),
            P(),
            P(),
            P(),
        ),
        out_specs=(P("gx", "gy", "gz", None), P(None, "gx", "gy", "gz", None)),
        check_vma=False,
    )
```

time: 333 us -> 89.1 us (0.27); the launches traced: 327 us -> 88.9 us
  other arithmetic: 151 us -> 0 us
  local copies, waits for them, and re-layouts: 75.4 us -> 4.35 us
  matrix products: 50.1 us -> 0 us
  Pallas kernels: 0 us -> 24.6 us
  waiting for transfers between devices: 15 us -> 31 us
  starting transfers between devices: 32.5 us -> 28.3 us
    scatter-add x13 -> x0, other arithmetic: 130 us -> none  [the longest x2 78.4 us: edge_frame(): offset_vec = source[:, nbr_slots] - centre[:, None, :]]
    gather x9 -> x0, local copies, waits for them, and re-layouts: 55.8 us -> none  [the longest x2 27.2 us: edge_frame(): offset_vec = source[:, nbr_slots] - centre[:, None, :]]
    dot_general x20 -> x0, matrix products: 50.1 us -> none  [the longest x3 22.6 us: per_block(): jnp.einsum('mja,jac->amc', angular, message, precision=HIGHEST)]
    pallas_call x0 -> x13, Pallas kernels: none -> 24.6 us  [call(): pl.pallas_call(kernel, out_shape=shapes, in_specs=specs, out_specs=[pl.Bl...]
    ppermute x20, waiting for transfers between devices: 15 us -> 31 us  [the longest x16 22.1 us: moved(): lax.ppermute(x, axis, [(i, (i + step) % count) for i in range(count)])]
    mul x14 -> x0, other arithmetic: 8.26 us -> none  [the longest x1 2.98 us: per_block(): message = radial * widened[block_slots]]
    select_n x6 -> x0, other arithmetic: 5.23 us -> none  [the longest x2 1.84 us: add_part(): return values.at[slot_list].add(update)]
    add_any x2 -> x0, local copies, waits for them, and re-layouts: 5.05 us -> none  [edge_frame(): distance = jnp.sqrt(jnp.sum(offset_vec * offset_vec, axis=0))]
  transfers between devices with their start and end apart: 20 -> 20, of which waited for: 12 -> 15; matrix products, arithmetic and copies ran while one was open for 4% -> 0% of each run, Pallas kernels for 0% -> 0%
where the time goes in v1:
time: 89.1 us; the launch traced here: 88.9 us
  waiting for transfers between devices  31 us (35%)
  starting transfers between devices  28.3 us (32%)
  Pallas kernels  24.6 us (28%)
  local copies, waits for them, and re-layouts  4.35 us (5%)
    pallas_call x13, Pallas kernels, call(): pl.pallas_call(kernel, out_shape=shapes, in_specs=specs, out_specs=[pl.Bl...  24.6 us
    ppermute x16, waiting for transfers between devices, moved(): lax.ppermute(x, axis, [(i, (i + step) % count) for i in range(count)])  22.1 us
    ppermute x16, starting transfers between devices, moved(): lax.ppermute(x, axis, [(i, (i + step) % count) for i in range(count)])  22 us
    ppermute x4, waiting for transfers between devices, partner(): lax.ppermute(x, axis, [(i, i ^ 1) for i in range(lax.axis_size(axis))])  8.85 us
    ppermute x4, starting transfers between devices, partner(): lax.ppermute(x, axis, [(i, i ^ 1) for i in range(lax.axis_size(axis))])  6.3 us
    unnamed x33, local copies, waits for them, and re-layouts  4.35 us
  transfers between devices with their start and end apart: 20, of which 15 were waited for; matrix products, arithmetic and copies ran while one was open for 0% of the time, Pallas kernels for 0%

profile of v1, /device:TPU:0, one launch (start us, length us, event | category | flops | bytes accessed | tf_op | source)
XLA Modules:
  0.0 88.9 jit_solution(5623864182554089489)
XLA Ops:
  0.6 0.7 copy.21
  2.1 5.1 %collective-permute-start.1 = (f32[8,128]{1,0:T(8,128)S(1)}, f32[8,128]{1,0:T(8,128)S(1)}, u32[]{:S(2)}, u32[]{:S(2)}) collective-permute-start(f32[8,128]{1,0:T(8,128)S(1)} %shard_map.158), channel_id=1, source_target_pairs={{0,24},{8,0},{16,8},{24,16},{1,25},{9,1},{17,9},{25,17},{2,26},{10... | collective-permute-start | bytes 12296 | tf_op jit(solution)/shard_map/ppermute | solution.py:574
  7.2 1.3 %collective-permute-done.1.hi_ref = f32[8,128]{1,0:T(8,128)S(1)} collective-permute-done((f32[8,128]{1,0:T(8,128)S(1)}, f32[8,128]{1,0:T(8,128)S(1)}, u32[]{:S(2)}, u32[]{:S(2)}) %collective-permute-start.1) | collective-permute-done | bytes 4128 | tf_op jit(solution)/shard_map/ppermute | solution.py:574
  8.5 4.1 %collective-permute-done.lo_ref = f32[8,128]{1,0:T(8,128)S(1)} collective-permute-done((f32[8,128]{1,0:T(8,128)S(1)}, f32[8,128]{1,0:T(8,128)S(1)}, u32[]{:S(2)}, u32[]{:S(2)}) %collective-permute-start) | collective-permute-done | bytes 4128 | tf_op jit(solution)/shard_map/ppermute | solution.py:574
  12.7 1.7 %collective-permute-start.3 = (f32[8,128]{1,0:T(8,128)S(1)}, f32[8,128]{1,0:T(8,128)S(1)}, u32[]{:S(2)}, u32[]{:S(2)}) collective-permute-start(f32[8,128]{1,0:T(8,128)S(1)} %get-tuple-element.40), channel_id=1, source_target_pairs={{0,6},{2,0},{4,2},{6,4},{1,7},{3,1},{5,3},{7,5},{8,14},{10,8},{12,... | collective-permute-start | bytes 12296 | tf_op jit(solution)/shard_map/ppermute | solution.py:574
  14.5 1.3 %collective-permute-done.2.lo_ref = f32[8,128]{1,0:T(8,128)S(1)} collective-permute-done((f32[8,128]{1,0:T(8,128)S(1)}, f32[8,128]{1,0:T(8,128)S(1)}, u32[]{:S(2)}, u32[]{:S(2)}) %collective-permute-start.2) | collective-permute-done | bytes 4128 | tf_op jit(solution)/shard_map/ppermute | solution.py:574
  15.9 1.5 %collective-permute-start.4 = (f32[8,128]{1,0:T(8,128)S(1)}, f32[8,128]{1,0:T(8,128)S(1)}, u32[]{:S(2)}, u32[]{:S(2)}) collective-permute-start(f32[8,128]{1,0:T(8,128)S(1)} %get-tuple-element.43), channel_id=1, source_target_pairs={{0,1},{1,0},{2,3},{3,2},{4,5},{5,4},{6,7},{7,6},{8,9},{9,8},{10,11... | collective-permute-start | bytes 12296 | tf_op jit(solution)/shard_map/ppermute | solution.py:578
  17.4 2.1 %collective-permute-done.4.pz_ref = f32[8,128]{1,0:T(8,128)S(1)} collective-permute-done((f32[8,128]{1,0:T(8,128)S(1)}, f32[8,128]{1,0:T(8,128)S(1)}, u32[]{:S(2)}, u32[]{:S(2)}) %collective-permute-start.4) | collective-permute-done | bytes 4128 | tf_op jit(solution)/shard_map/ppermute | solution.py:578
  20.1 0.9 %copy-done = bf16[384,128]{1,0:T(8,128)(2,1)S(1)} copy-done((bf16[384,128]{1,0:T(8,128)(2,1)S(1)}, bf16[384,128]{1,0:T(8,128)(2,1)}, u32[]{:S(2)}) %copy-start) | copy-done | bytes 98328
  21.0 1.4 %shard_map.161 = (f32[168,128]{1,0:T(8,128)S(1)}, f32[56,128]{1,0:T(8,128)S(1)}, f32[448,128]{1,0:T(8,128)S(1)}, f32[448,128]{1,0:T(8,128)S(1)}, f32[128,1152]{1...) custom-call(f32[3,128]{1,0:T(4,128)S(1)} %bitcast.21, ...), custom_call_target="tpu_custom_call" | custom-call | tf_op jit(solution)/shard_map/pallas_call | solution.py:561
  22.5 2.0 %collective-permute-start.5 = (bf16[128,128]{1,0:T(8,128)(2,1)S(1)}, bf16[128,128]{1,0:T(8,128)(2,1)S(1)}, u32[]{:S(2)}, u32[]{:S(2)}) collective-permute-start(bf16[128,128]{1,0:T(8,128)(2,1)S(1)} %get-tuple-element.45), channel_id=1, source_target_pairs={{0,8},{8,16},{16,24},{24,0},{1,9},{9,17},{17,25},{25,1},{2,10},{10... | collective-permute-start | bytes 98312 | tf_op jit(solution)/shard_map/ppermute | solution.py:574
  24.5 1.9 %collective-permute-done.6.hi_ref = bf16[128,128]{1,0:T(8,128)(2,1)S(1)} collective-permute-done((bf16[128,128]{1,0:T(8,128)(2,1)S(1)}, bf16[128,128]{1,0:T(8,128)(2,1)S(1)}, u32[]{:S(2)}, u32[]{:S(2)}) %collective-permute-start.6) | collective-permute-done | bytes 32800 | tf_op jit(solution)/shard_map/ppermute | solution.py:574
  26.4 1.9 %collective-permute-done.5.lo_ref = bf16[128,128]{1,0:T(8,128)(2,1)S(1)} collective-permute-done((bf16[128,128]{1,0:T(8,128)(2,1)S(1)}, bf16[128,128]{1,0:T(8,128)(2,1)S(1)}, u32[]{:S(2)}, u32[]{:S(2)}) %collective-permute-start.5) | collective-permute-done | bytes 32800 | tf_op jit(solution)/shard_map/ppermute | solution.py:574
  28.5 1.7 %collective-permute-start.8 = (bf16[128,128]{1,0:T(8,128)(2,1)S(1)}, bf16[128,128]{1,0:T(8,128)(2,1)S(1)}, u32[]{:S(2)}, u32[]{:S(2)}) collective-permute-start(bf16[128,128]{1,0:T(8,128)(2,1)S(1)} %get-tuple-element.48), channel_id=1, source_target_pairs={{0,6},{2,0},{4,2},{6,4},{1,7},{3,1},{5,3},{7,5},{8,14},{10,8},{12,... | collective-permute-start | bytes 98312 | tf_op jit(solution)/shard_map/ppermute | solution.py:574
  30.3 1.6 %collective-permute-done.7.h2_ref = bf16[128,128]{1,0:T(8,128)(2,1)S(1)} collective-permute-done((bf16[128,128]{1,0:T(8,128)(2,1)S(1)}, bf16[128,128]{1,0:T(8,128)(2,1)S(1)}, u32[]{:S(2)}, u32[]{:S(2)}) %collective-permute-start.7) | collective-permute-done | bytes 32800 | tf_op jit(solution)/shard_map/ppermute | solution.py:574
  32.0 1.6 %collective-permute-start.9 = (bf16[128,128]{1,0:T(8,128)(2,1)S(1)}, bf16[128,128]{1,0:T(8,128)(2,1)S(1)}, u32[]{:S(2)}, u32[]{:S(2)}) collective-permute-start(bf16[128,128]{1,0:T(8,128)(2,1)S(1)} %shard_map.163), channel_id=1, source_target_pairs={{0,1},{1,0},{2,3},{3,2},{4,5},{5,4},{6,7},{7,6},{8,9},{9,8},{10,11... | collective-permute-start | bytes 98312 | tf_op jit(solution)/shard_map/ppermute | solution.py:578
  33.7 2.3 %collective-permute-done.9.h4_ref = bf16[128,128]{1,0:T(8,128)(2,1)S(1)} collective-permute-done((bf16[128,128]{1,0:T(8,128)(2,1)S(1)}, bf16[128,128]{1,0:T(8,128)(2,1)S(1)}, u32[]{:S(2)}, u32[]{:S(2)}) %collective-permute-start.9) | collective-permute-done | bytes 32800 | tf_op jit(solution)/shard_map/ppermute | solution.py:578
  36.7 17.8 %shard_map.164 = (f32[1,128]{1,0:T(1,128)}, bf16[512,128]{1,0:T(8,128)(2,1)S(1)}, bf16[128,128]{1,0:T(8,128)(2,1)S(1)}, f32[224,128]{1,0:T(8,128)S(1)}) custom-call(bf16[128,128]{1,0:T(8,128)(2,1)S(1)} %get-tuple-element.44.h0_ref, bf16[128,128]{1,0:T(8,128)(2,1)S(1)} %get-tuple-element.46.h1_ref, bf16[128,128]{1,0:T(8,128)(2,1)S(1)} %collective-permute-done.7.h2_ref, ...), custom_call_target="tpu_custom_call" | custom-call | tf_op jit(solution)/shard_map/pallas_call | solution.py:561
  54.6 1.6 %collective-permute-start.10 = (bf16[128,128]{1,0:T(8,128)(2,1)S(1)}, bf16[128,128]{1,0:T(8,128)(2,1)S(1)}, u32[]{:S(2)}, u32[]{:S(2)}) collective-permute-start(bf16[128,128]{1,0:T(8,128)(2,1)S(1)} %get-tuple-element.55), channel_id=1, source_target_pairs={{0,1},{1,0},{2,3},{3,2},{4,5},{5,4},{6,7},{7,6},{8,9},{9,8},{10,11... | collective-permute-start | bytes 98312 | tf_op jit(solution)/shard_map/ppermute | solution.py:578
  56.2 2.4 %collective-permute-done.10.az_ref = bf16[128,128]{1,0:T(8,128)(2,1)S(1)} collective-permute-done((bf16[128,128]{1,0:T(8,128)(2,1)S(1)}, bf16[128,128]{1,0:T(8,128)(2,1)S(1)}, u32[]{:S(2)}, u32[]{:S(2)}) %collective-permute-start.10) | collective-permute-done | bytes 32800 | tf_op jit(solution)/shard_map/ppermute | solution.py:578
  58.8 1.7 %collective-permute-start.12 = (bf16[128,128]{1,0:T(8,128)(2,1)S(1)}, bf16[128,128]{1,0:T(8,128)(2,1)S(1)}, u32[]{:S(2)}, u32[]{:S(2)}) collective-permute-start(bf16[128,128]{1,0:T(8,128)(2,1)S(1)} %get-tuple-element.58), channel_id=1, source_target_pairs={{0,6},{2,0},{4,2},{6,4},{1,7},{3,1},{5,3},{7,5},{8,14},{10,8},{12,... | collective-permute-start | bytes 98312 | tf_op jit(solution)/shard_map/ppermute | solution.py:574
  60.5 1.6 %collective-permute-done.11.a0_ref = bf16[128,128]{1,0:T(8,128)(2,1)S(1)} collective-permute-done((bf16[128,128]{1,0:T(8,128)(2,1)S(1)}, bf16[128,128]{1,0:T(8,128)(2,1)S(1)}, u32[]{:S(2)}, u32[]{:S(2)}) %collective-permute-start.11) | collective-permute-done | bytes 32800 | tf_op jit(solution)/shard_map/ppermute | solution.py:574
  62.5 3.7 %collective-permute-start.14 = (bf16[64,128]{1,0:T(8,128)(2,1)S(1)}, bf16[64,128]{1,0:T(8,128)(2,1)S(1)}, u32[]{:S(2)}, u32[]{:S(2)}) collective-permute-start(bf16[64,128]{1,0:T(8,128)(2,1)S(1)} %get-tuple-element.61), channel_id=1, source_target_pairs={{0,24},{8,0},{16,8},{24,16},{1,25},{9,1},{17,9},{25,17},{2,26},{10... | collective-permute-start | bytes 49160 | tf_op jit(solution)/shard_map/ppermute | solution.py:574
  66.2 1.7 %collective-permute-done.13.a0_ref = bf16[64,128]{1,0:T(8,128)(2,1)S(1)} collective-permute-done((bf16[64,128]{1,0:T(8,128)(2,1)S(1)}, bf16[64,128]{1,0:T(8,128)(2,1)S(1)}, u32[]{:S(2)}, u32[]{:S(2)}) %collective-permute-start.13) | collective-permute-done | bytes 16416 | tf_op jit(solution)/shard_map/ppermute | solution.py:574
  67.9 3.4 %shard_map.167 = (f32[8,128]{1,0:T(8,128)S(1)}, f32[8,128]{1,0:T(8,128)S(1)}, f32[8,128]{1,0:T(8,128)S(1)}, f32[8,128]{1,0:T(8,128)S(1)}, f32[8,128]{1,0:T(8,128)S(1)}) custom-call(f32[128,128]{1,0:T(8,128)S(1)} %get-tuple-element.59.own_ref, bf16[64,128]{1,0:T(8,128)(2,1)S(1)} %collective-permute-done.13.a0_ref, ...), custom_call_target="tpu_custom_call" | custom-call | tf_op jit(solution)/shard_map/pallas_call | solution.py:561
  71.3 1.6 %collective-permute-start.15 = (f32[8,128]{1,0:T(8,128)S(1)}, f32[8,128]{1,0:T(8,128)S(1)}, u32[]{:S(2)}, u32[]{:S(2)}) collective-permute-start(f32[8,128]{1,0:T(8,128)S(1)} %get-tuple-element.68), channel_id=1, source_target_pairs={{0,1},{1,0},{2,3},{3,2},{4,5},{5,4},{6,7},{7,6},{8,9},{9,8},{10,11... | collective-permute-start | bytes 12296 | tf_op jit(solution)/shard_map/ppermute | solution.py:578
  72.9 2.1 %collective-permute-done.15.az_ref = f32[8,128]{1,0:T(8,128)S(1)} collective-permute-done((f32[8,128]{1,0:T(8,128)S(1)}, f32[8,128]{1,0:T(8,128)S(1)}, u32[]{:S(2)}, u32[]{:S(2)}) %collective-permute-start.15) | collective-permute-done | bytes 4128 | tf_op jit(solution)/shard_map/ppermute | solution.py:578
  75.3 1.8 %collective-permute-start.17 = (f32[8,128]{1,0:T(8,128)S(1)}, f32[8,128]{1,0:T(8,128)S(1)}, u32[]{:S(2)}, u32[]{:S(2)}) collective-permute-start(f32[8,128]{1,0:T(8,128)S(1)} %get-tuple-element.71), channel_id=1, source_target_pairs={{0,6},{2,0},{4,2},{6,4},{1,7},{3,1},{5,3},{7,5},{8,14},{10,8},{12,... | collective-permute-start | bytes 12296 | tf_op jit(solution)/shard_map/ppermute | solution.py:574
  77.1 1.3 %collective-permute-done.16.a0_ref = f32[8,128]{1,0:T(8,128)S(1)} collective-permute-done((f32[8,128]{1,0:T(8,128)S(1)}, f32[8,128]{1,0:T(8,128)S(1)}, u32[]{:S(2)}, u32[]{:S(2)}) %collective-permute-start.16) | collective-permute-done | bytes 4128 | tf_op jit(solution)/shard_map/ppermute | solution.py:574
  78.7 3.8 %collective-permute-start.19 = (f32[8,128]{1,0:T(8,128)S(1)}, f32[8,128]{1,0:T(8,128)S(1)}, u32[]{:S(2)}, u32[]{:S(2)}) collective-permute-start(f32[8,128]{1,0:T(8,128)S(1)} %get-tuple-element.73), channel_id=1, source_target_pairs={{0,24},{8,0},{16,8},{24,16},{1,25},{9,1},{17,9},{25,17},{2,26},{10... | collective-permute-start | bytes 12296 | tf_op jit(solution)/shard_map/ppermute | solution.py:574
  82.6 1.3 %collective-permute-done.19.a1_ref = f32[8,128]{1,0:T(8,128)S(1)} collective-permute-done((f32[8,128]{1,0:T(8,128)S(1)}, f32[8,128]{1,0:T(8,128)S(1)}, u32[]{:S(2)}, u32[]{:S(2)}) %collective-permute-start.19) | collective-permute-done | bytes 4128 | tf_op jit(solution)/shard_map/ppermute | solution.py:574
  83.9 4.1 %collective-permute-done.18.a0_ref = f32[8,128]{1,0:T(8,128)S(1)} collective-permute-done((f32[8,128]{1,0:T(8,128)S(1)}, f32[8,128]{1,0:T(8,128)S(1)}, u32[]{:S(2)}, u32[]{:S(2)}) %collective-permute-start.18) | collective-permute-done | bytes 4128 | tf_op jit(solution)/shard_map/ppermute | solution.py:574
  (54 shorter events, 5.2 us)
Async XLA Ops:
  2.0 13.8 %copy-start.8 = (s32[1,1,1,128]{3,2,1,0:T(1,128)S(1)}, s32[1,1,1,128]{3,2,1,0:T(1,128)}, u32[]{:S(2)}) copy-start(s32[1,1,1,128]{3,2,1,0:T(1,128)} %param.21) | copy-start | bytes 1540
  2.0 17.5 %copy-start.5 = (f32[8,128]{1,0:T(8,128)S(1)}, f32[8,128]{1,0:T(8,128)}, u32[]{:S(2)}) copy-start(f32[8,128]{1,0:T(8,128)} %radial_ref.5) | copy-start | bytes 12292
  2.1 10.5 %copy-start.6 = (s32[1,1,1,2,128]{4,3,2,1,0:T(2,128)S(1)}, s32[1,1,1,2,128]{4,3,2,1,0:T(2,128)}, u32[]{:S(2)}) copy-start(s32[1,1,1,2,128]{4,3,2,1,0:T(2,128)} %param.20) | copy-start | bytes 3076
  2.1 6.4 %collective-permute-start.1 = (f32[8,128]{1,0:T(8,128)S(1)}, f32[8,128]{1,0:T(8,128)S(1)}, u32[]{:S(2)}, u32[]{:S(2)}) collective-permute-start(f32[8,128]{1,0:T(8,128)S(1)} %shard_map.158), channel_id=1, source_target_pairs={{0,24},{8,0},{16,8},{24,16},{1,25},{9,1},{17,9},{25,17},{2,26},{10... | collective-permute-start | bytes 12296 | tf_op jit(solution)/shard_map/ppermute | solution.py:574
  7.2 5.4 %collective-permute-start = (f32[8,128]{1,0:T(8,128)S(1)}, f32[8,128]{1,0:T(8,128)S(1)}, u32[]{:S(2)}, u32[]{:S(2)}) collective-permute-start(f32[8,128]{1,0:T(8,128)S(1)} %shard_map.158), channel_id=1, source_target_pairs={{0,8},{8,16},{16,24},{24,0},{1,9},{9,17},{17,25},{25,1},{2,10},{10... | collective-permute-start | bytes 12296 | tf_op jit(solution)/shard_map/ppermute | solution.py:574
  12.6 6.9 %copy-start.4 = (s32[56,1,1,1,128]{4,3,2,1,0:T(1,128)S(1)}, s32[56,1,1,1,128]{4,3,2,1,0:T(1,128)}, u32[]{:S(2)}) copy-start(s32[56,1,1,1,128]{4,3,2,1,0:T(1,128)} %param.18) | copy-start | bytes 86020
  12.6 6.9 %copy-start.2 = (s32[56,1,1,1,128]{4,3,2,1,0:T(1,128)S(1)}, s32[56,1,1,1,128]{4,3,2,1,0:T(1,128)}, u32[]{:S(2)}) copy-start(s32[56,1,1,1,128]{4,3,2,1,0:T(1,128)} %param.17) | copy-start | bytes 86020
  12.7 3.0 %collective-permute-start.2 = (f32[8,128]{1,0:T(8,128)S(1)}, f32[8,128]{1,0:T(8,128)S(1)}, u32[]{:S(2)}, u32[]{:S(2)}) collective-permute-start(f32[8,128]{1,0:T(8,128)S(1)} %get-tuple-element.39), channel_id=1, source_target_pairs={{0,2},{2,4},{4,6},{6,0},{1,3},{3,5},{5,7},{7,1},{8,10},{10,12},{12... | collective-permute-start | bytes 12296 | tf_op jit(solution)/shard_map/ppermute | solution.py:574
  12.7 3.1 %collective-permute-start.3 = (f32[8,128]{1,0:T(8,128)S(1)}, f32[8,128]{1,0:T(8,128)S(1)}, u32[]{:S(2)}, u32[]{:S(2)}) collective-permute-start(f32[8,128]{1,0:T(8,128)S(1)} %get-tuple-element.40), channel_id=1, source_target_pairs={{0,6},{2,0},{4,2},{6,4},{1,7},{3,1},{5,3},{7,5},{8,14},{10,8},{12,... | collective-permute-start | bytes 12296 | tf_op jit(solution)/shard_map/ppermute | solution.py:574
  15.9 3.6 %collective-permute-start.4 = (f32[8,128]{1,0:T(8,128)S(1)}, f32[8,128]{1,0:T(8,128)S(1)}, u32[]{:S(2)}, u32[]{:S(2)}) collective-permute-start(f32[8,128]{1,0:T(8,128)S(1)} %get-tuple-element.43), channel_id=1, source_target_pairs={{0,1},{1,0},{2,3},{3,2},{4,5},{5,4},{6,7},{7,6},{8,9},{9,8},{10,11... | collective-permute-start | bytes 12296 | tf_op jit(solution)/shard_map/ppermute | solution.py:578
  20.1 0.9 %copy-start = (bf16[384,128]{1,0:T(8,128)(2,1)S(1)}, bf16[384,128]{1,0:T(8,128)(2,1)}, u32[]{:S(2)}) copy-start(bf16[384,128]{1,0:T(8,128)(2,1)} %mix_ref.5) | copy-start | bytes 294916
  22.4 4.0 %collective-permute-start.6 = (bf16[128,128]{1,0:T(8,128)(2,1)S(1)}, bf16[128,128]{1,0:T(8,128)(2,1)S(1)}, u32[]{:S(2)}, u32[]{:S(2)}) collective-permute-start(bf16[128,128]{1,0:T(8,128)(2,1)S(1)} %get-tuple-element.45), channel_id=1, source_target_pairs={{0,24},{8,0},{16,8},{24,16},{1,25},{9,1},{17,9},{25,17},{2,26},{10... | collective-permute-start | bytes 98312 | tf_op jit(solution)/shard_map/ppermute | solution.py:574
  22.5 5.8 %collective-permute-start.5 = (bf16[128,128]{1,0:T(8,128)(2,1)S(1)}, bf16[128,128]{1,0:T(8,128)(2,1)S(1)}, u32[]{:S(2)}, u32[]{:S(2)}) collective-permute-start(bf16[128,128]{1,0:T(8,128)(2,1)S(1)} %get-tuple-element.45), channel_id=1, source_target_pairs={{0,8},{8,16},{16,24},{24,0},{1,9},{9,17},{17,25},{25,1},{2,10},{10... | collective-permute-start | bytes 98312 | tf_op jit(solution)/shard_map/ppermute | solution.py:574
  28.5 3.4 %collective-permute-start.7 = (bf16[128,128]{1,0:T(8,128)(2,1)S(1)}, bf16[128,128]{1,0:T(8,128)(2,1)S(1)}, u32[]{:S(2)}, u32[]{:S(2)}) collective-permute-start(bf16[128,128]{1,0:T(8,128)(2,1)S(1)} %get-tuple-element.47), channel_id=1, source_target_pairs={{0,2},{2,4},{4,6},{6,0},{1,3},{3,5},{5,7},{7,1},{8,10},{10,12},{12... | collective-permute-start | bytes 98312 | tf_op jit(solution)/shard_map/ppermute | solution.py:574
  28.5 3.3 %collective-permute-start.8 = (bf16[128,128]{1,0:T(8,128)(2,1)S(1)}, bf16[128,128]{1,0:T(8,128)(2,1)S(1)}, u32[]{:S(2)}, u32[]{:S(2)}) collective-permute-start(bf16[128,128]{1,0:T(8,128)(2,1)S(1)} %get-tuple-element.48), channel_id=1, source_target_pairs={{0,6},{2,0},{4,2},{6,4},{1,7},{3,1},{5,3},{7,5},{8,14},{10,8},{12,... | collective-permute-start | bytes 98312 | tf_op jit(solution)/shard_map/ppermute | solution.py:574
  31.9 1.8 %copy-start.14 = (f32[128,16]{0,1:T(8,128)S(1)}, f32[128,16]{0,1:T(8,128)}, u32[]{:S(2)}) copy-start(f32[128,16]{0,1:T(8,128)} %param.28) | copy-start | bytes 24580
  31.9 4.2 %copy-start.3 = (bf16[384,128]{1,0:T(8,128)(2,1)S(1)}, bf16[384,128]{1,0:T(8,128)(2,1)}, u32[]{:S(2)}) copy-start(bf16[384,128]{1,0:T(8,128)(2,1)} %mix_ref.4) | copy-start | bytes 294916
  32.0 4.0 %collective-permute-start.9 = (bf16[128,128]{1,0:T(8,128)(2,1)S(1)}, bf16[128,128]{1,0:T(8,128)(2,1)S(1)}, u32[]{:S(2)}, u32[]{:S(2)}) collective-permute-start(bf16[128,128]{1,0:T(8,128)(2,1)S(1)} %shard_map.163), channel_id=1, source_target_pairs={{0,1},{1,0},{2,3},{3,2},{4,5},{5,4},{6,7},{7,6},{8,9},{9,8},{10,11... | collective-permute-start | bytes 98312 | tf_op jit(solution)/shard_map/ppermute | solution.py:578
  36.0 0.7 copy-start.11
  36.0 0.7 copy-start.12
  36.0 0.7 copy-start.13
  54.6 4.0 %collective-permute-start.10 = (bf16[128,128]{1,0:T(8,128)(2,1)S(1)}, bf16[128,128]{1,0:T(8,128)(2,1)S(1)}, u32[]{:S(2)}, u32[]{:S(2)}) collective-permute-start(bf16[128,128]{1,0:T(8,128)(2,1)S(1)} %get-tuple-element.55), channel_id=1, source_target_pairs={{0,1},{1,0},{2,3},{3,2},{4,5},{5,4},{6,7},{7,6},{8,9},{9,8},{10,11... | collective-permute-start | bytes 98312 | tf_op jit(solution)/shard_map/ppermute | solution.py:578
  58.7 3.4 %collective-permute-start.11 = (bf16[128,128]{1,0:T(8,128)(2,1)S(1)}, bf16[128,128]{1,0:T(8,128)(2,1)S(1)}, u32[]{:S(2)}, u32[]{:S(2)}) collective-permute-start(bf16[128,128]{1,0:T(8,128)(2,1)S(1)} %get-tuple-element.57), channel_id=1, source_target_pairs={{0,2},{2,4},{4,6},{6,0},{1,3},{3,5},{5,7},{7,1},{8,10},{10,12},{12... | collective-permute-start | bytes 98312 | tf_op jit(solution)/shard_map/ppermute | solution.py:574
  58.8 3.3 %collective-permute-start.12 = (bf16[128,128]{1,0:T(8,128)(2,1)S(1)}, bf16[128,128]{1,0:T(8,128)(2,1)S(1)}, u32[]{:S(2)}, u32[]{:S(2)}) collective-permute-start(bf16[128,128]{1,0:T(8,128)(2,1)S(1)} %get-tuple-element.58), channel_id=1, source_target_pairs={{0,6},{2,0},{4,2},{6,4},{1,7},{3,1},{5,3},{7,5},{8,14},{10,8},{12,... | collective-permute-start | bytes 98312 | tf_op jit(solution)/shard_map/ppermute | solution.py:574
  62.1 5.8 %copy-start.1 = (bf16[384,128]{1,0:T(8,128)(2,1)S(1)}, bf16[384,128]{1,0:T(8,128)(2,1)}, u32[]{:S(2)}) copy-start(bf16[384,128]{1,0:T(8,128)(2,1)} %mix_ref.5) | copy-start | bytes 294916
  62.3 5.6 %collective-permute-start.13 = (bf16[64,128]{1,0:T(8,128)(2,1)S(1)}, bf16[64,128]{1,0:T(8,128)(2,1)S(1)}, u32[]{:S(2)}, u32[]{:S(2)}) collective-permute-start(bf16[64,128]{1,0:T(8,128)(2,1)S(1)} %get-tuple-element.60), channel_id=1, source_target_pairs={{0,8},{8,16},{16,24},{24,0},{1,9},{9,17},{17,25},{25,1},{2,10},{10... | collective-permute-start | bytes 49160 | tf_op jit(solution)/shard_map/ppermute | solution.py:574
  62.5 5.4 %collective-permute-start.14 = (bf16[64,128]{1,0:T(8,128)(2,1)S(1)}, bf16[64,128]{1,0:T(8,128)(2,1)S(1)}, u32[]{:S(2)}, u32[]{:S(2)}) collective-permute-start(bf16[64,128]{1,0:T(8,128)(2,1)S(1)} %get-tuple-element.61), channel_id=1, source_target_pairs={{0,24},{8,0},{16,8},{24,16},{1,25},{9,1},{17,9},{25,17},{2,26},{10... | collective-permute-start | bytes 49160 | tf_op jit(solution)/shard_map/ppermute | solution.py:574
  71.3 3.7 %collective-permute-start.15 = (f32[8,128]{1,0:T(8,128)S(1)}, f32[8,128]{1,0:T(8,128)S(1)}, u32[]{:S(2)}, u32[]{:S(2)}) collective-permute-start(f32[8,128]{1,0:T(8,128)S(1)} %get-tuple-element.68), channel_id=1, source_target_pairs={{0,1},{1,0},{2,3},{3,2},{4,5},{5,4},{6,7},{7,6},{8,9},{9,8},{10,11... | collective-permute-start | bytes 12296 | tf_op jit(solution)/shard_map/ppermute | solution.py:578
  75.3 3.0 %collective-permute-start.16 = (f32[8,128]{1,0:T(8,128)S(1)}, f32[8,128]{1,0:T(8,128)S(1)}, u32[]{:S(2)}, u32[]{:S(2)}) collective-permute-start(f32[8,128]{1,0:T(8,128)S(1)} %get-tuple-element.70), channel_id=1, source_target_pairs={{0,2},{2,4},{4,6},{6,0},{1,3},{3,5},{5,7},{7,1},{8,10},{10,12},{12... | collective-permute-start | bytes 12296 | tf_op jit(solution)/shard_map/ppermute | solution.py:574
  75.3 3.1 %collective-permute-start.17 = (f32[8,128]{1,0:T(8,128)S(1)}, f32[8,128]{1,0:T(8,128)S(1)}, u32[]{:S(2)}, u32[]{:S(2)}) collective-permute-start(f32[8,128]{1,0:T(8,128)S(1)} %get-tuple-element.71), channel_id=1, source_target_pairs={{0,6},{2,0},{4,2},{6,4},{1,7},{3,1},{5,3},{7,5},{8,14},{10,8},{12,... | collective-permute-start | bytes 12296 | tf_op jit(solution)/shard_map/ppermute | solution.py:574
  78.7 5.2 %collective-permute-start.19 = (f32[8,128]{1,0:T(8,128)S(1)}, f32[8,128]{1,0:T(8,128)S(1)}, u32[]{:S(2)}, u32[]{:S(2)}) collective-permute-start(f32[8,128]{1,0:T(8,128)S(1)} %get-tuple-element.73), channel_id=1, source_target_pairs={{0,24},{8,0},{16,8},{24,16},{1,25},{9,1},{17,9},{25,17},{2,26},{10... | collective-permute-start | bytes 12296 | tf_op jit(solution)/shard_map/ppermute | solution.py:574
  82.6 5.4 %collective-permute-start.18 = (f32[8,128]{1,0:T(8,128)S(1)}, f32[8,128]{1,0:T(8,128)S(1)}, u32[]{:S(2)}, u32[]{:S(2)}) collective-permute-start(f32[8,128]{1,0:T(8,128)S(1)} %get-tuple-element.73), channel_id=1, source_target_pairs={{0,8},{8,16},{16,24},{24,0},{1,9},{9,17},{17,25},{25,1},{2,10},{10... | collective-permute-start | bytes 12296 | tf_op jit(solution)/shard_map/ppermute | solution.py:574
  (3 other events, 2.0 us)

commit v2 on v1

v2 whole, which is shorter than its diff:
```python
import functools
import math

import jax
import jax.numpy as jnp
from jax import lax
from jax.experimental import pallas as pl
from jax.experimental.pallas import tpu as pltpu
from jax.sharding import PartitionSpec as P

NB = 8
LX = 4
LY = 4
LZ = 8

SPACING = 1.8
CUTOFF = 5.0
SPREAD = 0.4
HIGHEST = lax.Precision.HIGHEST
F32 = jnp.float32
BF16 = jnp.bfloat16

ROOT3 = 3.0**0.5
ROOT5 = 5.0**0.5
ROOT15 = 15.0**0.5
GROUP = 4


def dot(a, b, ca=1, cb=0, precision=None):
    return lax.dot_general(
        a, b, (((ca,), (cb,)), ((), ())), precision=precision, preferred_element_type=F32
    )


def split2(x):
    hi = x.astype(BF16)
    lo = (x - hi.astype(F32)).astype(BF16)
    return hi, lo


def dot_split(a, b, ca=1, cb=0):
    hi, lo = split2(b)
    return dot(a, hi, ca, cb) + dot(a, lo, ca, cb)


def onehot(row, size):
    count = row.shape[-1]
    ids = lax.broadcasted_iota(jnp.int32, (size, count), 0)
    return jnp.where(ids == row, 1.0, 0.0).astype(BF16)


def lane_pick(blocks, rows):
    width = blocks[0].shape[-1]
    shift = width.bit_length() - 1
    lane = rows & (width - 1)
    block = rows >> shift
    out = jnp.take_along_axis(blocks[0], lane, axis=1)
    for index in range(1, len(blocks)):
        part = jnp.take_along_axis(blocks[index], lane, axis=1)
        out = jnp.where(block == index, part, out)
    return out


def spread_rows(row, count):
    return jnp.broadcast_to(row, (count, row.shape[-1]))


def by_side(side_ref, axis, if_odd, if_even):
    odd = side_ref[axis : axis + 1, 0 : if_odd.shape[1]] == 1
    return jnp.where(odd, if_odd, if_even)


def near_far(side_ref, axis, face_ref):
    low, high = face_ref[0:1, :], face_ref[1:2, :]
    return by_side(side_ref, axis, low, high), by_side(side_ref, axis, high, low)


def face_row(side_ref, fx_ref):
    return jnp.concatenate(near_far(side_ref, 0, fx_ref), axis=1)


def half_turn(x):
    half = x.shape[1] // 2
    return jnp.concatenate([x[:, half:], x[:, :half]], axis=1)


def low_lanes(shape):
    return lax.broadcasted_iota(jnp.int32, shape, 1) < shape[1] // 2


def shift_rows(shape, axis, amount):
    ids = lax.broadcasted_iota(jnp.int32, shape, 0)
    return jnp.where(ids == axis, amount, 0.0)


def pos_x_kernel(pos_ref, fx_ref, side_ref, coords_ref, send_ref):
    ids = lax.broadcasted_iota(jnp.int32, side_ref.shape, 0)
    first, second = lax.axis_index("gx") % 2, lax.axis_index("gy") % 2
    value = jnp.where(ids == 0, first, jnp.where(ids == 1, second, lax.axis_index("gz")))
    side_ref[...] = value
    rows = [pos_ref[i] for i in range(3)]
    coords = jnp.concatenate(rows + [jnp.zeros_like(rows[0])] * 5, axis=0)
    coords_ref[...] = coords
    send_ref[...] = lane_pick([coords], spread_rows(face_row(side_ref, fx_ref), 8))


def pos_y_kernel(side_ref, pos_ref, near_ref, far_ref, fy_ref, p1_ref, to_near_ref, to_far_ref):
    coords = pos_ref[...]
    shape = coords.shape
    first = low_lanes(shape)
    both = jnp.where(first, near_ref[...], far_ref[...])
    both = by_side(side_ref, 0, both, half_turn(both))
    step = shift_rows(shape, 0, LX * SPACING)
    ghost = jnp.where(first, both - step, both + step)
    p1_ref[...] = ghost
    near, far = near_far(side_ref, 1, fy_ref)
    to_near_ref[...] = lane_pick([coords, ghost], spread_rows(near, 8))
    to_far_ref[...] = lane_pick([coords, ghost], spread_rows(far, 8))


def pos_z_kernel(side_ref, pos_ref, p1_ref, near_ref, far_ref, fz_ref, p2_ref, p3_ref, out_ref):
    coords = pos_ref[...]
    shape = coords.shape
    near, far = near_ref[...], far_ref[...]
    low = by_side(side_ref, 1, near, far) - shift_rows(shape, 1, LY * SPACING)
    high = by_side(side_ref, 1, far, near) + shift_rows(shape, 1, LY * SPACING)
    p2_ref[...] = low
    p3_ref[...] = high
    out_ref[...] = lane_pick([coords, p1_ref[...], low, high], spread_rows(fz_ref[...], 8))


def layer_one_kernel(
    side_ref,
    pos_ref,
    p1_ref,
    p2_ref,
    p3_ref,
    pz_ref,
    nbr_ref,
    keep_ref,
    fx_ref,
    radial_ref,
    mix_ref,
    embed_ref,
    unit_ref,
    rinv_ref,
    basis_ref,
    slope_ref,
    amp_ref,
    h0_ref,
    to_near_ref,
    to_far_ref,
    mom_ref,
):
    entries, atoms = nbr_ref.shape
    nbr = nbr_ref[...]
    lane = nbr & (atoms - 1)
    block = nbr >> (atoms.bit_length() - 1)
    rise = jnp.where(side_ref[2:3, :] == 0, LZ * SPACING, -LZ * SPACING)
    last = pz_ref[...] + shift_rows(pz_ref.shape, 2, rise)
    tables = [pos_ref[...], p1_ref[...], p2_ref[...], p3_ref[...], last]
    vec = []
    for axis in range(3):
        got = None
        for index, table in enumerate(tables):
            spread = spread_rows(table[axis : axis + 1, :], entries)
            part = jnp.take_along_axis(spread, lane, axis=1)
            got = part if index == 0 else jnp.where(block == index, part, got)
        vec.append(got - pos_ref[axis : axis + 1, :])
    r_sq = vec[0] * vec[0] + vec[1] * vec[1] + vec[2] * vec[2]
    dist = jnp.sqrt(r_sq)
    rinv = 1.0 / dist
    ux, uy, uz = (v * rinv for v in vec)
    rinv_ref[...] = rinv
    unit_ref[0:entries, :] = ux
    unit_ref[entries : 2 * entries, :] = uy
    unit_ref[2 * entries : 3 * entries, :] = uz
    scaled = jnp.minimum(dist * (1.0 / CUTOFF), 1.0)
    phase = scaled * math.pi
    sine = jnp.sin(phase)
    cosine = jnp.cos(phase)
    inner = 1.0 - scaled * scaled
    weight = keep_ref[...].astype(F32) * (2.0 / CUTOFF) ** 0.5
    env = weight * inner * inner * rinv
    env_slope = -env * rinv - weight * rinv * (4.0 / CUTOFF) * scaled * inner
    twice = 2.0 * cosine
    s_prev, s_now = jnp.zeros_like(sine), sine
    c_prev, c_now = jnp.ones_like(cosine), cosine
    basis = []
    for k in range(NB):
        bk = s_now * env
        basis.append(bk)
        basis_ref[k * entries : (k + 1) * entries, :] = bk
        slope_ref[k * entries : (k + 1) * entries, :] = (
            c_now * env * ((k + 1) * math.pi / CUTOFF) + s_now * env_slope
        )
        s_prev, s_now = s_now, twice * s_now - s_prev
        c_prev, c_now = c_now, twice * c_now - c_prev
    angular = harmonics(ux, uy, uz)
    for m in range(9):
        for k in range(NB):
            prod = basis[k] if m == 0 else basis[k] * angular[m]
            mom_ref[k : k + 1, m * atoms : (m + 1) * atoms] = jnp.sum(prod, axis=0, keepdims=True)
    amp = SPREAD * dot(radial_ref[...], mom_ref[...], 0, 0, HIGHEST)
    amp_ref[...] = amp
    inv = invariants([amp[:, m * atoms : (m + 1) * atoms] for m in range(9)])
    h1 = dot(mix_ref[...], inv, 0, 0)
    h1 = h1 + dot(embed_ref[...], jnp.ones((1, atoms), F32), 0, 0, HIGHEST)
    h1b = h1.astype(BF16)
    h0_ref[...] = h1b
    both = dot(h1b, onehot(face_row(side_ref, fx_ref), atoms))
    to_near_ref[...], to_far_ref[...] = pack_halves(both)


def harmonics(ux, uy, uz):
    return [
        None,
        ROOT3 * ux,
        ROOT3 * uy,
        ROOT3 * uz,
        ROOT15 * ux * uy,
        ROOT15 * uy * uz,
        0.5 * ROOT5 * (3.0 * uz * uz - 1.0),
        ROOT15 * ux * uz,
        0.5 * ROOT15 * (ux * ux - uy * uy),
    ]


def invariants(amp):
    first = amp[1] * amp[1] + amp[2] * amp[2] + amp[3] * amp[3]
    second = amp[4] * amp[4] + amp[5] * amp[5] + amp[6] * amp[6]
    second = second + amp[7] * amp[7] + amp[8] * amp[8]
    return jnp.concatenate([amp[0], first, second], axis=0).astype(BF16)


def pack_halves(both):
    rows, _ = both.shape
    top, low = both[0 : rows // 2], both[rows // 2 :]
    first = low_lanes(top.shape)
    near = jnp.where(first, top, half_turn(low))
    far = jnp.where(first, half_turn(top), low)
    return near.astype(BF16), far.astype(BF16)


def unpack_halves(low, high):
    first = low_lanes(low.shape)
    top = jnp.where(first, low, half_turn(high))
    bottom = jnp.where(first, half_turn(low), high)
    return jnp.concatenate([top, bottom], axis=0)


def feat_y_kernel(side_ref, h0_ref, near_ref, far_ref, fy_ref, h1_ref, to_near_ref, to_far_ref):
    near, far = near_ref[...].astype(F32), far_ref[...].astype(F32)
    low, high = by_side(side_ref, 0, near, far), by_side(side_ref, 0, far, near)
    ghost = unpack_halves(low, high).astype(BF16)
    h1_ref[...] = ghost
    table = jnp.concatenate([h0_ref[...], ghost], axis=1)
    size = table.shape[1]
    near, far = near_far(side_ref, 1, fy_ref)
    to_near_ref[...] = dot(table, onehot(near, size)).astype(BF16)
    to_far_ref[...] = dot(table, onehot(far, size)).astype(BF16)


def sides(side_ref, axis, near_ref, far_ref):
    near, far = near_ref[...].astype(F32), far_ref[...].astype(F32)
    low, high = by_side(side_ref, axis, near, far), by_side(side_ref, axis, far, near)
    return low.astype(BF16), high.astype(BF16)


def feat_z_kernel(side_ref, h0_ref, h1_ref, near_ref, far_ref, fz_ref, out_ref, h2_ref, h3_ref):
    low, high = sides(side_ref, 1, near_ref, far_ref)
    h2_ref[...] = low
    h3_ref[...] = high
    table = jnp.concatenate([h0_ref[...], h1_ref[...], low, high], axis=1)
    out_ref[...] = dot(table, onehot(fz_ref[...], table.shape[1])).astype(BF16)


def entry_rows(ref, first):
    return jnp.concatenate([ref[pl.ds(first + jj, 1), :] for jj in range(GROUP)], axis=1)


def hot_kernel(nbr_ref, hot_ref, lane_ref):
    atoms = nbr_ref.shape[1]

    def body(step, carry):
        row = entry_rows(nbr_ref, step * GROUP)
        hot_ref[step] = onehot(row, hot_ref.shape[1])
        lane_ref[step] = onehot(row & (atoms - 1), atoms)
        return carry

    lax.fori_loop(0, hot_ref.shape[0], body, 0)


def stack3(hi, lo):
    return jnp.concatenate([hi, lo, hi], axis=0).astype(BF16)


def radial_kernel(basis_ref, slope_ref, unit_ref, radial_ref, rad_ref, slo_ref, y_ref, rts_ref):
    entries = basis_ref.shape[0] // NB
    channels = radial_ref.shape[1]
    rt = radial_ref[...]
    hi = rt.astype(BF16).astype(F32)
    lo = rt - hi
    pad = jnp.zeros((channels - 3 * NB, channels), F32)
    rts_ref[...] = jnp.transpose(jnp.concatenate([hi, hi, lo, pad], axis=0)).astype(BF16)
    ux = unit_ref[0:entries, :]
    uy = unit_ref[entries : 2 * entries, :]
    uz = unit_ref[2 * entries : 3 * entries, :]
    for m, val in enumerate(harmonics(ux, uy, uz)):
        if m:
            y_ref[(m - 1) * entries : m * entries, :] = val

    def radial_cols(ref, first):
        cols = [ref[pl.ds(first + jj, NB, stride=entries), :] for jj in range(GROUP)]
        value = jnp.concatenate(cols, axis=1)
        top = value.astype(BF16).astype(F32)
        return stack3(top, value - top)

    rts = rts_ref[:, 0 : 3 * NB]
    for step in range(rad_ref.shape[0]):
        rad_ref[step] = dot(rts, radial_cols(basis_ref, step * GROUP))
        slo_ref[step] = dot(rts, radial_cols(slope_ref, step * GROUP))


def gather_first_kernel(h0_ref, h1_ref, hot_ref, hg_ref, table_ref):
    atoms = h0_ref.shape[1]
    table_ref[:, 0:atoms] = h0_ref[...]
    table_ref[:, atoms:] = h1_ref[...]

    for step in range(hot_ref.shape[0]):
        hg_ref[step] = dot(table_ref[...], hot_ref[step, 0 : 2 * atoms, :])


def gather_more_kernel(h2_ref, h3_ref, hot_ref, old_ref, hg_ref, table_ref):
    atoms = h2_ref.shape[1]
    table_ref[:, 0:atoms] = h2_ref[...]
    table_ref[:, atoms:] = h3_ref[...]

    for step in range(hot_ref.shape[0]):
        more = dot(table_ref[...], hot_ref[step, 2 * atoms : 4 * atoms, :])
        hg_ref[step] = old_ref[step] + more


def layer_two_kernel(
    h0_ref,
    h4_ref,
    hot_ref,
    old_ref,
    rad_ref,
    y_ref,
    occ_ref,
    mix_ref,
    rone_ref,
    rhid_ref,
    rout_ref,
    hg_ref,
    en_ref,
    raw_ref,
    extra_ref,
    rq_ref,
    gy_ref,
    gz_ref,
    acc_ref,
    dh_ref,
):
    channels, atoms = h0_ref.shape
    steps = hot_ref.shape[0]
    entries = steps * GROUP
    blocks = channels // 8
    acc_ref[...] = jnp.zeros_like(acc_ref)

    def prepare(step):
        hg_ref[step] = old_ref[step] + dot(h4_ref[...], hot_ref[step, 4 * atoms :, :])

    def accumulate(step):
        first = step * GROUP
        for pair in range(blocks // 2):
            spans = [slice(cb * 8, cb * 8 + 8) for cb in (2 * pair, 2 * pair + 1)]
            msgs = []
            for rows in spans:
                line = []
                for jj in range(GROUP):
                    cols = slice(jj * atoms, (jj + 1) * atoms)
                    line.append(hg_ref[step, rows, cols] * rad_ref[step, rows, cols])
                msgs.append(line)
            for m in range(9):
                if m:
                    at = (m - 1) * entries + first
                    yvs = [y_ref[pl.ds(at + jj, 1), :] for jj in range(GROUP)]
                for rows, line in zip(spans, msgs):
                    if m:
                        terms = [line[jj] * yvs[jj] for jj in range(GROUP)]
                    else:
                        terms = line
                    while len(terms) > 1:
                        terms = [a + b for a, b in zip(terms[::2], terms[1::2])]
                    acc_ref[m, rows, :] += terms[0]

    prepare(0)

    def forward_body(step, carry):
        accumulate(step - 1)
        prepare(step)
        return carry

    lax.fori_loop(1, steps, forward_body, 0)
    accumulate(steps - 1)

    occ = occ_ref[...].astype(F32)
    ones = jnp.ones((1, atoms), F32)
    amp = [SPREAD * acc_ref[m] for m in range(9)]
    own = h0_ref[...].astype(F32)
    h2 = dot(mix_ref[...], invariants(amp), 0, 0) + own
    pre = dot(rhid_ref[...], h2, 1, 0, HIGHEST)
    sig = 1.0 / (1.0 + jnp.exp(-pre))
    rout = dot(rout_ref[...], ones, 0, 0, HIGHEST)
    rone = dot(rone_ref[...], ones, 0, 0, HIGHEST)
    energy = jnp.sum(own * rone, axis=0, keepdims=True)
    energy = energy + jnp.sum(rout * pre * sig, axis=0, keepdims=True)
    en_ref[...] = occ * energy
    dpre = occ * rout * sig * (1.0 + pre * (1.0 - sig))
    dh2 = dot(rhid_ref[...], dpre, 0, 0, HIGHEST)
    dinv = dot_split(mix_ref[...], dh2)
    low = dinv[channels : 2 * channels]
    top = dinv[2 * channels :]
    extra_ref[...] = dh2 + occ * rone
    twice = 2.0 * SPREAD
    raw_ref[0] = SPREAD * dinv[0:channels]
    for m in range(1, 9):
        raw_ref[m] = (twice * amp[m]) * (low if m < 4 else top)
    dh_ref[...] = jnp.zeros_like(dh_ref)

    def reverse(step):
        first = step * GROUP
        for pair in range(blocks // 2):
            spans = [slice(cb * 8, cb * 8 + 8) for cb in (2 * pair, 2 * pair + 1)]
            ds = [[raw_ref[m, rows, :] for m in range(9)] for rows in spans]
            for jj in range(GROUP):
                cols = slice(jj * atoms, (jj + 1) * atoms)
                yvs = [y_ref[pl.ds((m - 1) * entries + first + jj, 1), :] for m in range(1, 9)]
                parts = []
                for rows, d in zip(spans, ds):
                    terms = [d[0]] + [yv * dm for yv, dm in zip(yvs, d[1:])]
                    q = terms[0] + terms[1]
                    for a, b in ((2, 3), (4, 5), (6, 7)):
                        q = q + (terms[a] + terms[b])
                    parts.append(rad_ref[step, rows, cols] * (q + terms[8]))
                value = jnp.concatenate(parts, axis=0).astype(BF16)
                rq_ref[step, pair * 16 : pair * 16 + 16, cols] = value

    def send(step):
        dh_ref[...] += dot(hot_ref[step, 2 * atoms :, :], rq_ref[step], 1, 1)

    reverse(0)

    def reverse_body(step, carry):
        send(step - 1)
        reverse(step)
        return carry

    lax.fori_loop(1, steps, reverse_body, 0)
    send(steps - 1)
    gy_ref[...] = dh_ref[0 : 2 * atoms, :].astype(BF16)
    gz_ref[...] = dh_ref[2 * atoms :, :].astype(BF16)


def directions(d, unit):
    vx, vy, vz = unit
    cx = vy * d[4] + vz * d[7] + vx * d[8]
    cy = vx * d[4] + vz * d[5] - vy * d[8]
    cz = vy * d[5] + vx * d[7] + vz * d[6]
    return d[1] + cx, d[2] + cy, d[3] + cz, (cx, cy, cz)


def scatter_kernel(first, hot_ref, rq_ref, out_ref):
    size = out_ref.shape[0]
    total = None
    for step in range(hot_ref.shape[0]):
        part = dot(hot_ref[step, first : first + size, :], rq_ref[step], 1, 1)
        total = part if total is None else total + part
    out_ref[...] = total


def edge_kernel(start, hg_ref, rad_ref, slo_ref, d_ref, unit_ref, grad_ref, dd_ref):
    channels, atoms = d_ref.shape[1:]
    entries = hg_ref.shape[0] * GROUP
    count = grad_ref.shape[0] // (4 * GROUP)
    for m in range(9):
        if m == 0:
            dd_ref[m] = d_ref[0] - (0.5 * ROOT5) * d_ref[6]
        elif m < 4:
            dd_ref[m] = ROOT3 * d_ref[m]
        else:
            dd_ref[m] = (1.5 * ROOT5 if m == 6 else 0.5 * ROOT15) * d_ref[m]

    def body(step, carry):
        first = step * GROUP
        units = []
        for jj in range(GROUP):
            units.append([unit_ref[pl.ds(i * entries + first + jj, 1), :] for i in range(3)])
        sums = [[None] * 4 for _ in range(GROUP)]
        for cb in range(channels // 8):
            rows = slice(cb * 8, cb * 8 + 8)
            d = [dd_ref[m, rows, :] for m in range(9)]
            for jj in range(GROUP):
                cols = slice(jj * atoms, (jj + 1) * atoms)
                hg = hg_ref[step, rows, cols]
                ex, ey, ez, (cx, cy, cz) = directions(d, units[jj])
                vx, vy, vz = units[jj]
                q = d[0] + vx * ex + vy * ey + vz * ez
                msg = hg * rad_ref[step, rows, cols]
                parts = [
                    msg * (ex + cx),
                    msg * (ey + cy),
                    msg * (ez + cz),
                    hg * q * slo_ref[step, rows, cols],
                ]
                for i in range(4):
                    prior = sums[jj][i]
                    sums[jj][i] = parts[i] if prior is None else prior + parts[i]
        for jj in range(GROUP):
            for i in range(4):
                row = pl.ds(i * count * GROUP + first - start * GROUP + jj, 1)
                grad_ref[row, :] = jnp.sum(sums[jj][i], axis=0, keepdims=True)
        return carry

    lax.fori_loop(start, start + count, body, 0)


def fold_z_kernel(side_ref, gy_ref, az_ref, fz_ref, acc_ref, to_near_ref, to_far_ref):
    size = gy_ref.shape[0]
    quarter = size // 2
    add = dot(onehot(fz_ref[...], 2 * size), az_ref[...])
    acc_ref[...] = add[0:size]
    rows = gy_ref[...].astype(F32) + add[size:]
    low, high = rows[0:quarter], rows[quarter:]
    to_near_ref[...] = by_side(side_ref, 1, low, high).astype(BF16)
    to_far_ref[...] = by_side(side_ref, 1, high, low).astype(BF16)


def fold_y_kernel(
    side_ref, acc_ref, gx_ref, extra_ref, near_ref, far_ref, fy_ref, own_ref, to_near_ref, to_far_ref
):
    size = acc_ref.shape[0]
    half = size // 2
    quarter = half // 2
    near, far = near_far(side_ref, 1, fy_ref)
    rows = acc_ref[...] + dot(onehot(near, size), near_ref[...])
    rows = rows + dot(onehot(far, size), far_ref[...])
    own = gx_ref[0:half, :] + jnp.transpose(extra_ref[...])
    own_ref[...] = rows[0:half] + own.astype(BF16).astype(F32)
    ghost = rows[half:] + gx_ref[half:, :].astype(BF16).astype(F32)
    low, high = ghost[0:quarter], ghost[quarter:]
    to_near_ref[...] = by_side(side_ref, 0, low, high).astype(BF16)
    to_far_ref[...] = by_side(side_ref, 0, high, low).astype(BF16)


def layer_one_reverse_kernel(
    side_ref,
    own_ref,
    near_ref,
    far_ref,
    fx_ref,
    amp_ref,
    nbr_ref,
    unit_ref,
    rinv_ref,
    basis_ref,
    slope_ref,
    ga_ref,
    gb_ref,
    gc_ref,
    lane_ref,
    radial_ref,
    mix_ref,
    f0_ref,
    f1_ref,
    f2_ref,
    f3_ref,
    f4_ref,
    dv_ref,
    sc_ref,
):
    entries, atoms = nbr_ref.shape
    channels = own_ref.shape[1]
    rows = own_ref[...]
    near, far = near_far(side_ref, 0, fx_ref)
    rows = rows + dot(onehot(near, atoms), near_ref[...])
    rows = rows + dot(onehot(far, atoms), far_ref[...])
    cot = jnp.transpose(rows)
    dinv = dot_split(mix_ref[...], cot)
    low = dinv[channels : 2 * channels]
    top = dinv[2 * channels :]
    pieces = [dinv[0:channels]]
    for m in range(1, 9):
        amp = amp_ref[:, m * atoms : (m + 1) * atoms]
        pieces.append(2.0 * amp * (low if m < 4 else top))
    dmom = SPREAD * dot(radial_ref[...], jnp.concatenate(pieces, axis=1), 1, 0, HIGHEST)
    ux = unit_ref[0:entries, :]
    uy = unit_ref[entries : 2 * entries, :]
    uz = unit_ref[2 * entries : 3 * entries, :]
    basis = [basis_ref[k * entries : (k + 1) * entries, :] for k in range(NB)]
    slope = [slope_ref[k * entries : (k + 1) * entries, :] for k in range(NB)]
    angular = harmonics(ux, uy, uz)
    edge = []
    for i in range(4):
        rows = []
        for ref in (ga_ref, gb_ref, gc_ref):
            count = ref.shape[0] // 4
            rows.append(ref[i * count : (i + 1) * count, :])
        edge.append(jnp.concatenate(rows, axis=0))
    dr = edge[3]
    dy = []
    for m in range(9):
        part = None
        sl = None
        for k in range(NB):
            row = dmom[k : k + 1, m * atoms : (m + 1) * atoms]
            sl = slope[k] * row if sl is None else sl + slope[k] * row
            if m:
                part = basis[k] * row if part is None else part + basis[k] * row
        dr = dr + (sl if m == 0 else sl * angular[m])
        dy.append(part)
    wx = edge[0] + ROOT3 * dy[1]
    wx = wx + ROOT15 * (uy * dy[4] + uz * dy[7] + ux * dy[8])
    wy = edge[1] + ROOT3 * dy[2]
    wy = wy + ROOT15 * (ux * dy[4] + uz * dy[5] - uy * dy[8])
    wz = edge[2] + ROOT3 * dy[3]
    wz = wz + ROOT15 * (uy * dy[5] + ux * dy[7]) + (3.0 * ROOT5) * uz * dy[6]
    rinv = rinv_ref[...]
    along = dr - rinv * (ux * wx + uy * wy + uz * wz)
    grads = [wx * rinv + along * ux, wy * rinv + along * uy, wz * rinv + along * uz]
    centre = []
    for i in range(3):
        centre.append(jnp.sum(grads[i], axis=0, keepdims=True))
        top16 = grads[i].astype(BF16).astype(F32)
        dv_ref[i * entries : (i + 1) * entries, :] = top16
        dv_ref[(3 + i) * entries : (4 + i) * entries, :] = grads[i] - top16
    shift = atoms.bit_length() - 1
    total = None
    for step in range(entries // GROUP):
        first = step * GROUP
        block = entry_rows(nbr_ref, first) >> shift
        cols = [dv_ref[pl.ds(first + jj, 6, stride=entries), :] for jj in range(GROUP)]
        value = jnp.concatenate(cols, axis=1)
        value = jnp.concatenate([value, jnp.zeros_like(value[0:2])], axis=0)
        parts = [jnp.where(block == index, value, 0.0) for index in range(5)]
        part = dot(jnp.concatenate(parts, axis=0).astype(BF16), lane_ref[step], 1, 1)
        total = part if total is None else total + part
    sc_ref[...] = total
    zero = jnp.zeros((5, atoms), F32)
    own = jnp.concatenate(centre + [zero], axis=0)
    for index, ref in enumerate((f0_ref, f1_ref, f2_ref, f3_ref, f4_ref)):
        base = index * 8
        value = sc_ref[base : base + 3, :] + sc_ref[base + 3 : base + 6, :]
        value = jnp.concatenate([value, zero], axis=0)
        ref[...] = value - own if index == 0 else value


def scatter_lanes(values, row, size):
    return dot(values, onehot(row, size).astype(F32), 1, 1, HIGHEST)


def force_z_kernel(
    side_ref, f0_ref, f1_ref, f2_ref, f3_ref, az_ref, fz_ref, out_ref, to_near_ref, to_far_ref
):
    atoms = f0_ref.shape[1]
    add = scatter_lanes(az_ref[...], fz_ref[...], 4 * atoms)
    out_ref[:, 0:atoms] = f0_ref[...] + add[:, 0:atoms]
    out_ref[:, atoms : 2 * atoms] = f1_ref[...] + add[:, atoms : 2 * atoms]
    low = f2_ref[...] + add[:, 2 * atoms : 3 * atoms]
    high = f3_ref[...] + add[:, 3 * atoms :]
    to_near_ref[...] = by_side(side_ref, 1, low, high)
    to_far_ref[...] = by_side(side_ref, 1, high, low)


def force_y_kernel(side_ref, acc_ref, near_ref, far_ref, fy_ref, own_ref, ghost_ref):
    size = acc_ref.shape[1]
    rows = acc_ref[...]
    near, far = near_far(side_ref, 1, fy_ref)
    rows = rows + scatter_lanes(near_ref[...], near, size)
    rows = rows + scatter_lanes(far_ref[...], far, size)
    own_ref[...] = rows[:, 0 : size // 2]
    ghost = rows[:, size // 2 :]
    ghost_ref[...] = by_side(side_ref, 0, ghost, half_turn(ghost))


def force_x_kernel(side_ref, own_ref, near_ref, far_ref, fx_ref, out_ref):
    size = own_ref.shape[1]
    both = jnp.where(low_lanes(own_ref.shape), near_ref[...], far_ref[...])
    rows = own_ref[...] + scatter_lanes(both, face_row(side_ref, fx_ref), size)
    for i in range(3):
        out_ref[i] = -rows[i : i + 1]


def call(kernel, outs, *args, scratch=(), vmem=8, aliases={}, cost=1):
    specs = []
    for arg in args:
        specs.append(pl.BlockSpec(memory_space=pltpu.VMEM))
    single = not isinstance(outs, (list, tuple))
    shapes = [outs] if single else list(outs)
    result = pl.pallas_call(
        kernel,
        out_shape=shapes,
        in_specs=specs,
        out_specs=[pl.BlockSpec(memory_space=pltpu.VMEM)] * len(shapes),
        scratch_shapes=list(scratch),
        input_output_aliases=aliases,
        cost_estimate=pl.CostEstimate(
            flops=cost * 10**9, bytes_accessed=cost * 10**6, transcendentals=0
        ),
        compiler_params=pltpu.CompilerParams(vmem_limit_bytes=vmem * 1024 * 1024),
    )(*args)
    return result[0] if single else result


def pair_swap(x, axis, far):
    count = lax.axis_size(axis)
    assert count % 2 == 0
    pairs = []
    for i in range(count):
        up = (i % 2 == 0) != far
        pairs.append((i, (i + (1 if up else -1)) % count))
    return lax.ppermute(x, axis, pairs)


def partner(x):
    axis = "gz"
    return lax.ppermute(x, axis, [(i, i ^ 1) for i in range(lax.axis_size(axis))])


def swap_both(near, far, axis):
    from_far = pair_swap(far, axis, True)
    from_near = pair_swap(near, axis, False)
    return from_near, from_far


def per_device(
    positions,
    occupancy,
    neighbours,
    keep,
    face_x,
    face_y,
    face_z,
    radial_one,
    mix_one,
    embed,
    radial_two,
    mix_two,
    read_one,
    read_hidden,
    read_out,
):
    atoms = positions.shape[-1]
    entries = neighbours.shape[0]
    channels = radial_one.shape[1]
    pos = positions.reshape(3, 1, atoms)
    nbr = neighbours.reshape(entries, atoms)
    kept = keep.reshape(entries, atoms)
    occ = occupancy.reshape(1, atoms)
    fx = face_x.reshape(2, face_x.shape[-1])
    fy = face_y.reshape(2, face_y.shape[-1])
    fz = face_z.reshape(1, face_z.shape[-1])
    embed = embed.reshape(1, channels)
    read_one = read_one.reshape(1, channels)
    read_out = read_out.reshape(1, read_out.shape[0])
    read_hidden = read_hidden.T

    def f32(*shape):
        return jax.ShapeDtypeStruct(shape, F32)

    def b16(*shape):
        return jax.ShapeDtypeStruct(shape, BF16)

    small = f32(8, atoms)
    side = jax.ShapeDtypeStruct((8, atoms), jnp.int32)
    side, pos, sent = call(pos_x_kernel, [side, small, small], pos, fx)
    steps = entries // GROUP
    width = GROUP * atoms
    hot, lanes = call(
        hot_kernel, [b16(steps, 5 * atoms, width), b16(steps, atoms, width)], nbr
    )
    near, far = swap_both(sent, sent, "gx")
    p1, near, far = call(pos_y_kernel, [small] * 3, side, pos, near, far, fy)
    near, far = swap_both(near, far, "gy")
    p2, p3, sent = call(pos_z_kernel, [small] * 3, side, pos, p1, near, far, fz)
    pz = partner(sent)

    half = atoms // 2
    square = b16(channels, atoms)
    unit, rinv, basis, slope, amp, h0, near, far = call(
        layer_one_kernel,
        [
            f32(3 * entries, atoms),
            f32(entries, atoms),
            f32(NB * entries, atoms),
            f32(NB * entries, atoms),
            f32(channels, 9 * atoms),
            square,
            b16(channels // 2, atoms),
            b16(channels // 2, atoms),
        ],
        side,
        pos,
        p1,
        p2,
        p3,
        pz,
        nbr,
        kept,
        fx,
        radial_one,
        mix_one,
        embed,
        scratch=[pltpu.VMEM((NB, 9 * atoms), F32)],
    )
    big = f32(steps, channels, width)
    rad, slo, ylm = call(
        radial_kernel,
        [big, big, f32(8 * entries, atoms)],
        basis,
        slope,
        unit,
        radial_two,
        scratch=[pltpu.VMEM((channels, channels), BF16)],
    )
    near, far = swap_both(near, far, "gx")
    h1, near, far = call(feat_y_kernel, [square] * 3, side, h0, near, far, fy)
    table = [pltpu.VMEM((channels, 2 * atoms), BF16)]
    hg = call(gather_first_kernel, big, h0, h1, hot, scratch=table)
    near, far = swap_both(near, far, "gy")
    sent, h2, h3 = call(feat_z_kernel, [square] * 3, side, h0, h1, near, far, fz)
    hg = call(gather_more_kernel, big, h2, h3, hot, hg, scratch=table, aliases={3: 0})
    h4 = partner(sent)

    hg, energies, dmat, extra, rq, gy, gz = call(
        layer_two_kernel,
        [
            big,
            f32(1, atoms),
            f32(9, channels, atoms),
            f32(channels, atoms),
            b16(steps, channels, width),
            b16(2 * atoms, channels),
            b16(atoms, channels),
        ],
        h0,
        h4,
        hot,
        hg,
        rad,
        ylm,
        occ,
        mix_two,
        read_one,
        read_hidden,
        read_out,
        scratch=[pltpu.VMEM((9, channels, atoms), F32), pltpu.VMEM((3 * atoms, channels), F32)],
        aliases={3: 0},
    )
    az = partner(gz)
    rows = f32(2 * atoms, channels)

    def edges(start, count):
        out = f32(4 * count * GROUP, atoms)
        scaled = [pltpu.VMEM((9, channels, atoms), F32)]
        kernel = functools.partial(edge_kernel, start)
        return call(kernel, out, hg, rad, slo, dmat, unit, scratch=scaled)

    cuts = [0, 3 * (steps // 7), 4 * (steps // 7), steps]
    ga = edges(cuts[0], cuts[1] - cuts[0])
    acc, near, far = call(
        fold_z_kernel,
        [rows, b16(atoms, channels), b16(atoms, channels)],
        side,
        gy,
        az,
        fz,
    )
    dx = call(functools.partial(scatter_kernel, 0), rows, hot, rq)
    gb = edges(cuts[1], cuts[2] - cuts[1])
    near, far = swap_both(near, far, "gy")
    own, near, far = call(
        fold_y_kernel,
        [f32(atoms, channels), b16(half, channels), b16(half, channels)],
        side,
        acc,
        dx,
        extra,
        near,
        far,
        fy,
    )
    gc = edges(cuts[2], cuts[3] - cuts[2])
    near, far = swap_both(near, far, "gx")
    f0, f1, f2, f3, f4 = call(
        layer_one_reverse_kernel,
        [small] * 5,
        side,
        own,
        near,
        far,
        fx,
        amp,
        nbr,
        unit,
        rinv,
        basis,
        slope,
        ga,
        gb,
        gc,
        lanes,
        radial_one,
        mix_one,
        scratch=[pltpu.VMEM((6 * entries, atoms), F32), pltpu.VMEM((40, atoms), F32)],
    )
    az = partner(f4)
    acc, near, far = call(
        force_z_kernel, [f32(8, 2 * atoms), small, small], side, f0, f1, f2, f3, az, fz
    )
    near, far = swap_both(near, far, "gy")
    own, ghost = call(force_y_kernel, [small, small], side, acc, near, far, fy)
    near, far = swap_both(ghost, ghost, "gx")
    forces = call(force_x_kernel, f32(3, 1, atoms), side, own, near, far, fx)
    return (energies.reshape(occupancy.shape), forces.reshape(positions.shape))


def solution(mesh):
    return jax.shard_map(
        per_device,
        mesh=mesh,
        in_specs=(
            P(None, "gx", "gy", "gz", None),
            P("gx", "gy", "gz", None),
            P(None, "gx", "gy", "gz", None),
            P(None, "gx", "gy", "gz", None),
            P("gx", "gy", "gz", None, None),
            P("gx", "gy", "gz", None, None),
            P("gx", "gy", "gz", None),
            P(),
            P(),
            P(),
            P(),
            P(),
            P(),
            P(),
            P(),
        ),
        out_specs=(P("gx", "gy", "gz", None), P(None, "gx", "gy", "gz", None)),
        check_vma=False,
    )
```

time: 89.1 us -> 73.8 us (0.83)
  waiting for transfers between devices: 31 us -> 20.1 us
  starting transfers between devices: 28.3 us -> 22.8 us
  Pallas kernels: 24.6 us -> 28.4 us
  local copies, waits for them, and re-layouts: 4.35 us -> 1.42 us
    ppermute x16, waiting for transfers between devices: 22.1 us -> 15.9 us  [pair_swap(): return lax.ppermute(x, axis, pairs)]
    ppermute x4, waiting for transfers between devices: 8.85 us -> 4.29 us  [partner(): lax.ppermute(x, axis, [(i, i ^ 1) for i in range(lax.axis_size(axis))])]
    ppermute x16, starting transfers between devices: 22 us -> 17.4 us  [pair_swap(): return lax.ppermute(x, axis, pairs)]
    pallas_call x13 -> x21, Pallas kernels: 24.6 us -> 28.4 us  [call(): pl.pallas_call(kernel, out_shape=shapes, in_specs=specs, out_specs=[pl.Bl...]
    unnamed x33 -> x32, local copies, waits for them, and re-layouts: 4.35 us -> 1.42 us
    ppermute x4, starting transfers between devices: 6.3 us -> 5.35 us  [partner(): lax.ppermute(x, axis, [(i, i ^ 1) for i in range(lax.axis_size(axis))])]
  transfers between devices with their start and end apart: 20 -> 20, of which waited for: 15 -> 13; matrix products, arithmetic and copies ran while one was open for 0% -> 0% of each run, Pallas kernels for 0% -> 16%
where the time goes in v2:
time: 73.8 us; the launch traced here: 73.7 us
  Pallas kernels  28.4 us (38%)
  starting transfers between devices  22.8 us (31%)
  waiting for transfers between devices  20.1 us (27%)
  local copies, waits for them, and re-layouts  1.42 us (2%)
  between operations  0.87 us (1%)
    pallas_call x21, Pallas kernels, call(): pl.pallas_call(kernel, out_shape=shapes, in_specs=specs, out_specs=[pl.Bl...  28.4 us
    ppermute x16, starting transfers between devices, pair_swap(): return lax.ppermute(x, axis, pairs)  17.4 us
    ppermute x16, waiting for transfers between devices, pair_swap(): return lax.ppermute(x, axis, pairs)  15.9 us
    ppermute x4, starting transfers between devices, partner(): lax.ppermute(x, axis, [(i, i ^ 1) for i in range(lax.axis_size(axis))])  5.35 us
    ppermute x4, waiting for transfers between devices, partner(): lax.ppermute(x, axis, [(i, i ^ 1) for i in range(lax.axis_size(axis))])  4.29 us
  transfers between devices with their start and end apart: 20, of which 13 were waited for; matrix products, arithmetic and copies ran while one was open for 0% of the time, Pallas kernels for 16%

profile of v2, /device:TPU:0, one launch (start us, length us, event | category | flops | bytes accessed | tf_op | source)
XLA Modules:
  0.0 73.7 jit_solution(12422641412562408045)
XLA Ops:
  2.2 5.1 %collective-permute-start.1 = (f32[8,128]{1,0:T(8,128)S(1)}, f32[8,128]{1,0:T(8,128)S(1)}, u32[]{:S(2)}, u32[]{:S(2)}) collective-permute-start(f32[8,128]{1,0:T(8,128)S(1)} %get-tuple-element.55), channel_id=1, source_target_pairs={{0,24},{8,16},{16,8},{24,0},{1,25},{9,17},{17,9},{25,1},{2,26},{10... | collective-permute-start | bytes 12296 | tf_op jit(solution)/shard_map/ppermute | solution.py:724
  7.3 1.6 %collective-permute-done.1.far_ref = f32[8,128]{1,0:T(8,128)S(1)} collective-permute-done((f32[8,128]{1,0:T(8,128)S(1)}, f32[8,128]{1,0:T(8,128)S(1)}, u32[]{:S(2)}, u32[]{:S(2)}) %collective-permute-start.1) | collective-permute-done | bytes 4128 | tf_op jit(solution)/shard_map/ppermute | solution.py:724
  8.8 2.0 %collective-permute-done.near_ref = f32[8,128]{1,0:T(8,128)S(1)} collective-permute-done((f32[8,128]{1,0:T(8,128)S(1)}, f32[8,128]{1,0:T(8,128)S(1)}, u32[]{:S(2)}, u32[]{:S(2)}) %collective-permute-start) | collective-permute-done | bytes 4128 | tf_op jit(solution)/shard_map/ppermute | solution.py:724
  11.0 1.6 %collective-permute-start.3 = (f32[8,128]{1,0:T(8,128)S(1)}, f32[8,128]{1,0:T(8,128)S(1)}, u32[]{:S(2)}, u32[]{:S(2)}) collective-permute-start(f32[8,128]{1,0:T(8,128)S(1)} %get-tuple-element.58), channel_id=1, source_target_pairs={{0,6},{2,4},{4,2},{6,0},{1,7},{3,5},{5,3},{7,1},{8,14},{10,12},{12... | collective-permute-start | bytes 12296 | tf_op jit(solution)/shard_map/ppermute | solution.py:724
  12.6 1.4 %collective-permute-done.3.far_ref = f32[8,128]{1,0:T(8,128)S(1)} collective-permute-done((f32[8,128]{1,0:T(8,128)S(1)}, f32[8,128]{1,0:T(8,128)S(1)}, u32[]{:S(2)}, u32[]{:S(2)}) %collective-permute-start.3) | collective-permute-done | bytes 4128 | tf_op jit(solution)/shard_map/ppermute | solution.py:724
  14.2 1.5 %collective-permute-start.4 = (f32[8,128]{1,0:T(8,128)S(1)}, f32[8,128]{1,0:T(8,128)S(1)}, u32[]{:S(2)}, u32[]{:S(2)}) collective-permute-start(f32[8,128]{1,0:T(8,128)S(1)} %get-tuple-element.61), channel_id=1, source_target_pairs={{0,1},{1,0},{2,3},{3,2},{4,5},{5,4},{6,7},{7,6},{8,9},{9,8},{10,11... | collective-permute-start | bytes 12296 | tf_op jit(solution)/shard_map/ppermute | solution.py:729
  15.7 2.0 %shard_map.164 = (bf16[14,640,512]{2,1,0:T(8,128)(2,1)S(1)}, bf16[14,128,512]{2,1,0:T(8,128)(2,1)S(1)}) custom-call(s32[56,128]{1,0:T(8,128)S(1)} %bitcast.20), custom_call_target="tpu_custom_call" | custom-call | flops 1000000000 | bytes 1000000 | tf_op jit(solution)/shard_map/pallas_call | solution.py:702
  17.8 1.5 %shard_map.161 = (f32[168,128]{1,0:T(8,128)S(1)}, f32[56,128]{1,0:T(8,128)S(1)}, f32[448,128]{1,0:T(8,128)S(1)}, f32[448,128]{1,0:T(8,128)S(1)}, f32[128,1152]{1...) custom-call(s32[8,128]{1,0:T(8,128)S(1)} %get-tuple-element.53.side_ref, ...), custom_call_target="tpu_custom_call" | custom-call | flops 1000000000 | bytes 1000000 | tf_op jit(solution)/shard_map/pallas_call | solution.py:702
  19.4 1.8 %collective-permute-start.6 = (bf16[64,128]{1,0:T(8,128)(2,1)S(1)}, bf16[64,128]{1,0:T(8,128)(2,1)S(1)}, u32[]{:S(2)}, u32[]{:S(2)}) collective-permute-start(bf16[64,128]{1,0:T(8,128)(2,1)S(1)} %get-tuple-element.64), channel_id=1, source_target_pairs={{0,24},{8,16},{16,8},{24,0},{1,25},{9,17},{17,9},{25,1},{2,26},{10... | collective-permute-start | bytes 49160 | tf_op jit(solution)/shard_map/ppermute | solution.py:724
  21.3 1.2 %shard_map.167 = (f32[14,128,512]{2,1,0:T(8,128)S(1)}, f32[14,128,512]{2,1,0:T(8,128)S(1)}, f32[448,128]{1,0:T(8,128)S(1)}) custom-call(f32[448,128]{1,0:T(8,128)S(1)} %get-tuple-element.72.basis_ref, f32[448,128]{1,0:T(8,128)S(1)} %get-tuple-element.73.slope_ref, f32[168,128]{1,0:T(8,128)S(1)} %get-tuple-element.74.unit_ref, f32[8,128]{1,0:T(8,128)S(1)} %copy-done.8), custom_call_target="tpu_custom_call" | custom-call | flops 1000000000 | bytes 1000000 | tf_op jit(solution)/shard_map/pallas_call | solution.py:702
  23.1 1.9 %collective-permute-done.6.far_ref = bf16[64,128]{1,0:T(8,128)(2,1)S(1)} collective-permute-done((bf16[64,128]{1,0:T(8,128)(2,1)S(1)}, bf16[64,128]{1,0:T(8,128)(2,1)S(1)}, u32[]{:S(2)}, u32[]{:S(2)}) %collective-permute-start.6) | collective-permute-done | bytes 16416 | tf_op jit(solution)/shard_map/ppermute | solution.py:724
  25.3 1.6 %collective-permute-start.8 = (bf16[128,128]{1,0:T(8,128)(2,1)S(1)}, bf16[128,128]{1,0:T(8,128)(2,1)S(1)}, u32[]{:S(2)}, u32[]{:S(2)}) collective-permute-start(bf16[128,128]{1,0:T(8,128)(2,1)S(1)} %get-tuple-element.67), channel_id=1, source_target_pairs={{0,6},{2,4},{4,2},{6,0},{1,7},{3,5},{5,3},{7,1},{8,14},{10,12},{12... | collective-permute-start | bytes 98312 | tf_op jit(solution)/shard_map/ppermute | solution.py:724
  27.6 1.2 %collective-permute-done.8.far_ref = bf16[128,128]{1,0:T(8,128)(2,1)S(1)} collective-permute-done((bf16[128,128]{1,0:T(8,128)(2,1)S(1)}, bf16[128,128]{1,0:T(8,128)(2,1)S(1)}, u32[]{:S(2)}, u32[]{:S(2)}) %collective-permute-start.8) | collective-permute-done | bytes 32800 | tf_op jit(solution)/shard_map/ppermute | solution.py:724
  28.9 1.6 %collective-permute-start.9 = (bf16[128,128]{1,0:T(8,128)(2,1)S(1)}, bf16[128,128]{1,0:T(8,128)(2,1)S(1)}, u32[]{:S(2)}, u32[]{:S(2)}) collective-permute-start(bf16[128,128]{1,0:T(8,128)(2,1)S(1)} %get-tuple-element.68), channel_id=1, source_target_pairs={{0,1},{1,0},{2,3},{3,2},{4,5},{5,4},{6,7},{7,6},{8,9},{9,8},{10,11... | collective-permute-start | bytes 98312 | tf_op jit(solution)/shard_map/ppermute | solution.py:729
  30.5 1.1 %shard_map.166.old_ref = f32[14,128,512]{2,1,0:T(8,128)S(1)} custom-call(bf16[128,128]{1,0:T(8,128)(2,1)S(1)} %get-tuple-element.70.h2_ref, bf16[128,128]{1,0:T(8,128)(2,1)S(1)} %get-tuple-element.71.h3_ref, bf16[14,640,512]{2,1,0:T(8,128)(2,1)S(1)} %get-tuple-element.69.hot_ref, f32[14,128,512]{2,1,0:T(8,128)S(1)} %shard_map.165.old_ref), custom_call_target="tpu_custom_call", output_to_operand_aliasing={{}: (3, {})} | custom-call | flops 1000000000 | bytes 1000000 | tf_op jit(solution)/shard_map/pallas_call | solution.py:702
  31.6 1.2 %collective-permute-done.9.h4_ref = bf16[128,128]{1,0:T(8,128)(2,1)S(1)} collective-permute-done((bf16[128,128]{1,0:T(8,128)(2,1)S(1)}, bf16[128,128]{1,0:T(8,128)(2,1)S(1)}, u32[]{:S(2)}, u32[]{:S(2)}) %collective-permute-start.9) | collective-permute-done | bytes 32800 | tf_op jit(solution)/shard_map/ppermute | solution.py:729
  32.9 10.8 %shard_map.168 = (f32[14,128,512]{2,1,0:T(8,128)S(1)}, f32[1,128]{1,0:T(1,128)}, f32[9,128,128]{2,1,0:T(8,128)S(1)}, f32[128,128]{1,0:T(8,128)S(1)}, bf16[14,128...) custom-call(bf16[128,128]{1,0:T(8,128)(2,1)S(1)} %get-tuple-element., ...), custom_call_target="tpu_custom_call", output_to_operand_aliasing={{0}: (3, {})} | custom-call | flops 1000000000 | bytes 1000000 | tf_op jit(solution)/shard_map/pallas_call | solution.py:702
  43.7 1.5 %collective-permute-start.10 = (bf16[128,128]{1,0:T(8,128)(2,1)S(1)}, bf16[128,128]{1,0:T(8,128)(2,1)S(1)}, u32[]{:S(2)}, u32[]{:S(2)}) collective-permute-start(bf16[128,128]{1,0:T(8,128)(2,1)S(1)} %get-tuple-element.79), channel_id=1, source_target_pairs={{0,1},{1,0},{2,3},{3,2},{4,5},{5,4},{6,7},{7,6},{8,9},{9,8},{10,11... | collective-permute-start | bytes 98312 | tf_op jit(solution)/shard_map/ppermute | solution.py:729
  45.2 0.8 %shard_map.173.gb_ref = f32[32,128]{1,0:T(8,128)S(1)} custom-call(f32[14,128,512]{2,1,0:T(8,128)S(1)} %get-tuple-element.90.hg_ref, f32[14,128,512]{2,1,0:T(8,128)S(1)} %get-tuple-element.75.rad_ref, f32[14,128,512]{2,1,0:T(8,128)S(1)} %get-tuple-element.91.slo_ref, f32[9,128,128]{2,1,0:T(8,128)S(1)} %get-tuple-element.92.d_ref, ...), custom_call_target="tpu_custom_call" | custom-call | flops 1000000000 | bytes 1000000 | tf_op jit(solution)/shard_map/pallas_call | solution.py:702
  46.1 2.4 %shard_map.174.gc_ref = f32[96,128]{1,0:T(8,128)S(1)} custom-call(f32[14,128,512]{2,1,0:T(8,128)S(1)} %get-tuple-element.90.hg_ref, f32[14,128,512]{2,1,0:T(8,128)S(1)} %get-tuple-element.75.rad_ref, f32[14,128,512]{2,1,0:T(8,128)S(1)} %get-tuple-element.91.slo_ref, f32[9,128,128]{2,1,0:T(8,128)S(1)} %get-tuple-element.92.d_ref, ...), custom_call_target="tpu_custom_call" | custom-call | flops 1000000000 | bytes 1000000 | tf_op jit(solution)/shard_map/pallas_call | solution.py:702
  48.8 1.6 %collective-permute-start.12 = (bf16[128,128]{1,0:T(8,128)(2,1)S(1)}, bf16[128,128]{1,0:T(8,128)(2,1)S(1)}, u32[]{:S(2)}, u32[]{:S(2)}) collective-permute-start(bf16[128,128]{1,0:T(8,128)(2,1)S(1)} %get-tuple-element.84), channel_id=1, source_target_pairs={{0,6},{2,4},{4,2},{6,0},{1,7},{3,5},{5,3},{7,1},{8,14},{10,12},{12... | collective-permute-start | bytes 98312 | tf_op jit(solution)/shard_map/ppermute | solution.py:724
  50.4 1.1 %shard_map.170.gx_ref = f32[256,128]{1,0:T(8,128)S(1)} custom-call(bf16[14,640,512]{2,1,0:T(8,128)(2,1)S(1)} %get-tuple-element.69.hot_ref, bf16[14,128,512]{2,1,0:T(8,128)(2,1)S(1)} %get-tuple-element.81.rq_ref), custom_call_target="tpu_custom_call" | custom-call | flops 1000000000 | bytes 1000000 | tf_op jit(solution)/shard_map/pallas_call | solution.py:702
  52.6 1.8 %collective-permute-start.14 = (bf16[64,128]{1,0:T(8,128)(2,1)S(1)}, bf16[64,128]{1,0:T(8,128)(2,1)S(1)}, u32[]{:S(2)}, u32[]{:S(2)}) collective-permute-start(bf16[64,128]{1,0:T(8,128)(2,1)S(1)} %get-tuple-element.87), channel_id=1, source_target_pairs={{0,24},{8,16},{16,8},{24,0},{1,25},{9,17},{17,9},{25,1},{2,26},{10... | collective-permute-start | bytes 49160 | tf_op jit(solution)/shard_map/ppermute | solution.py:724
  54.4 2.4 %shard_map.172.ga_ref = f32[96,128]{1,0:T(8,128)S(1)} custom-call(f32[14,128,512]{2,1,0:T(8,128)S(1)} %get-tuple-element.90.hg_ref, f32[14,128,512]{2,1,0:T(8,128)S(1)} %get-tuple-element.75.rad_ref, f32[14,128,512]{2,1,0:T(8,128)S(1)} %get-tuple-element.91.slo_ref, f32[9,128,128]{2,1,0:T(8,128)S(1)} %get-tuple-element.92.d_ref, ...), custom_call_target="tpu_custom_call" | custom-call | flops 1000000000 | bytes 1000000 | tf_op jit(solution)/shard_map/pallas_call | solution.py:702
  56.8 1.3 %collective-permute-done.14.far_ref = bf16[64,128]{1,0:T(8,128)(2,1)S(1)} collective-permute-done((bf16[64,128]{1,0:T(8,128)(2,1)S(1)}, bf16[64,128]{1,0:T(8,128)(2,1)S(1)}, u32[]{:S(2)}, u32[]{:S(2)}) %collective-permute-start.14) | collective-permute-done | bytes 16416 | tf_op jit(solution)/shard_map/ppermute | solution.py:724
  58.1 1.8 %shard_map.175 = (f32[8,128]{1,0:T(8,128)S(1)}, f32[8,128]{1,0:T(8,128)S(1)}, f32[8,128]{1,0:T(8,128)S(1)}, f32[8,128]{1,0:T(8,128)S(1)}, f32[8,128]{1,0:T(8,128)S(1)}) custom-call(s32[8,128]{1,0:T(8,128)S(1)} %get-tuple-element.53.side_ref, f32[128,128]{1,0:T(8,128)S(1)} %get-tuple-element.85.own_ref, bf16[64,128]{1,0:T(8,128)(2,1)S(1)} %collective-permute-done.13.near_ref, ...), custom_call_target="tpu_custom_call" | custom-call | flops 1000000000 | bytes 1000000 | tf_op jit(solution)/shard_map/pallas_call | solution.py:702
  60.6 3.0 %collective-permute-done.15.az_ref = f32[8,128]{1,0:T(8,128)S(1)} collective-permute-done((f32[8,128]{1,0:T(8,128)S(1)}, f32[8,128]{1,0:T(8,128)S(1)}, u32[]{:S(2)}, u32[]{:S(2)}) %collective-permute-start.15) | collective-permute-done | bytes 4128 | tf_op jit(solution)/shard_map/ppermute | solution.py:729
  63.9 1.6 %collective-permute-start.17 = (f32[8,128]{1,0:T(8,128)S(1)}, f32[8,128]{1,0:T(8,128)S(1)}, u32[]{:S(2)}, u32[]{:S(2)}) collective-permute-start(f32[8,128]{1,0:T(8,128)S(1)} %get-tuple-element.101), channel_id=1, source_target_pairs={{0,6},{2,4},{4,2},{6,0},{1,7},{3,5},{5,3},{7,1},{8,14},{10,12},{12... | collective-permute-start | bytes 12296 | tf_op jit(solution)/shard_map/ppermute | solution.py:724
  65.5 1.5 %collective-permute-done.17.far_ref = f32[8,128]{1,0:T(8,128)S(1)} collective-permute-done((f32[8,128]{1,0:T(8,128)S(1)}, f32[8,128]{1,0:T(8,128)S(1)}, u32[]{:S(2)}, u32[]{:S(2)}) %collective-permute-start.17) | collective-permute-done | bytes 4128 | tf_op jit(solution)/shard_map/ppermute | solution.py:724
  67.3 1.8 %collective-permute-start.19 = (f32[8,128]{1,0:T(8,128)S(1)}, f32[8,128]{1,0:T(8,128)S(1)}, u32[]{:S(2)}, u32[]{:S(2)}) collective-permute-start(f32[8,128]{1,0:T(8,128)S(1)} %get-tuple-element.103), channel_id=1, source_target_pairs={{0,24},{8,16},{16,8},{24,0},{1,25},{9,17},{17,9},{25,1},{2,26},{10... | collective-permute-start | bytes 12296 | tf_op jit(solution)/shard_map/ppermute | solution.py:724
  69.2 3.6 %collective-permute-done.19.far_ref = f32[8,128]{1,0:T(8,128)S(1)} collective-permute-done((f32[8,128]{1,0:T(8,128)S(1)}, f32[8,128]{1,0:T(8,128)S(1)}, u32[]{:S(2)}, u32[]{:S(2)}) %collective-permute-start.19) | collective-permute-done | bytes 4128 | tf_op jit(solution)/shard_map/ppermute | solution.py:724
  72.8 0.9 %shard_map.178 = f32[3,1,128]{2,1,0:T(1,128)} custom-call(s32[8,128]{1,0:T(8,128)S(1)} %get-tuple-element.53.side_ref, f32[8,128]{1,0:T(8,128)S(1)} %get-tuple-element.102.own_ref, f32[8,128]{1,0:T(8,128)S(1)} %collective-permute-done.18.near_ref, f32[8,128]{1,0:T(8,128)S(1)} %collective-permute-done.19.far_ref, s32[2,64]{1,0:T(2,128)S(1)} %bitcast.31), custom_call_target="tpu_custom_call" | custom-call | flops 1000000000 | bytes 1000000 | tf_op jit(solution)/shard_map/pallas_call | solution.py:702
  (61 shorter events, 6.6 us)
Async XLA Ops:
  0.6 10.2 %copy-start.11 = (s32[1,1,1,2,128]{4,3,2,1,0:T(2,128)S(1)}, s32[1,1,1,2,128]{4,3,2,1,0:T(2,128)}, u32[]{:S(2)}) copy-start(s32[1,1,1,2,128]{4,3,2,1,0:T(2,128)} %param.20) | copy-start | bytes 3076
  2.0 12.1 %copy-start.15 = (s32[1,1,1,128]{3,2,1,0:T(1,128)S(1)}, s32[1,1,1,128]{3,2,1,0:T(1,128)}, u32[]{:S(2)}) copy-start(s32[1,1,1,128]{3,2,1,0:T(1,128)} %param.21) | copy-start | bytes 1540
  2.2 6.7 %collective-permute-start.1 = (f32[8,128]{1,0:T(8,128)S(1)}, f32[8,128]{1,0:T(8,128)S(1)}, u32[]{:S(2)}, u32[]{:S(2)}) collective-permute-start(f32[8,128]{1,0:T(8,128)S(1)} %get-tuple-element.55), channel_id=1, source_target_pairs={{0,24},{8,16},{16,8},{24,0},{1,25},{9,17},{17,9},{25,1},{2,26},{10... | collective-permute-start | bytes 12296 | tf_op jit(solution)/shard_map/ppermute | solution.py:724
  7.2 3.6 %collective-permute-start = (f32[8,128]{1,0:T(8,128)S(1)}, f32[8,128]{1,0:T(8,128)S(1)}, u32[]{:S(2)}, u32[]{:S(2)}) collective-permute-start(f32[8,128]{1,0:T(8,128)S(1)} %get-tuple-element.55), channel_id=1, source_target_pairs={{0,8},{8,0},{16,24},{24,16},{1,9},{9,1},{17,25},{25,17},{2,10},{10... | collective-permute-start | bytes 12296 | tf_op jit(solution)/shard_map/ppermute | solution.py:724
  10.9 4.8 %copy-start.7 = (s32[56,1,1,1,128]{4,3,2,1,0:T(1,128)S(1)}, s32[56,1,1,1,128]{4,3,2,1,0:T(1,128)}, u32[]{:S(2)}) copy-start(s32[56,1,1,1,128]{4,3,2,1,0:T(1,128)} %param.17) | copy-start | bytes 86020
  11.0 1.6 %collective-permute-start.2 = (f32[8,128]{1,0:T(8,128)S(1)}, f32[8,128]{1,0:T(8,128)S(1)}, u32[]{:S(2)}, u32[]{:S(2)}) collective-permute-start(f32[8,128]{1,0:T(8,128)S(1)} %get-tuple-element.57), channel_id=1, source_target_pairs={{0,2},{2,0},{4,6},{6,4},{1,3},{3,1},{5,7},{7,5},{8,10},{10,8},{12,... | collective-permute-start | bytes 12296 | tf_op jit(solution)/shard_map/ppermute | solution.py:724
  11.0 3.1 %collective-permute-start.3 = (f32[8,128]{1,0:T(8,128)S(1)}, f32[8,128]{1,0:T(8,128)S(1)}, u32[]{:S(2)}, u32[]{:S(2)}) collective-permute-start(f32[8,128]{1,0:T(8,128)S(1)} %get-tuple-element.58), channel_id=1, source_target_pairs={{0,6},{2,4},{4,2},{6,0},{1,7},{3,5},{5,3},{7,1},{8,14},{10,12},{12... | collective-permute-start | bytes 12296 | tf_op jit(solution)/shard_map/ppermute | solution.py:724
  14.1 3.7 %copy-start.5 = (bf16[384,128]{1,0:T(8,128)(2,1)S(1)}, bf16[384,128]{1,0:T(8,128)(2,1)}, u32[]{:S(2)}) copy-start(bf16[384,128]{1,0:T(8,128)(2,1)} %mix_ref.5) | copy-start | bytes 294916
  14.1 3.7 %copy-start.6 = (s32[56,1,1,1,128]{4,3,2,1,0:T(1,128)S(1)}, s32[56,1,1,1,128]{4,3,2,1,0:T(1,128)}, u32[]{:S(2)}) copy-start(s32[56,1,1,1,128]{4,3,2,1,0:T(1,128)} %param.18) | copy-start | bytes 86020
  14.1 3.7 %copy-start.9 = (f32[8,128]{1,0:T(8,128)S(1)}, f32[8,128]{1,0:T(8,128)}, u32[]{:S(2)}) copy-start(f32[8,128]{1,0:T(8,128)} %radial_ref.5) | copy-start | bytes 12292
  14.1 3.7 %copy-start.13 = (s32[1,1,1,2,64]{4,3,2,1,0:T(2,128)S(1)}, s32[1,1,1,2,64]{4,3,2,1,0:T(2,128)}, u32[]{:S(2)}) copy-start(s32[1,1,1,2,64]{4,3,2,1,0:T(2,128)} %param.19) | copy-start | bytes 1540
  14.1 3.7 %copy-start.14 = (f32[128]{0:T(128)S(1)}, f32[128]{0:T(128)}, u32[]{:S(2)}) copy-start(f32[128]{0:T(128)} %param.24) | copy-start | bytes 1540
  14.2 3.6 %collective-permute-start.4 = (f32[8,128]{1,0:T(8,128)S(1)}, f32[8,128]{1,0:T(8,128)S(1)}, u32[]{:S(2)}, u32[]{:S(2)}) collective-permute-start(f32[8,128]{1,0:T(8,128)S(1)} %get-tuple-element.61), channel_id=1, source_target_pairs={{0,1},{1,0},{2,3},{3,2},{4,5},{5,4},{6,7},{7,6},{8,9},{9,8},{10,11... | collective-permute-start | bytes 12296 | tf_op jit(solution)/shard_map/ppermute | solution.py:729
  15.7 5.6 %copy-start.8 = (f32[8,128]{1,0:T(8,128)S(1)}, f32[8,128]{1,0:T(8,128)}, u32[]{:S(2)}) copy-start(f32[8,128]{1,0:T(8,128)} %radial_ref.4) | copy-start | bytes 12292
  19.3 3.8 %collective-permute-start.5 = (bf16[64,128]{1,0:T(8,128)(2,1)S(1)}, bf16[64,128]{1,0:T(8,128)(2,1)S(1)}, u32[]{:S(2)}, u32[]{:S(2)}) collective-permute-start(bf16[64,128]{1,0:T(8,128)(2,1)S(1)} %get-tuple-element.63), channel_id=1, source_target_pairs={{0,8},{8,0},{16,24},{24,16},{1,9},{9,1},{17,25},{25,17},{2,10},{10... | collective-permute-start | bytes 49160 | tf_op jit(solution)/shard_map/ppermute | solution.py:724
  19.4 5.6 %collective-permute-start.6 = (bf16[64,128]{1,0:T(8,128)(2,1)S(1)}, bf16[64,128]{1,0:T(8,128)(2,1)S(1)}, u32[]{:S(2)}, u32[]{:S(2)}) collective-permute-start(bf16[64,128]{1,0:T(8,128)(2,1)S(1)} %get-tuple-element.64), channel_id=1, source_target_pairs={{0,24},{8,16},{16,8},{24,0},{1,25},{9,17},{17,9},{25,1},{2,26},{10... | collective-permute-start | bytes 49160 | tf_op jit(solution)/shard_map/ppermute | solution.py:724
  25.2 2.3 %collective-permute-start.7 = (bf16[128,128]{1,0:T(8,128)(2,1)S(1)}, bf16[128,128]{1,0:T(8,128)(2,1)S(1)}, u32[]{:S(2)}, u32[]{:S(2)}) collective-permute-start(bf16[128,128]{1,0:T(8,128)(2,1)S(1)} %get-tuple-element.66), channel_id=1, source_target_pairs={{0,2},{2,0},{4,6},{6,4},{1,3},{3,1},{5,7},{7,5},{8,10},{10,8},{12,... | collective-permute-start | bytes 98312 | tf_op jit(solution)/shard_map/ppermute | solution.py:724
  25.3 3.4 %collective-permute-start.8 = (bf16[128,128]{1,0:T(8,128)(2,1)S(1)}, bf16[128,128]{1,0:T(8,128)(2,1)S(1)}, u32[]{:S(2)}, u32[]{:S(2)}) collective-permute-start(bf16[128,128]{1,0:T(8,128)(2,1)S(1)} %get-tuple-element.67), channel_id=1, source_target_pairs={{0,6},{2,4},{4,2},{6,0},{1,7},{3,5},{5,3},{7,1},{8,14},{10,12},{12... | collective-permute-start | bytes 98312 | tf_op jit(solution)/shard_map/ppermute | solution.py:724
  28.9 4.0 %collective-permute-start.9 = (bf16[128,128]{1,0:T(8,128)(2,1)S(1)}, bf16[128,128]{1,0:T(8,128)(2,1)S(1)}, u32[]{:S(2)}, u32[]{:S(2)}) collective-permute-start(bf16[128,128]{1,0:T(8,128)(2,1)S(1)} %get-tuple-element.68), channel_id=1, source_target_pairs={{0,1},{1,0},{2,3},{3,2},{4,5},{5,4},{6,7},{7,6},{8,9},{9,8},{10,11... | collective-permute-start | bytes 98312 | tf_op jit(solution)/shard_map/ppermute | solution.py:729
  30.5 2.4 %copy-start.2 = (s32[1,1,1,128]{3,2,1,0:T(1,128)S(1)}, s32[1,1,1,128]{3,2,1,0:T(1,128)}, u32[]{:S(2)}) copy-start(s32[1,1,1,128]{3,2,1,0:T(1,128)} %param.16) | copy-start | bytes 1540
  30.5 2.4 %copy-start.3 = (f32[128]{0:T(128)S(1)}, f32[128]{0:T(128)}, u32[]{:S(2)}) copy-start(f32[128]{0:T(128)} %param.27) | copy-start | bytes 1540
  30.5 2.4 %copy-start.4 = (f32[16]{0:T(128)S(1)}, f32[16]{0:T(128)}, u32[]{:S(2)}) copy-start(f32[16]{0:T(128)} %param.29) | copy-start | bytes 196
  43.7 4.8 %collective-permute-start.10 = (bf16[128,128]{1,0:T(8,128)(2,1)S(1)}, bf16[128,128]{1,0:T(8,128)(2,1)S(1)}, u32[]{:S(2)}, u32[]{:S(2)}) collective-permute-start(bf16[128,128]{1,0:T(8,128)(2,1)S(1)} %get-tuple-element.79), channel_id=1, source_target_pairs={{0,1},{1,0},{2,3},{3,2},{4,5},{5,4},{6,7},{7,6},{8,9},{9,8},{10,11... | collective-permute-start | bytes 98312 | tf_op jit(solution)/shard_map/ppermute | solution.py:729
  48.7 2.8 %collective-permute-start.11 = (bf16[128,128]{1,0:T(8,128)(2,1)S(1)}, bf16[128,128]{1,0:T(8,128)(2,1)S(1)}, u32[]{:S(2)}, u32[]{:S(2)}) collective-permute-start(bf16[128,128]{1,0:T(8,128)(2,1)S(1)} %get-tuple-element.83), channel_id=1, source_target_pairs={{0,2},{2,0},{4,6},{6,4},{1,3},{3,1},{5,7},{7,5},{8,10},{10,8},{12,... | collective-permute-start | bytes 98312 | tf_op jit(solution)/shard_map/ppermute | solution.py:724
  48.8 3.4 %collective-permute-start.12 = (bf16[128,128]{1,0:T(8,128)(2,1)S(1)}, bf16[128,128]{1,0:T(8,128)(2,1)S(1)}, u32[]{:S(2)}, u32[]{:S(2)}) collective-permute-start(bf16[128,128]{1,0:T(8,128)(2,1)S(1)} %get-tuple-element.84), channel_id=1, source_target_pairs={{0,6},{2,4},{4,2},{6,0},{1,7},{3,5},{5,3},{7,1},{8,14},{10,12},{12... | collective-permute-start | bytes 98312 | tf_op jit(solution)/shard_map/ppermute | solution.py:724
  52.4 4.4 %collective-permute-start.13 = (bf16[64,128]{1,0:T(8,128)(2,1)S(1)}, bf16[64,128]{1,0:T(8,128)(2,1)S(1)}, u32[]{:S(2)}, u32[]{:S(2)}) collective-permute-start(bf16[64,128]{1,0:T(8,128)(2,1)S(1)} %get-tuple-element.86), channel_id=1, source_target_pairs={{0,8},{8,0},{16,24},{24,16},{1,9},{9,1},{17,25},{25,17},{2,10},{10... | collective-permute-start | bytes 49160 | tf_op jit(solution)/shard_map/ppermute | solution.py:724
  52.6 5.5 %collective-permute-start.14 = (bf16[64,128]{1,0:T(8,128)(2,1)S(1)}, bf16[64,128]{1,0:T(8,128)(2,1)S(1)}, u32[]{:S(2)}, u32[]{:S(2)}) collective-permute-start(bf16[64,128]{1,0:T(8,128)(2,1)S(1)} %get-tuple-element.87), channel_id=1, source_target_pairs={{0,24},{8,16},{16,8},{24,0},{1,25},{9,17},{17,9},{25,1},{2,26},{10... | collective-permute-start | bytes 49160 | tf_op jit(solution)/shard_map/ppermute | solution.py:724
  59.9 3.7 %collective-permute-start.15 = (f32[8,128]{1,0:T(8,128)S(1)}, f32[8,128]{1,0:T(8,128)S(1)}, u32[]{:S(2)}, u32[]{:S(2)}) collective-permute-start(f32[8,128]{1,0:T(8,128)S(1)} %get-tuple-element.98), channel_id=1, source_target_pairs={{0,1},{1,0},{2,3},{3,2},{4,5},{5,4},{6,7},{7,6},{8,9},{9,8},{10,11... | collective-permute-start | bytes 12296 | tf_op jit(solution)/shard_map/ppermute | solution.py:729
  63.9 1.6 %collective-permute-start.16 = (f32[8,128]{1,0:T(8,128)S(1)}, f32[8,128]{1,0:T(8,128)S(1)}, u32[]{:S(2)}, u32[]{:S(2)}) collective-permute-start(f32[8,128]{1,0:T(8,128)S(1)} %get-tuple-element.100), channel_id=1, source_target_pairs={{0,2},{2,0},{4,6},{6,4},{1,3},{3,1},{5,7},{7,5},{8,10},{10,8},{12,... | collective-permute-start | bytes 12296 | tf_op jit(solution)/shard_map/ppermute | solution.py:724
  63.9 3.1 %collective-permute-start.17 = (f32[8,128]{1,0:T(8,128)S(1)}, f32[8,128]{1,0:T(8,128)S(1)}, u32[]{:S(2)}, u32[]{:S(2)}) collective-permute-start(f32[8,128]{1,0:T(8,128)S(1)} %get-tuple-element.101), channel_id=1, source_target_pairs={{0,6},{2,4},{4,2},{6,0},{1,7},{3,5},{5,3},{7,1},{8,14},{10,12},{12... | collective-permute-start | bytes 12296 | tf_op jit(solution)/shard_map/ppermute | solution.py:724
  67.3 5.4 %collective-permute-start.19 = (f32[8,128]{1,0:T(8,128)S(1)}, f32[8,128]{1,0:T(8,128)S(1)}, u32[]{:S(2)}, u32[]{:S(2)}) collective-permute-start(f32[8,128]{1,0:T(8,128)S(1)} %get-tuple-element.103), channel_id=1, source_target_pairs={{0,24},{8,16},{16,8},{24,0},{1,25},{9,17},{17,9},{25,1},{2,26},{10... | collective-permute-start | bytes 12296 | tf_op jit(solution)/shard_map/ppermute | solution.py:724
  69.2 3.6 %collective-permute-start.18 = (f32[8,128]{1,0:T(8,128)S(1)}, f32[8,128]{1,0:T(8,128)S(1)}, u32[]{:S(2)}, u32[]{:S(2)}) collective-permute-start(f32[8,128]{1,0:T(8,128)S(1)} %get-tuple-element.103), channel_id=1, source_target_pairs={{0,8},{8,0},{16,24},{24,16},{1,9},{9,1},{17,25},{25,17},{2,10},{10... | collective-permute-start | bytes 12296 | tf_op jit(solution)/shard_map/ppermute | solution.py:724
  (4 other events, 6.2 us)

commit v3 on v2

--- a/solution.py
+++ b/solution.py
@@ -16,7 +16,6 @@
 SPACING = 1.8
 CUTOFF = 5.0
 SPREAD = 0.4
-HIGHEST = lax.Precision.HIGHEST
 F32 = jnp.float32
 BF16 = jnp.bfloat16
 
@@ -32,15 +31,28 @@
     )
 
 
-def split2(x):
-    hi = x.astype(BF16)
-    lo = (x - hi.astype(F32)).astype(BF16)
-    return hi, lo
-
-
-def dot_split(a, b, ca=1, cb=0):
-    hi, lo = split2(b)
-    return dot(a, hi, ca, cb) + dot(a, lo, ca, cb)
+def rounded(x):
+    return x.astype(BF16).astype(F32)
+
+
+def dot3(a, b, ca=1, cb=0):
+    a_hi, b_hi = rounded(a), rounded(b)
+    left = jnp.concatenate([a_hi, a_hi, a - a_hi], axis=ca).astype(BF16)
+    right = jnp.concatenate([b_hi, b - b_hi, b_hi], axis=cb).astype(BF16)
+    return dot(left, right, ca, cb)
+
+
+def dot_split(a, b):
+    hi = rounded(b)
+    right = jnp.concatenate([hi, b - hi], axis=0).astype(BF16)
+    return dot(jnp.concatenate([a, a], axis=1), right)
+
+
+def columns(row, count):
+    hi = rounded(row)
+    mid = rounded(row - hi)
+    parts = jnp.concatenate([hi, mid, row - hi - mid], axis=0).astype(BF16)
+    return dot(parts, jnp.ones((3, count), BF16), 0, 0)
 
 
 def onehot(row, size):
@@ -201,11 +213,11 @@
         for k in range(NB):
             prod = basis[k] if m == 0 else basis[k] * angular[m]
             mom_ref[k : k + 1, m * atoms : (m + 1) * atoms] = jnp.sum(prod, axis=0, keepdims=True)
-    amp = SPREAD * dot(radial_ref[...], mom_ref[...], 0, 0, HIGHEST)
+    amp = SPREAD * dot3(radial_ref[...], mom_ref[...], 0, 0)
     amp_ref[...] = amp
     inv = invariants([amp[:, m * atoms : (m + 1) * atoms] for m in range(9)])
     h1 = dot(mix_ref[...], inv, 0, 0)
-    h1 = h1 + dot(embed_ref[...], jnp.ones((1, atoms), F32), 0, 0, HIGHEST)
+    h1 = h1 + columns(embed_ref[...], atoms)
     h1b = h1.astype(BF16)
     h0_ref[...] = h1b
     both = dot(h1b, onehot(face_row(side_ref, fx_ref), atoms))
@@ -358,7 +370,6 @@
     raw_ref,
     extra_ref,
     rq_ref,
-    gy_ref,
     gz_ref,
     acc_ref,
     dh_ref,
@@ -397,29 +408,32 @@
                     acc_ref[m, rows, :] += terms[0]
 
     prepare(0)
-
-    def forward_body(step, carry):
-        accumulate(step - 1)
-        prepare(step)
+    prepare(1)
+
+    def forward_body(trip, carry):
+        for part in range(2):
+            accumulate(2 * trip + part)
+        for part in range(2):
+            prepare(2 * trip + 2 + part)
         return carry
 
-    lax.fori_loop(1, steps, forward_body, 0)
-    accumulate(steps - 1)
+    lax.fori_loop(0, steps // 2 - 1, forward_body, 0)
+    for part in range(2):
+        accumulate(steps - 2 + part)
 
     occ = occ_ref[...].astype(F32)
-    ones = jnp.ones((1, atoms), F32)
     amp = [SPREAD * acc_ref[m] for m in range(9)]
     own = h0_ref[...].astype(F32)
     h2 = dot(mix_ref[...], invariants(amp), 0, 0) + own
-    pre = dot(rhid_ref[...], h2, 1, 0, HIGHEST)
+    pre = dot3(rhid_ref[...], h2, 1, 0)
     sig = 1.0 / (1.0 + jnp.exp(-pre))
-    rout = dot(rout_ref[...], ones, 0, 0, HIGHEST)
-    rone = dot(rone_ref[...], ones, 0, 0, HIGHEST)
+    rout = columns(rout_ref[...], atoms)
+    rone = columns(rone_ref[...], atoms)
     energy = jnp.sum(own * rone, axis=0, keepdims=True)
     energy = energy + jnp.sum(rout * pre * sig, axis=0, keepdims=True)
     en_ref[...] = occ * energy
     dpre = occ * rout * sig * (1.0 + pre * (1.0 - sig))
-    dh2 = dot(rhid_ref[...], dpre, 0, 0, HIGHEST)
+    dh2 = dot3(rhid_ref[...], dpre, 0, 0)
     dinv = dot_split(mix_ref[...], dh2)
     low = dinv[channels : 2 * channels]
     top = dinv[2 * channels :]
@@ -449,19 +463,20 @@
                 rq_ref[step, pair * 16 : pair * 16 + 16, cols] = value
 
     def send(step):
-        dh_ref[...] += dot(hot_ref[step, 2 * atoms :, :], rq_ref[step], 1, 1)
+        low = dot(hot_ref[step, 4 * atoms :, :], rq_ref[step], 1, 1)
+        return low + dot(hot_ref[step + 1, 4 * atoms :, :], rq_ref[step + 1], 1, 1)
 
     reverse(0)
-
-    def reverse_body(step, carry):
-        send(step - 1)
-        reverse(step)
+    reverse(1)
+
+    def reverse_body(trip, carry):
+        dh_ref[...] += send(2 * trip)
+        for part in range(2):
+            reverse(2 * trip + 2 + part)
         return carry
 
-    lax.fori_loop(1, steps, reverse_body, 0)
-    send(steps - 1)
-    gy_ref[...] = dh_ref[0 : 2 * atoms, :].astype(BF16)
-    gz_ref[...] = dh_ref[2 * atoms :, :].astype(BF16)
+    lax.fori_loop(0, steps // 2 - 1, reverse_body, 0)
+    gz_ref[...] = (dh_ref[...] + send(steps - 2)).astype(BF16)
 
 
 def directions(d, unit):
@@ -532,7 +547,7 @@
     quarter = size // 2
     add = dot(onehot(fz_ref[...], 2 * size), az_ref[...])
     acc_ref[...] = add[0:size]
-    rows = gy_ref[...].astype(F32) + add[size:]
+    rows = rounded(gy_ref[...]) + add[size:]
     low, high = rows[0:quarter], rows[quarter:]
     to_near_ref[...] = by_side(side_ref, 1, low, high).astype(BF16)
     to_far_ref[...] = by_side(side_ref, 1, high, low).astype(BF16)
@@ -595,7 +610,7 @@
     for m in range(1, 9):
         amp = amp_ref[:, m * atoms : (m + 1) * atoms]
         pieces.append(2.0 * amp * (low if m < 4 else top))
-    dmom = SPREAD * dot(radial_ref[...], jnp.concatenate(pieces, axis=1), 1, 0, HIGHEST)
+    dmom = SPREAD * dot3(radial_ref[...], jnp.concatenate(pieces, axis=1), 1, 0)
     ux = unit_ref[0:entries, :]
     uy = unit_ref[entries : 2 * entries, :]
     uz = unit_ref[2 * entries : 3 * entries, :]
@@ -658,7 +673,12 @@
 
 
 def scatter_lanes(values, row, size):
-    return dot(values, onehot(row, size).astype(F32), 1, 1, HIGHEST)
+    hi = rounded(values)
+    mid = rounded(values - hi)
+    parts = jnp.concatenate([hi, mid, values - hi - mid], axis=0).astype(BF16)
+    out = dot(parts, onehot(row, size), 1, 1)
+    rows = values.shape[0]
+    return out[0:rows] + out[rows : 2 * rows] + out[2 * rows :]
 
 
 def force_z_kernel(
@@ -685,7 +705,8 @@
     ghost_ref[...] = by_side(side_ref, 0, ghost, half_turn(ghost))
 
 
-def force_x_kernel(side_ref, own_ref, near_ref, far_ref, fx_ref, out_ref):
+def force_x_kernel(side_ref, own_ref, near_ref, far_ref, fx_ref, en_ref, out_ref, total_ref):
+    total_ref[...] = en_ref[...]
     size = own_ref.shape[1]
     both = jnp.where(low_lanes(own_ref.shape), near_ref[...], far_ref[...])
     rows = own_ref[...] + scatter_lanes(both, face_row(side_ref, fx_ref), size)
@@ -834,7 +855,7 @@
     hg = call(gather_more_kernel, big, h2, h3, hot, hg, scratch=table, aliases={3: 0})
     h4 = partner(sent)
 
-    hg, energies, dmat, extra, rq, gy, gz = call(
+    hg, energies, dmat, extra, rq, gz = call(
         layer_two_kernel,
         [
             big,
@@ -842,7 +863,6 @@
             f32(9, channels, atoms),
             f32(channels, atoms),
             b16(steps, channels, width),
-            b16(2 * atoms, channels),
             b16(atoms, channels),
         ],
         h0,
@@ -856,7 +876,7 @@
         read_one,
         read_hidden,
         read_out,
-        scratch=[pltpu.VMEM((9, channels, atoms), F32), pltpu.VMEM((3 * atoms, channels), F32)],
+        scratch=[pltpu.VMEM((9, channels, atoms), F32), pltpu.VMEM((atoms, channels), F32)],
         aliases={3: 0},
     )
     az = partner(gz)
@@ -868,7 +888,8 @@
         kernel = functools.partial(edge_kernel, start)
         return call(kernel, out, hg, rad, slo, dmat, unit, scratch=scaled)
 
-    cuts = [0, 3 * (steps // 7), 4 * (steps // 7), steps]
+    cuts = [0, 2 * (steps // 7), 3 * (steps // 7), steps]
+    gy = call(functools.partial(scatter_kernel, 2 * atoms), rows, hot, rq)
     ga = edges(cuts[0], cuts[1] - cuts[0])
     acc, near, far = call(
         fold_z_kernel,
@@ -923,7 +944,9 @@
     near, far = swap_both(near, far, "gy")
     own, ghost = call(force_y_kernel, [small, small], side, acc, near, far, fy)
     near, far = swap_both(ghost, ghost, "gx")
-    forces = call(force_x_kernel, f32(3, 1, atoms), side, own, near, far, fx)
+    forces, energies = call(
+        force_x_kernel, [f32(3, 1, atoms), f32(1, atoms)], side, own, near, far, fx, energies
+    )
     return (energies.reshape(occupancy.shape), forces.reshape(positions.shape))
 
 

time: 73.8 us -> 71.1 us (0.963)
  Pallas kernels: 28.4 us -> 25.1 us
  starting transfers between devices: 22.8 us -> 23.7 us
    pallas_call x21 -> x22, Pallas kernels: 28.4 us -> 25.1 us  [call(): pl.pallas_call(kernel, out_shape=shapes, in_specs=specs, out_specs=[pl.Bl...]
    ppermute x4, starting transfers between devices: 5.35 us -> 6.28 us  [partner(): lax.ppermute(x, axis, [(i, i ^ 1) for i in range(lax.axis_size(axis))])]
    ppermute x16, waiting for transfers between devices: 15.9 us -> 15.1 us  [pair_swap(): return lax.ppermute(x, axis, pairs)]
  transfers between devices with their start and end apart: 20 -> 20, of which waited for: 13 -> 14; matrix products, arithmetic and copies ran while one was open for 0% -> 0% of each run, Pallas kernels for 16% -> 15%
where the time goes in v3:
time: 71.1 us; the launch traced here: 71 us
  Pallas kernels  25.1 us (35%)
  starting transfers between devices  23.7 us (33%)
  waiting for transfers between devices  19.8 us (28%)
  local copies, waits for them, and re-layouts  1.42 us (2%)
  between operations  0.88 us (1%)
    pallas_call x22, Pallas kernels, call(): pl.pallas_call(kernel, out_shape=shapes, in_specs=specs, out_specs=[pl.Bl...  25.1 us
    ppermute x16, starting transfers between devices, pair_swap(): return lax.ppermute(x, axis, pairs)  17.4 us
    ppermute x16, waiting for transfers between devices, pair_swap(): return lax.ppermute(x, axis, pairs)  15.1 us
    ppermute x4, starting transfers between devices, partner(): lax.ppermute(x, axis, [(i, i ^ 1) for i in range(lax.axis_size(axis))])  6.28 us
    ppermute x4, waiting for transfers between devices, partner(): lax.ppermute(x, axis, [(i, i ^ 1) for i in range(lax.axis_size(axis))])  4.7 us
  transfers between devices with their start and end apart: 20, of which 14 were waited for; matrix products, arithmetic and copies ran while one was open for 0% of the time, Pallas kernels for 15%

profile of v3, /device:TPU:0, one launch (start us, length us, event | category | flops | bytes accessed | tf_op | source)
XLA Modules:
  0.0 71.0 jit_solution(15654308106809000875)
XLA Ops:
  2.2 5.1 %collective-permute-start.1 = (f32[8,128]{1,0:T(8,128)S(1)}, f32[8,128]{1,0:T(8,128)S(1)}, u32[]{:S(2)}, u32[]{:S(2)}) collective-permute-start(f32[8,128]{1,0:T(8,128)S(1)} %get-tuple-element.57), channel_id=1, source_target_pairs={{0,24},{8,16},{16,8},{24,0},{1,25},{9,17},{17,9},{25,1},{2,26},{10... | collective-permute-start | bytes 12296 | tf_op jit(solution)/shard_map/ppermute | solution.py:745
  7.3 1.6 %collective-permute-done.1.far_ref = f32[8,128]{1,0:T(8,128)S(1)} collective-permute-done((f32[8,128]{1,0:T(8,128)S(1)}, f32[8,128]{1,0:T(8,128)S(1)}, u32[]{:S(2)}, u32[]{:S(2)}) %collective-permute-start.1) | collective-permute-done | bytes 4128 | tf_op jit(solution)/shard_map/ppermute | solution.py:745
  8.8 2.0 %collective-permute-done.near_ref = f32[8,128]{1,0:T(8,128)S(1)} collective-permute-done((f32[8,128]{1,0:T(8,128)S(1)}, f32[8,128]{1,0:T(8,128)S(1)}, u32[]{:S(2)}, u32[]{:S(2)}) %collective-permute-start) | collective-permute-done | bytes 4128 | tf_op jit(solution)/shard_map/ppermute | solution.py:745
  11.0 1.6 %collective-permute-start.3 = (f32[8,128]{1,0:T(8,128)S(1)}, f32[8,128]{1,0:T(8,128)S(1)}, u32[]{:S(2)}, u32[]{:S(2)}) collective-permute-start(f32[8,128]{1,0:T(8,128)S(1)} %get-tuple-element.60), channel_id=1, source_target_pairs={{0,6},{2,4},{4,2},{6,0},{1,7},{3,5},{5,3},{7,1},{8,14},{10,12},{12... | collective-permute-start | bytes 12296 | tf_op jit(solution)/shard_map/ppermute | solution.py:745
  12.6 1.4 %collective-permute-done.3.far_ref = f32[8,128]{1,0:T(8,128)S(1)} collective-permute-done((f32[8,128]{1,0:T(8,128)S(1)}, f32[8,128]{1,0:T(8,128)S(1)}, u32[]{:S(2)}, u32[]{:S(2)}) %collective-permute-start.3) | collective-permute-done | bytes 4128 | tf_op jit(solution)/shard_map/ppermute | solution.py:745
  14.2 1.5 %collective-permute-start.4 = (f32[8,128]{1,0:T(8,128)S(1)}, f32[8,128]{1,0:T(8,128)S(1)}, u32[]{:S(2)}, u32[]{:S(2)}) collective-permute-start(f32[8,128]{1,0:T(8,128)S(1)} %get-tuple-element.63), channel_id=1, source_target_pairs={{0,1},{1,0},{2,3},{3,2},{4,5},{5,4},{6,7},{7,6},{8,9},{9,8},{10,11... | collective-permute-start | bytes 12296 | tf_op jit(solution)/shard_map/ppermute | solution.py:750
  15.7 2.0 %shard_map.159 = (bf16[14,640,512]{2,1,0:T(8,128)(2,1)S(1)}, bf16[14,128,512]{2,1,0:T(8,128)(2,1)S(1)}) custom-call(s32[56,128]{1,0:T(8,128)S(1)} %bitcast.20), custom_call_target="tpu_custom_call" | custom-call | flops 1000000000 | bytes 1000000 | tf_op jit(solution)/shard_map/pallas_call | solution.py:723
  17.8 1.1 %shard_map.162 = (f32[168,128]{1,0:T(8,128)S(1)}, f32[56,128]{1,0:T(8,128)S(1)}, f32[448,128]{1,0:T(8,128)S(1)}, f32[448,128]{1,0:T(8,128)S(1)}, f32[128,1152]{1...) custom-call(s32[8,128]{1,0:T(8,128)S(1)} %get-tuple-element.54.side_ref, ...), custom_call_target="tpu_custom_call" | custom-call | flops 1000000000 | bytes 1000000 | tf_op jit(solution)/shard_map/pallas_call | solution.py:723
  19.1 1.8 %collective-permute-start.6 = (bf16[64,128]{1,0:T(8,128)(2,1)S(1)}, bf16[64,128]{1,0:T(8,128)(2,1)S(1)}, u32[]{:S(2)}, u32[]{:S(2)}) collective-permute-start(bf16[64,128]{1,0:T(8,128)(2,1)S(1)} %get-tuple-element.66), channel_id=1, source_target_pairs={{0,24},{8,16},{16,8},{24,0},{1,25},{9,17},{17,9},{25,1},{2,26},{10... | collective-permute-start | bytes 49160 | tf_op jit(solution)/shard_map/ppermute | solution.py:745
  20.9 1.2 %shard_map.167 = (f32[14,128,512]{2,1,0:T(8,128)S(1)}, f32[14,128,512]{2,1,0:T(8,128)S(1)}, f32[448,128]{1,0:T(8,128)S(1)}) custom-call(f32[448,128]{1,0:T(8,128)S(1)} %get-tuple-element.73.basis_ref, f32[448,128]{1,0:T(8,128)S(1)} %get-tuple-element.74.slope_ref, f32[168,128]{1,0:T(8,128)S(1)} %get-tuple-element.75.unit_ref, f32[8,128]{1,0:T(8,128)S(1)} %copy-done.8), custom_call_target="tpu_custom_call" | custom-call | flops 1000000000 | bytes 1000000 | tf_op jit(solution)/shard_map/pallas_call | solution.py:723
  22.8 1.9 %collective-permute-done.6.far_ref = bf16[64,128]{1,0:T(8,128)(2,1)S(1)} collective-permute-done((bf16[64,128]{1,0:T(8,128)(2,1)S(1)}, bf16[64,128]{1,0:T(8,128)(2,1)S(1)}, u32[]{:S(2)}, u32[]{:S(2)}) %collective-permute-start.6) | collective-permute-done | bytes 16416 | tf_op jit(solution)/shard_map/ppermute | solution.py:745
  25.0 1.6 %collective-permute-start.8 = (bf16[128,128]{1,0:T(8,128)(2,1)S(1)}, bf16[128,128]{1,0:T(8,128)(2,1)S(1)}, u32[]{:S(2)}, u32[]{:S(2)}) collective-permute-start(bf16[128,128]{1,0:T(8,128)(2,1)S(1)} %get-tuple-element.69), channel_id=1, source_target_pairs={{0,6},{2,4},{4,2},{6,0},{1,7},{3,5},{5,3},{7,1},{8,14},{10,12},{12... | collective-permute-start | bytes 98312 | tf_op jit(solution)/shard_map/ppermute | solution.py:745
  27.2 1.1 %collective-permute-done.8.far_ref = bf16[128,128]{1,0:T(8,128)(2,1)S(1)} collective-permute-done((bf16[128,128]{1,0:T(8,128)(2,1)S(1)}, bf16[128,128]{1,0:T(8,128)(2,1)S(1)}, u32[]{:S(2)}, u32[]{:S(2)}) %collective-permute-start.8) | collective-permute-done | bytes 32800 | tf_op jit(solution)/shard_map/ppermute | solution.py:745
  28.5 1.6 %collective-permute-start.9 = (bf16[128,128]{1,0:T(8,128)(2,1)S(1)}, bf16[128,128]{1,0:T(8,128)(2,1)S(1)}, u32[]{:S(2)}, u32[]{:S(2)}) collective-permute-start(bf16[128,128]{1,0:T(8,128)(2,1)S(1)} %get-tuple-element.70), channel_id=1, source_target_pairs={{0,1},{1,0},{2,3},{3,2},{4,5},{5,4},{6,7},{7,6},{8,9},{9,8},{10,11... | collective-permute-start | bytes 98312 | tf_op jit(solution)/shard_map/ppermute | solution.py:750
  30.2 1.1 %shard_map.166.old_ref = f32[14,128,512]{2,1,0:T(8,128)S(1)} custom-call(bf16[128,128]{1,0:T(8,128)(2,1)S(1)} %get-tuple-element.71.h2_ref, bf16[128,128]{1,0:T(8,128)(2,1)S(1)} %get-tuple-element.72.h3_ref, bf16[14,640,512]{2,1,0:T(8,128)(2,1)S(1)} %get-tuple-element.55.hot_ref, f32[14,128,512]{2,1,0:T(8,128)S(1)} %shard_map.165.old_ref), custom_call_target="tpu_custom_call", output_to_operand_aliasing={{}: (3, {})} | custom-call | flops 1000000000 | bytes 1000000 | tf_op jit(solution)/shard_map/pallas_call | solution.py:723
  31.3 1.2 %collective-permute-done.9.h4_ref = bf16[128,128]{1,0:T(8,128)(2,1)S(1)} collective-permute-done((bf16[128,128]{1,0:T(8,128)(2,1)S(1)}, bf16[128,128]{1,0:T(8,128)(2,1)S(1)}, u32[]{:S(2)}, u32[]{:S(2)}) %collective-permute-start.9) | collective-permute-done | bytes 32800 | tf_op jit(solution)/shard_map/ppermute | solution.py:750
  32.6 7.4 %shard_map.168 = (f32[14,128,512]{2,1,0:T(8,128)S(1)}, f32[1,128]{1,0:T(1,128)S(1)}, f32[9,128,128]{2,1,0:T(8,128)S(1)}, f32[128,128]{1,0:T(8,128)S(1)}, bf16[14...) custom-call(bf16[128,128]{1,0:T(8,128)(2,1)S(1)} %get-tuple-element.64.h0_ref, ...), custom_call_target="tpu_custom_call", output_to_operand_aliasing={{0}: (3, {})} | custom-call | flops 1000000000 | bytes 1000000 | tf_op jit(solution)/shard_map/pallas_call | solution.py:723
  40.8 1.6 %shard_map.173.ga_ref = f32[64,128]{1,0:T(8,128)S(1)} custom-call(f32[14,128,512]{2,1,0:T(8,128)S(1)} %get-tuple-element.89.hg_ref, f32[14,128,512]{2,1,0:T(8,128)S(1)} %get-tuple-element.76.rad_ref, f32[14,128,512]{2,1,0:T(8,128)S(1)} %get-tuple-element.90.slo_ref, f32[9,128,128]{2,1,0:T(8,128)S(1)} %get-tuple-element.91.d_ref, ...), custom_call_target="tpu_custom_call" | custom-call | flops 1000000000 | bytes 1000000 | tf_op jit(solution)/shard_map/pallas_call | solution.py:723
  42.4 1.6 %collective-permute-start.10 = (bf16[128,128]{1,0:T(8,128)(2,1)S(1)}, bf16[128,128]{1,0:T(8,128)(2,1)S(1)}, u32[]{:S(2)}, u32[]{:S(2)}) collective-permute-start(bf16[128,128]{1,0:T(8,128)(2,1)S(1)} %get-tuple-element.79), channel_id=1, source_target_pairs={{0,1},{1,0},{2,3},{3,2},{4,5},{5,4},{6,7},{7,6},{8,9},{9,8},{10,11... | collective-permute-start | bytes 98312 | tf_op jit(solution)/shard_map/ppermute | solution.py:750
  44.0 1.1 %shard_map.169.gy_ref = f32[256,128]{1,0:T(8,128)S(1)} custom-call(bf16[14,640,512]{2,1,0:T(8,128)(2,1)S(1)} %get-tuple-element.55.hot_ref, bf16[14,128,512]{2,1,0:T(8,128)(2,1)S(1)} %get-tuple-element.78.rq_ref), custom_call_target="tpu_custom_call" | custom-call | flops 1000000000 | bytes 1000000 | tf_op jit(solution)/shard_map/pallas_call | solution.py:723
  45.1 1.3 %collective-permute-done.10.az_ref = bf16[128,128]{1,0:T(8,128)(2,1)S(1)} collective-permute-done((bf16[128,128]{1,0:T(8,128)(2,1)S(1)}, bf16[128,128]{1,0:T(8,128)(2,1)S(1)}, u32[]{:S(2)}, u32[]{:S(2)}) %collective-permute-start.10) | collective-permute-done | bytes 32800 | tf_op jit(solution)/shard_map/ppermute | solution.py:750
  46.7 1.6 %collective-permute-start.12 = (bf16[128,128]{1,0:T(8,128)(2,1)S(1)}, bf16[128,128]{1,0:T(8,128)(2,1)S(1)}, u32[]{:S(2)}, u32[]{:S(2)}) collective-permute-start(bf16[128,128]{1,0:T(8,128)(2,1)S(1)} %get-tuple-element.83), channel_id=1, source_target_pairs={{0,6},{2,4},{4,2},{6,0},{1,7},{3,5},{5,3},{7,1},{8,14},{10,12},{12... | collective-permute-start | bytes 98312 | tf_op jit(solution)/shard_map/ppermute | solution.py:745
  48.2 1.1 %shard_map.171.gx_ref = f32[256,128]{1,0:T(8,128)S(1)} custom-call(bf16[14,640,512]{2,1,0:T(8,128)(2,1)S(1)} %get-tuple-element.55.hot_ref, bf16[14,128,512]{2,1,0:T(8,128)(2,1)S(1)} %get-tuple-element.78.rq_ref), custom_call_target="tpu_custom_call" | custom-call | flops 1000000000 | bytes 1000000 | tf_op jit(solution)/shard_map/pallas_call | solution.py:723
  50.5 1.8 %collective-permute-start.14 = (bf16[64,128]{1,0:T(8,128)(2,1)S(1)}, bf16[64,128]{1,0:T(8,128)(2,1)S(1)}, u32[]{:S(2)}, u32[]{:S(2)}) collective-permute-start(bf16[64,128]{1,0:T(8,128)(2,1)S(1)} %get-tuple-element.86), channel_id=1, source_target_pairs={{0,24},{8,16},{16,8},{24,0},{1,25},{9,17},{17,9},{25,1},{2,26},{10... | collective-permute-start | bytes 49160 | tf_op jit(solution)/shard_map/ppermute | solution.py:745
  52.3 3.2 %shard_map.175.gc_ref = f32[128,128]{1,0:T(8,128)S(1)} custom-call(f32[14,128,512]{2,1,0:T(8,128)S(1)} %get-tuple-element.89.hg_ref, f32[14,128,512]{2,1,0:T(8,128)S(1)} %get-tuple-element.76.rad_ref, f32[14,128,512]{2,1,0:T(8,128)S(1)} %get-tuple-element.90.slo_ref, f32[9,128,128]{2,1,0:T(8,128)S(1)} %get-tuple-element.91.d_ref, ...), custom_call_target="tpu_custom_call" | custom-call | flops 1000000000 | bytes 1000000 | tf_op jit(solution)/shard_map/pallas_call | solution.py:723
  56.0 1.6 %shard_map.176 = (f32[8,128]{1,0:T(8,128)S(1)}, f32[8,128]{1,0:T(8,128)S(1)}, f32[8,128]{1,0:T(8,128)S(1)}, f32[8,128]{1,0:T(8,128)S(1)}, f32[8,128]{1,0:T(8,128)S(1)}) custom-call(s32[8,128]{1,0:T(8,128)S(1)} %get-tuple-element.54.side_ref, f32[128,128]{1,0:T(8,128)S(1)} %get-tuple-element.84.own_ref, bf16[64,128]{1,0:T(8,128)(2,1)S(1)} %collective-permute-done.13.near_ref, ...), custom_call_target="tpu_custom_call" | custom-call | flops 1000000000 | bytes 1000000 | tf_op jit(solution)/shard_map/pallas_call | solution.py:723
  57.5 1.6 %collective-permute-start.15 = (f32[8,128]{1,0:T(8,128)S(1)}, f32[8,128]{1,0:T(8,128)S(1)}, u32[]{:S(2)}, u32[]{:S(2)}) collective-permute-start(f32[8,128]{1,0:T(8,128)S(1)} %get-tuple-element.97), channel_id=1, source_target_pairs={{0,1},{1,0},{2,3},{3,2},{4,5},{5,4},{6,7},{7,6},{8,9},{9,8},{10,11... | collective-permute-start | bytes 12296 | tf_op jit(solution)/shard_map/ppermute | solution.py:750
  59.1 2.1 %collective-permute-done.15.az_ref = f32[8,128]{1,0:T(8,128)S(1)} collective-permute-done((f32[8,128]{1,0:T(8,128)S(1)}, f32[8,128]{1,0:T(8,128)S(1)}, u32[]{:S(2)}, u32[]{:S(2)}) %collective-permute-start.15) | collective-permute-done | bytes 4128 | tf_op jit(solution)/shard_map/ppermute | solution.py:750
  61.4 1.6 %collective-permute-start.17 = (f32[8,128]{1,0:T(8,128)S(1)}, f32[8,128]{1,0:T(8,128)S(1)}, u32[]{:S(2)}, u32[]{:S(2)}) collective-permute-start(f32[8,128]{1,0:T(8,128)S(1)} %get-tuple-element.100), channel_id=1, source_target_pairs={{0,6},{2,4},{4,2},{6,0},{1,7},{3,5},{5,3},{7,1},{8,14},{10,12},{12... | collective-permute-start | bytes 12296 | tf_op jit(solution)/shard_map/ppermute | solution.py:745
  63.0 1.5 %collective-permute-done.17.far_ref = f32[8,128]{1,0:T(8,128)S(1)} collective-permute-done((f32[8,128]{1,0:T(8,128)S(1)}, f32[8,128]{1,0:T(8,128)S(1)}, u32[]{:S(2)}, u32[]{:S(2)}) %collective-permute-start.17) | collective-permute-done | bytes 4128 | tf_op jit(solution)/shard_map/ppermute | solution.py:745
  64.7 1.8 %collective-permute-start.19 = (f32[8,128]{1,0:T(8,128)S(1)}, f32[8,128]{1,0:T(8,128)S(1)}, u32[]{:S(2)}, u32[]{:S(2)}) collective-permute-start(f32[8,128]{1,0:T(8,128)S(1)} %get-tuple-element.102), channel_id=1, source_target_pairs={{0,24},{8,16},{16,8},{24,0},{1,25},{9,17},{17,9},{25,1},{2,26},{10... | collective-permute-start | bytes 12296 | tf_op jit(solution)/shard_map/ppermute | solution.py:745
  66.5 3.6 %collective-permute-done.19.far_ref = f32[8,128]{1,0:T(8,128)S(1)} collective-permute-done((f32[8,128]{1,0:T(8,128)S(1)}, f32[8,128]{1,0:T(8,128)S(1)}, u32[]{:S(2)}, u32[]{:S(2)}) %collective-permute-start.19) | collective-permute-done | bytes 4128 | tf_op jit(solution)/shard_map/ppermute | solution.py:745
  (62 shorter events, 7.7 us)
Async XLA Ops:
  0.6 10.2 %copy-start.11 = (s32[1,1,1,2,128]{4,3,2,1,0:T(2,128)S(1)}, s32[1,1,1,2,128]{4,3,2,1,0:T(2,128)}, u32[]{:S(2)}) copy-start(s32[1,1,1,2,128]{4,3,2,1,0:T(2,128)} %param.20) | copy-start | bytes 3076
  2.0 12.1 %copy-start.15 = (s32[1,1,1,128]{3,2,1,0:T(1,128)S(1)}, s32[1,1,1,128]{3,2,1,0:T(1,128)}, u32[]{:S(2)}) copy-start(s32[1,1,1,128]{3,2,1,0:T(1,128)} %param.21) | copy-start | bytes 1540
  2.2 6.7 %collective-permute-start.1 = (f32[8,128]{1,0:T(8,128)S(1)}, f32[8,128]{1,0:T(8,128)S(1)}, u32[]{:S(2)}, u32[]{:S(2)}) collective-permute-start(f32[8,128]{1,0:T(8,128)S(1)} %get-tuple-element.57), channel_id=1, source_target_pairs={{0,24},{8,16},{16,8},{24,0},{1,25},{9,17},{17,9},{25,1},{2,26},{10... | collective-permute-start | bytes 12296 | tf_op jit(solution)/shard_map/ppermute | solution.py:745
  7.2 3.6 %collective-permute-start = (f32[8,128]{1,0:T(8,128)S(1)}, f32[8,128]{1,0:T(8,128)S(1)}, u32[]{:S(2)}, u32[]{:S(2)}) collective-permute-start(f32[8,128]{1,0:T(8,128)S(1)} %get-tuple-element.57), channel_id=1, source_target_pairs={{0,8},{8,0},{16,24},{24,16},{1,9},{9,1},{17,25},{25,17},{2,10},{10... | collective-permute-start | bytes 12296 | tf_op jit(solution)/shard_map/ppermute | solution.py:745
  10.9 4.8 %copy-start.7 = (s32[56,1,1,1,128]{4,3,2,1,0:T(1,128)S(1)}, s32[56,1,1,1,128]{4,3,2,1,0:T(1,128)}, u32[]{:S(2)}) copy-start(s32[56,1,1,1,128]{4,3,2,1,0:T(1,128)} %param.17) | copy-start | bytes 86020
  11.0 1.6 %collective-permute-start.2 = (f32[8,128]{1,0:T(8,128)S(1)}, f32[8,128]{1,0:T(8,128)S(1)}, u32[]{:S(2)}, u32[]{:S(2)}) collective-permute-start(f32[8,128]{1,0:T(8,128)S(1)} %get-tuple-element.59), channel_id=1, source_target_pairs={{0,2},{2,0},{4,6},{6,4},{1,3},{3,1},{5,7},{7,5},{8,10},{10,8},{12,... | collective-permute-start | bytes 12296 | tf_op jit(solution)/shard_map/ppermute | solution.py:745
  11.0 3.1 %collective-permute-start.3 = (f32[8,128]{1,0:T(8,128)S(1)}, f32[8,128]{1,0:T(8,128)S(1)}, u32[]{:S(2)}, u32[]{:S(2)}) collective-permute-start(f32[8,128]{1,0:T(8,128)S(1)} %get-tuple-element.60), channel_id=1, source_target_pairs={{0,6},{2,4},{4,2},{6,0},{1,7},{3,5},{5,3},{7,1},{8,14},{10,12},{12... | collective-permute-start | bytes 12296 | tf_op jit(solution)/shard_map/ppermute | solution.py:745
  14.1 3.7 %copy-start.5 = (bf16[384,128]{1,0:T(8,128)(2,1)S(1)}, bf16[384,128]{1,0:T(8,128)(2,1)}, u32[]{:S(2)}) copy-start(bf16[384,128]{1,0:T(8,128)(2,1)} %mix_ref.5) | copy-start | bytes 294916
  14.1 3.7 %copy-start.6 = (s32[56,1,1,1,128]{4,3,2,1,0:T(1,128)S(1)}, s32[56,1,1,1,128]{4,3,2,1,0:T(1,128)}, u32[]{:S(2)}) copy-start(s32[56,1,1,1,128]{4,3,2,1,0:T(1,128)} %param.18) | copy-start | bytes 86020
  14.1 3.7 %copy-start.9 = (f32[8,128]{1,0:T(8,128)S(1)}, f32[8,128]{1,0:T(8,128)}, u32[]{:S(2)}) copy-start(f32[8,128]{1,0:T(8,128)} %radial_ref.5) | copy-start | bytes 12292
  14.1 3.7 %copy-start.13 = (s32[1,1,1,2,64]{4,3,2,1,0:T(2,128)S(1)}, s32[1,1,1,2,64]{4,3,2,1,0:T(2,128)}, u32[]{:S(2)}) copy-start(s32[1,1,1,2,64]{4,3,2,1,0:T(2,128)} %param.19) | copy-start | bytes 1540
  14.1 3.7 %copy-start.14 = (f32[128]{0:T(128)S(1)}, f32[128]{0:T(128)}, u32[]{:S(2)}) copy-start(f32[128]{0:T(128)} %param.24) | copy-start | bytes 1540
  14.2 3.6 %collective-permute-start.4 = (f32[8,128]{1,0:T(8,128)S(1)}, f32[8,128]{1,0:T(8,128)S(1)}, u32[]{:S(2)}, u32[]{:S(2)}) collective-permute-start(f32[8,128]{1,0:T(8,128)S(1)} %get-tuple-element.63), channel_id=1, source_target_pairs={{0,1},{1,0},{2,3},{3,2},{4,5},{5,4},{6,7},{7,6},{8,9},{9,8},{10,11... | collective-permute-start | bytes 12296 | tf_op jit(solution)/shard_map/ppermute | solution.py:750
  15.7 5.2 %copy-start.8 = (f32[8,128]{1,0:T(8,128)S(1)}, f32[8,128]{1,0:T(8,128)}, u32[]{:S(2)}) copy-start(f32[8,128]{1,0:T(8,128)} %radial_ref.4) | copy-start | bytes 12292
  19.0 3.8 %collective-permute-start.5 = (bf16[64,128]{1,0:T(8,128)(2,1)S(1)}, bf16[64,128]{1,0:T(8,128)(2,1)S(1)}, u32[]{:S(2)}, u32[]{:S(2)}) collective-permute-start(bf16[64,128]{1,0:T(8,128)(2,1)S(1)} %get-tuple-element.65), channel_id=1, source_target_pairs={{0,8},{8,0},{16,24},{24,16},{1,9},{9,1},{17,25},{25,17},{2,10},{10... | collective-permute-start | bytes 49160 | tf_op jit(solution)/shard_map/ppermute | solution.py:745
  19.1 5.6 %collective-permute-start.6 = (bf16[64,128]{1,0:T(8,128)(2,1)S(1)}, bf16[64,128]{1,0:T(8,128)(2,1)S(1)}, u32[]{:S(2)}, u32[]{:S(2)}) collective-permute-start(bf16[64,128]{1,0:T(8,128)(2,1)S(1)} %get-tuple-element.66), channel_id=1, source_target_pairs={{0,24},{8,16},{16,8},{24,0},{1,25},{9,17},{17,9},{25,1},{2,26},{10... | collective-permute-start | bytes 49160 | tf_op jit(solution)/shard_map/ppermute | solution.py:745
  24.9 2.3 %collective-permute-start.7 = (bf16[128,128]{1,0:T(8,128)(2,1)S(1)}, bf16[128,128]{1,0:T(8,128)(2,1)S(1)}, u32[]{:S(2)}, u32[]{:S(2)}) collective-permute-start(bf16[128,128]{1,0:T(8,128)(2,1)S(1)} %get-tuple-element.68), channel_id=1, source_target_pairs={{0,2},{2,0},{4,6},{6,4},{1,3},{3,1},{5,7},{7,5},{8,10},{10,8},{12,... | collective-permute-start | bytes 98312 | tf_op jit(solution)/shard_map/ppermute | solution.py:745
  25.0 3.4 %collective-permute-start.8 = (bf16[128,128]{1,0:T(8,128)(2,1)S(1)}, bf16[128,128]{1,0:T(8,128)(2,1)S(1)}, u32[]{:S(2)}, u32[]{:S(2)}) collective-permute-start(bf16[128,128]{1,0:T(8,128)(2,1)S(1)} %get-tuple-element.69), channel_id=1, source_target_pairs={{0,6},{2,4},{4,2},{6,0},{1,7},{3,5},{5,3},{7,1},{8,14},{10,12},{12... | collective-permute-start | bytes 98312 | tf_op jit(solution)/shard_map/ppermute | solution.py:745
  28.5 4.0 %collective-permute-start.9 = (bf16[128,128]{1,0:T(8,128)(2,1)S(1)}, bf16[128,128]{1,0:T(8,128)(2,1)S(1)}, u32[]{:S(2)}, u32[]{:S(2)}) collective-permute-start(bf16[128,128]{1,0:T(8,128)(2,1)S(1)} %get-tuple-element.70), channel_id=1, source_target_pairs={{0,1},{1,0},{2,3},{3,2},{4,5},{5,4},{6,7},{7,6},{8,9},{9,8},{10,11... | collective-permute-start | bytes 98312 | tf_op jit(solution)/shard_map/ppermute | solution.py:750
  30.1 2.4 %copy-start.2 = (s32[1,1,1,128]{3,2,1,0:T(1,128)S(1)}, s32[1,1,1,128]{3,2,1,0:T(1,128)}, u32[]{:S(2)}) copy-start(s32[1,1,1,128]{3,2,1,0:T(1,128)} %param.16) | copy-start | bytes 1540
  30.1 2.4 %copy-start.3 = (f32[128]{0:T(128)S(1)}, f32[128]{0:T(128)}, u32[]{:S(2)}) copy-start(f32[128]{0:T(128)} %param.27) | copy-start | bytes 1540
  30.1 2.4 %copy-start.4 = (f32[16]{0:T(128)S(1)}, f32[16]{0:T(128)}, u32[]{:S(2)}) copy-start(f32[16]{0:T(128)} %param.29) | copy-start | bytes 196
  42.4 4.0 %collective-permute-start.10 = (bf16[128,128]{1,0:T(8,128)(2,1)S(1)}, bf16[128,128]{1,0:T(8,128)(2,1)S(1)}, u32[]{:S(2)}, u32[]{:S(2)}) collective-permute-start(bf16[128,128]{1,0:T(8,128)(2,1)S(1)} %get-tuple-element.79), channel_id=1, source_target_pairs={{0,1},{1,0},{2,3},{3,2},{4,5},{5,4},{6,7},{7,6},{8,9},{9,8},{10,11... | collective-permute-start | bytes 98312 | tf_op jit(solution)/shard_map/ppermute | solution.py:750
  46.6 2.8 %collective-permute-start.11 = (bf16[128,128]{1,0:T(8,128)(2,1)S(1)}, bf16[128,128]{1,0:T(8,128)(2,1)S(1)}, u32[]{:S(2)}, u32[]{:S(2)}) collective-permute-start(bf16[128,128]{1,0:T(8,128)(2,1)S(1)} %get-tuple-element.82), channel_id=1, source_target_pairs={{0,2},{2,0},{4,6},{6,4},{1,3},{3,1},{5,7},{7,5},{8,10},{10,8},{12,... | collective-permute-start | bytes 98312 | tf_op jit(solution)/shard_map/ppermute | solution.py:745
  46.7 3.4 %collective-permute-start.12 = (bf16[128,128]{1,0:T(8,128)(2,1)S(1)}, bf16[128,128]{1,0:T(8,128)(2,1)S(1)}, u32[]{:S(2)}, u32[]{:S(2)}) collective-permute-start(bf16[128,128]{1,0:T(8,128)(2,1)S(1)} %get-tuple-element.83), channel_id=1, source_target_pairs={{0,6},{2,4},{4,2},{6,0},{1,7},{3,5},{5,3},{7,1},{8,14},{10,12},{12... | collective-permute-start | bytes 98312 | tf_op jit(solution)/shard_map/ppermute | solution.py:745
  50.2 5.2 %collective-permute-start.13 = (bf16[64,128]{1,0:T(8,128)(2,1)S(1)}, bf16[64,128]{1,0:T(8,128)(2,1)S(1)}, u32[]{:S(2)}, u32[]{:S(2)}) collective-permute-start(bf16[64,128]{1,0:T(8,128)(2,1)S(1)} %get-tuple-element.85), channel_id=1, source_target_pairs={{0,8},{8,0},{16,24},{24,16},{1,9},{9,1},{17,25},{25,17},{2,10},{10... | collective-permute-start | bytes 49160 | tf_op jit(solution)/shard_map/ppermute | solution.py:745
  50.5 5.5 %collective-permute-start.14 = (bf16[64,128]{1,0:T(8,128)(2,1)S(1)}, bf16[64,128]{1,0:T(8,128)(2,1)S(1)}, u32[]{:S(2)}, u32[]{:S(2)}) collective-permute-start(bf16[64,128]{1,0:T(8,128)(2,1)S(1)} %get-tuple-element.86), channel_id=1, source_target_pairs={{0,24},{8,16},{16,8},{24,0},{1,25},{9,17},{17,9},{25,1},{2,26},{10... | collective-permute-start | bytes 49160 | tf_op jit(solution)/shard_map/ppermute | solution.py:745
  57.5 3.7 %collective-permute-start.15 = (f32[8,128]{1,0:T(8,128)S(1)}, f32[8,128]{1,0:T(8,128)S(1)}, u32[]{:S(2)}, u32[]{:S(2)}) collective-permute-start(f32[8,128]{1,0:T(8,128)S(1)} %get-tuple-element.97), channel_id=1, source_target_pairs={{0,1},{1,0},{2,3},{3,2},{4,5},{5,4},{6,7},{7,6},{8,9},{9,8},{10,11... | collective-permute-start | bytes 12296 | tf_op jit(solution)/shard_map/ppermute | solution.py:750
  61.4 1.6 %collective-permute-start.16 = (f32[8,128]{1,0:T(8,128)S(1)}, f32[8,128]{1,0:T(8,128)S(1)}, u32[]{:S(2)}, u32[]{:S(2)}) collective-permute-start(f32[8,128]{1,0:T(8,128)S(1)} %get-tuple-element.99), channel_id=1, source_target_pairs={{0,2},{2,0},{4,6},{6,4},{1,3},{3,1},{5,7},{7,5},{8,10},{10,8},{12,... | collective-permute-start | bytes 12296 | tf_op jit(solution)/shard_map/ppermute | solution.py:745
  61.4 3.1 %collective-permute-start.17 = (f32[8,128]{1,0:T(8,128)S(1)}, f32[8,128]{1,0:T(8,128)S(1)}, u32[]{:S(2)}, u32[]{:S(2)}) collective-permute-start(f32[8,128]{1,0:T(8,128)S(1)} %get-tuple-element.100), channel_id=1, source_target_pairs={{0,6},{2,4},{4,2},{6,0},{1,7},{3,5},{5,3},{7,1},{8,14},{10,12},{12... | collective-permute-start | bytes 12296 | tf_op jit(solution)/shard_map/ppermute | solution.py:745
  64.7 5.4 %collective-permute-start.19 = (f32[8,128]{1,0:T(8,128)S(1)}, f32[8,128]{1,0:T(8,128)S(1)}, u32[]{:S(2)}, u32[]{:S(2)}) collective-permute-start(f32[8,128]{1,0:T(8,128)S(1)} %get-tuple-element.102), channel_id=1, source_target_pairs={{0,24},{8,16},{16,8},{24,0},{1,25},{9,17},{17,9},{25,1},{2,26},{10... | collective-permute-start | bytes 12296 | tf_op jit(solution)/shard_map/ppermute | solution.py:745
  66.5 3.6 %collective-permute-start.18 = (f32[8,128]{1,0:T(8,128)S(1)}, f32[8,128]{1,0:T(8,128)S(1)}, u32[]{:S(2)}, u32[]{:S(2)}) collective-permute-start(f32[8,128]{1,0:T(8,128)S(1)} %get-tuple-element.102), channel_id=1, source_target_pairs={{0,8},{8,0},{16,24},{24,16},{1,9},{9,1},{17,25},{25,17},{2,10},{10... | collective-permute-start | bytes 12296 | tf_op jit(solution)/shard_map/ppermute | solution.py:745
  (4 other events, 6.2 us)

commit v4 on v3

--- a/solution.py
+++ b/solution.py
@@ -162,6 +162,7 @@
     h0_ref,
     to_near_ref,
     to_far_ref,
+    last_ref,
     mom_ref,
 ):
     entries, atoms = nbr_ref.shape
@@ -170,6 +171,7 @@
     block = nbr >> (atoms.bit_length() - 1)
     rise = jnp.where(side_ref[2:3, :] == 0, LZ * SPACING, -LZ * SPACING)
     last = pz_ref[...] + shift_rows(pz_ref.shape, 2, rise)
+    last_ref[...] = last
     tables = [pos_ref[...], p1_ref[...], p2_ref[...], p3_ref[...], last]
     vec = []
     for axis in range(3):
@@ -187,27 +189,10 @@
     unit_ref[0:entries, :] = ux
     unit_ref[entries : 2 * entries, :] = uy
     unit_ref[2 * entries : 3 * entries, :] = uz
-    scaled = jnp.minimum(dist * (1.0 / CUTOFF), 1.0)
-    phase = scaled * math.pi
-    sine = jnp.sin(phase)
-    cosine = jnp.cos(phase)
-    inner = 1.0 - scaled * scaled
-    weight = keep_ref[...].astype(F32) * (2.0 / CUTOFF) ** 0.5
-    env = weight * inner * inner * rinv
-    env_slope = -env * rinv - weight * rinv * (4.0 / CUTOFF) * scaled * inner
-    twice = 2.0 * cosine
-    s_prev, s_now = jnp.zeros_like(sine), sine
-    c_prev, c_now = jnp.ones_like(cosine), cosine
-    basis = []
+    basis, slopes = radial_parts(dist, rinv, keep_ref[...].astype(F32), True)
     for k in range(NB):
-        bk = s_now * env
-        basis.append(bk)
-        basis_ref[k * entries : (k + 1) * entries, :] = bk
-        slope_ref[k * entries : (k + 1) * entries, :] = (
-            c_now * env * ((k + 1) * math.pi / CUTOFF) + s_now * env_slope
-        )
-        s_prev, s_now = s_now, twice * s_now - s_prev
-        c_prev, c_now = c_now, twice * c_now - c_prev
+        basis_ref[k * entries : (k + 1) * entries, :] = basis[k]
+        slope_ref[k * entries : (k + 1) * entries, :] = slopes[k]
     angular = harmonics(ux, uy, uz)
     for m in range(9):
         for k in range(NB):
@@ -224,6 +209,28 @@
     to_near_ref[...], to_far_ref[...] = pack_halves(both)
 
 
+def radial_parts(dist, rinv, weight, with_slope):
+    scaled = jnp.minimum(dist * (1.0 / CUTOFF), 1.0)
+    phase = scaled * math.pi
+    sine = jnp.sin(phase)
+    cosine = jnp.cos(phase)
+    inner = 1.0 - scaled * scaled
+    weight = weight * (2.0 / CUTOFF) ** 0.5
+    env = weight * inner * inner * rinv
+    env_slope = -env * rinv - weight * rinv * (4.0 / CUTOFF) * scaled * inner
+    twice = 2.0 * cosine
+    s_prev, s_now = jnp.zeros_like(sine), sine
+    c_prev, c_now = jnp.ones_like(cosine), cosine
+    basis, slopes = [], []
+    for k in range(NB):
+        basis.append(s_now * env)
+        if with_slope:
+            slopes.append(c_now * env * ((k + 1) * math.pi / CUTOFF) + s_now * env_slope)
+            c_prev, c_now = c_now, twice * c_now - c_prev
+        s_prev, s_now = s_now, twice * s_now - s_prev
+    return basis, slopes
+
+
 def harmonics(ux, uy, uz):
     return [
         None,
@@ -291,16 +298,42 @@
     return jnp.concatenate([ref[pl.ds(first + jj, 1), :] for jj in range(GROUP)], axis=1)
 
 
-def hot_kernel(nbr_ref, hot_ref, lane_ref):
+def hot_kernel(nbr_ref, keep_ref, hot_ref, lane_ref, count_ref):
     atoms = nbr_ref.shape[1]
+    count_ref[...] = jnp.zeros_like(count_ref)
+    ids = lax.broadcasted_iota(jnp.int32, (atoms, atoms), 0) + 4 * atoms
 
     def body(step, carry):
-        row = entry_rows(nbr_ref, step * GROUP)
+        first = step * GROUP
+        row = entry_rows(nbr_ref, first)
         hot_ref[step] = onehot(row, hot_ref.shape[1])
         lane_ref[step] = onehot(row & (atoms - 1), atoms)
+        count = count_ref[...]
+        for jj in range(GROUP):
+            at = pl.ds(first + jj, 1)
+            count = count + jnp.where(ids == nbr_ref[at, :], keep_ref[at, :].astype(F32), 0.0)
+        count_ref[...] = count
         return carry
 
     lax.fori_loop(0, hot_ref.shape[0], body, 0)
+
+
+def pair_kernel(pos_ref, last_ref, count_ref, radial_ref, pair_ref, wide_ref):
+    atoms = pos_ref.shape[1]
+    weight = count_ref[...]
+    vec = []
+    for axis in range(3):
+        vec.append(columns(last_ref[axis : axis + 1, :], atoms) - pos_ref[axis : axis + 1, :])
+    r_sq = vec[0] * vec[0] + vec[1] * vec[1] + vec[2] * vec[2]
+    dist = jnp.sqrt(jnp.where(weight > 0.0, r_sq, 1.0))
+    rinv = 1.0 / dist
+    basis, _ = radial_parts(dist, rinv, weight, False)
+    angular = harmonics(*(v * rinv for v in vec))
+    for k in range(NB):
+        wide_ref[:, k * atoms : (k + 1) * atoms] = columns(radial_ref[k : k + 1, :], atoms)
+        for m in range(9):
+            value = basis[k] if m == 0 else basis[k] * angular[m]
+            pair_ref[k * atoms : (k + 1) * atoms, m * atoms : (m + 1) * atoms] = value.astype(BF16)
 
 
 def stack3(hi, lo):
@@ -353,35 +386,18 @@
         hg_ref[step] = old_ref[step] + more
 
 
-def layer_two_kernel(
-    h0_ref,
-    h4_ref,
-    hot_ref,
-    old_ref,
-    rad_ref,
-    y_ref,
-    occ_ref,
-    mix_ref,
-    rone_ref,
-    rhid_ref,
-    rout_ref,
-    hg_ref,
-    en_ref,
-    raw_ref,
-    extra_ref,
-    rq_ref,
-    gz_ref,
-    acc_ref,
-    dh_ref,
-):
-    channels, atoms = h0_ref.shape
-    steps = hot_ref.shape[0]
+def gather_last_kernel(h4_ref, hot_ref, old_ref, hg_ref):
+    atoms = h4_ref.shape[1]
+    for step in range(hot_ref.shape[0]):
+        hg_ref[step] = old_ref[step] + dot(h4_ref[...], hot_ref[step, 4 * atoms :, :])
+
+
+def partial_kernel(hg_ref, rad_ref, y_ref, acc_ref):
+    steps, channels, width = hg_ref.shape
+    atoms = width // GROUP
     entries = steps * GROUP
     blocks = channels // 8
     acc_ref[...] = jnp.zeros_like(acc_ref)
-
-    def prepare(step):
-        hg_ref[step] = old_ref[step] + dot(h4_ref[...], hot_ref[step, 4 * atoms :, :])
 
     def accumulate(step):
         first = step * GROUP
@@ -407,22 +423,41 @@
                         terms = [a + b for a, b in zip(terms[::2], terms[1::2])]
                     acc_ref[m, rows, :] += terms[0]
 
-    prepare(0)
-    prepare(1)
-
-    def forward_body(trip, carry):
+    def body(trip, carry):
         for part in range(2):
             accumulate(2 * trip + part)
-        for part in range(2):
-            prepare(2 * trip + 2 + part)
         return carry
 
-    lax.fori_loop(0, steps // 2 - 1, forward_body, 0)
-    for part in range(2):
-        accumulate(steps - 2 + part)
-
+    lax.fori_loop(0, steps // 2, body, 0)
+
+
+def layer_two_kernel(
+    h0_ref,
+    h4_ref,
+    acc_ref,
+    pair_ref,
+    wide_ref,
+    occ_ref,
+    mix_ref,
+    radial_ref,
+    rone_ref,
+    rhid_ref,
+    rout_ref,
+    en_ref,
+    raw_ref,
+    extra_ref,
+    gz_ref,
+    wz_ref,
+    dcat_ref,
+):
+    channels, atoms = h0_ref.shape
+    h4 = h4_ref[...].astype(F32)
+    for k in range(NB):
+        cols = slice(k * atoms, (k + 1) * atoms)
+        wz_ref[:, cols] = (h4 * wide_ref[:, cols]).astype(BF16)
+    more = dot(wz_ref[...], pair_ref[...])
+    amp = [SPREAD * (acc_ref[m] + more[:, m * atoms : (m + 1) * atoms]) for m in range(9)]
     occ = occ_ref[...].astype(F32)
-    amp = [SPREAD * acc_ref[m] for m in range(9)]
     own = h0_ref[...].astype(F32)
     h2 = dot(mix_ref[...], invariants(amp), 0, 0) + own
     pre = dot3(rhid_ref[...], h2, 1, 0)
@@ -439,10 +474,23 @@
     top = dinv[2 * channels :]
     extra_ref[...] = dh2 + occ * rone
     twice = 2.0 * SPREAD
-    raw_ref[0] = SPREAD * dinv[0:channels]
-    for m in range(1, 9):
-        raw_ref[m] = (twice * amp[m]) * (low if m < 4 else top)
-    dh_ref[...] = jnp.zeros_like(dh_ref)
+    for m in range(9):
+        value = (twice * amp[m]) * (low if m < 4 else top) if m else SPREAD * dinv[0:channels]
+        raw_ref[m] = value
+        dcat_ref[:, m * atoms : (m + 1) * atoms] = value.astype(BF16)
+    back = dot(pair_ref[...], dcat_ref[...], 1, 1)
+    total = None
+    for k in range(NB):
+        part = radial_ref[k : k + 1, :] * back[k * atoms : (k + 1) * atoms, :]
+        total = part if total is None else total + part
+    gz_ref[...] = total.astype(BF16)
+
+
+def reverse_kernel(raw_ref, rad_ref, y_ref, rq_ref, q_ref):
+    steps, channels, width = rad_ref.shape
+    atoms = width // GROUP
+    entries = steps * GROUP
+    blocks = channels // 8
 
     def reverse(step):
         first = step * GROUP
@@ -458,33 +506,18 @@
                     q = terms[0] + terms[1]
                     for a, b in ((2, 3), (4, 5), (6, 7)):
                         q = q + (terms[a] + terms[b])
-                    parts.append(rad_ref[step, rows, cols] * (q + terms[8]))
+                    q = q + terms[8]
+                    q_ref[step, rows, cols] = q
+                    parts.append(rad_ref[step, rows, cols] * q)
                 value = jnp.concatenate(parts, axis=0).astype(BF16)
                 rq_ref[step, pair * 16 : pair * 16 + 16, cols] = value
 
-    def send(step):
-        low = dot(hot_ref[step, 4 * atoms :, :], rq_ref[step], 1, 1)
-        return low + dot(hot_ref[step + 1, 4 * atoms :, :], rq_ref[step + 1], 1, 1)
-
-    reverse(0)
-    reverse(1)
-
-    def reverse_body(trip, carry):
-        dh_ref[...] += send(2 * trip)
+    def body(trip, carry):
         for part in range(2):
-            reverse(2 * trip + 2 + part)
+            reverse(2 * trip + part)
         return carry
 
-    lax.fori_loop(0, steps // 2 - 1, reverse_body, 0)
-    gz_ref[...] = (dh_ref[...] + send(steps - 2)).astype(BF16)
-
-
-def directions(d, unit):
-    vx, vy, vz = unit
-    cx = vy * d[4] + vz * d[7] + vx * d[8]
-    cy = vx * d[4] + vz * d[5] - vy * d[8]
-    cz = vy * d[5] + vx * d[7] + vz * d[6]
-    return d[1] + cx, d[2] + cy, d[3] + cz, (cx, cy, cz)
+    lax.fori_loop(0, steps // 2, body, 0)
 
 
 def scatter_kernel(first, hot_ref, rq_ref, out_ref):
@@ -496,17 +529,15 @@
     out_ref[...] = total
 
 
-def edge_kernel(start, hg_ref, rad_ref, slo_ref, d_ref, unit_ref, grad_ref, dd_ref):
+def edge_kernel(start, hg_ref, rad_ref, slo_ref, q_ref, d_ref, unit_ref, grad_ref, dd_ref):
     channels, atoms = d_ref.shape[1:]
     entries = hg_ref.shape[0] * GROUP
     count = grad_ref.shape[0] // (4 * GROUP)
-    for m in range(9):
-        if m == 0:
-            dd_ref[m] = d_ref[0] - (0.5 * ROOT5) * d_ref[6]
-        elif m < 4:
+    for m in range(1, 9):
+        if m < 4:
             dd_ref[m] = ROOT3 * d_ref[m]
         else:
-            dd_ref[m] = (1.5 * ROOT5 if m == 6 else 0.5 * ROOT15) * d_ref[m]
+            dd_ref[m] = (3.0 * ROOT5 if m == 6 else ROOT15) * d_ref[m]
 
     def body(step, carry):
         first = step * GROUP
@@ -516,19 +547,17 @@
         sums = [[None] * 4 for _ in range(GROUP)]
         for cb in range(channels // 8):
             rows = slice(cb * 8, cb * 8 + 8)
-            d = [dd_ref[m, rows, :] for m in range(9)]
+            d = [None] + [dd_ref[m, rows, :] for m in range(1, 9)]
             for jj in range(GROUP):
                 cols = slice(jj * atoms, (jj + 1) * atoms)
                 hg = hg_ref[step, rows, cols]
-                ex, ey, ez, (cx, cy, cz) = directions(d, units[jj])
                 vx, vy, vz = units[jj]
-                q = d[0] + vx * ex + vy * ey + vz * ez
                 msg = hg * rad_ref[step, rows, cols]
                 parts = [
-                    msg * (ex + cx),
-                    msg * (ey + cy),
-                    msg * (ez + cz),
-                    hg * q * slo_ref[step, rows, cols],
+                    msg * ((d[1] + vy * d[4]) + (vz * d[7] + vx * d[8])),
+                    msg * ((d[2] + vx * d[4]) + (vz * d[5] - vy * d[8])),
+                    msg * ((d[3] + vy * d[5]) + (vx * d[7] + vz * d[6])),
+                    hg * q_ref[step, rows, cols] * slo_ref[step, rows, cols],
                 ]
                 for i in range(4):
                     prior = sums[jj][i]
@@ -582,7 +611,6 @@
     rinv_ref,
     basis_ref,
     slope_ref,
-    ga_ref,
     gb_ref,
     gc_ref,
     lane_ref,
@@ -620,7 +648,7 @@
     edge = []
     for i in range(4):
         rows = []
-        for ref in (ga_ref, gb_ref, gc_ref):
+        for ref in (gb_ref, gc_ref):
             count = ref.shape[0] // 4
             rows.append(ref[i * count : (i + 1) * count, :])
         edge.append(jnp.concatenate(rows, axis=0))
@@ -799,8 +827,11 @@
     side, pos, sent = call(pos_x_kernel, [side, small, small], pos, fx)
     steps = entries // GROUP
     width = GROUP * atoms
-    hot, lanes = call(
-        hot_kernel, [b16(steps, 5 * atoms, width), b16(steps, atoms, width)], nbr
+    hot, lanes, count = call(
+        hot_kernel,
+        [b16(steps, 5 * atoms, width), b16(steps, atoms, width), f32(atoms, atoms)],
+        nbr,
+        kept,
     )
     near, far = swap_both(sent, sent, "gx")
     p1, near, far = call(pos_y_kernel, [small] * 3, side, pos, near, far, fy)
@@ -810,7 +841,7 @@
 
     half = atoms // 2
     square = b16(channels, atoms)
-    unit, rinv, basis, slope, amp, h0, near, far = call(
+    unit, rinv, basis, slope, amp, h0, near, far, last = call(
         layer_one_kernel,
         [
             f32(3 * entries, atoms),
@@ -821,6 +852,7 @@
             square,
             b16(channels // 2, atoms),
             b16(channels // 2, atoms),
+            small,
         ],
         side,
         pos,
@@ -846,6 +878,14 @@
         radial_two,
         scratch=[pltpu.VMEM((channels, channels), BF16)],
     )
+    pairs, wide = call(
+        pair_kernel,
+        [b16(NB * atoms, 9 * atoms), f32(channels, NB * atoms)],
+        pos,
+        last,
+        count,
+        radial_two,
+    )
     near, far = swap_both(near, far, "gx")
     h1, near, far = call(feat_y_kernel, [square] * 3, side, h0, near, far, fy)
     table = [pltpu.VMEM((channels, 2 * atoms), BF16)]
@@ -853,44 +893,41 @@
     near, far = swap_both(near, far, "gy")
     sent, h2, h3 = call(feat_z_kernel, [square] * 3, side, h0, h1, near, far, fz)
     hg = call(gather_more_kernel, big, h2, h3, hot, hg, scratch=table, aliases={3: 0})
+    part = call(partial_kernel, f32(9, channels, atoms), hg, rad, ylm)
     h4 = partner(sent)
 
-    hg, energies, dmat, extra, rq, gz = call(
+    energies, raw, extra, gz = call(
         layer_two_kernel,
-        [
-            big,
-            f32(1, atoms),
-            f32(9, channels, atoms),
-            f32(channels, atoms),
-            b16(steps, channels, width),
-            b16(atoms, channels),
-        ],
+        [f32(1, atoms), f32(9, channels, atoms), f32(channels, atoms), b16(atoms, channels)],
         h0,
         h4,
-        hot,
-        hg,
-        rad,
-        ylm,
+        part,
+        pairs,
+        wide,
         occ,
         mix_two,
+        radial_two,
         read_one,
         read_hidden,
         read_out,
-        scratch=[pltpu.VMEM((9, channels, atoms), F32), pltpu.VMEM((atoms, channels), F32)],
-        aliases={3: 0},
-    )
+        scratch=[
+            pltpu.VMEM((channels, NB * atoms), BF16),
+            pltpu.VMEM((channels, 9 * atoms), BF16),
+        ],
+    )
+    rows = f32(2 * atoms, channels)
+    rq, quad = call(reverse_kernel, [b16(steps, channels, width), big], raw, rad, ylm)
+    gy = call(functools.partial(scatter_kernel, 2 * atoms), rows, hot, rq)
+    hg = call(gather_last_kernel, big, h4, hot, hg, aliases={2: 0})
     az = partner(gz)
-    rows = f32(2 * atoms, channels)
 
     def edges(start, count):
         out = f32(4 * count * GROUP, atoms)
         scaled = [pltpu.VMEM((9, channels, atoms), F32)]
         kernel = functools.partial(edge_kernel, start)
-        return call(kernel, out, hg, rad, slo, dmat, unit, scratch=scaled)
-
-    cuts = [0, 2 * (steps // 7), 3 * (steps // 7), steps]
-    gy = call(functools.partial(scatter_kernel, 2 * atoms), rows, hot, rq)
-    ga = edges(cuts[0], cuts[1] - cuts[0])
+        return call(kernel, out, hg, rad, slo, quad, raw, unit, scratch=scaled)
+
+    cut = steps // 7
     acc, near, far = call(
         fold_z_kernel,
         [rows, b16(atoms, channels), b16(atoms, channels)],
@@ -900,7 +937,7 @@
         fz,
     )
     dx = call(functools.partial(scatter_kernel, 0), rows, hot, rq)
-    gb = edges(cuts[1], cuts[2] - cuts[1])
+    gb = edges(0, cut)
     near, far = swap_both(near, far, "gy")
     own, near, far = call(
         fold_y_kernel,
@@ -913,7 +950,7 @@
         far,
         fy,
     )
-    gc = edges(cuts[2], cuts[3] - cuts[2])
+    gc = edges(cut, steps - cut)
     near, far = swap_both(near, far, "gx")
     f0, f1, f2, f3, f4 = call(
         layer_one_reverse_kernel,
@@ -929,7 +966,6 @@
         rinv,
         basis,
         slope,
-        ga,
         gb,
         gc,
         lanes,

time: 71.1 us -> 70.8 us (level)
    ppermute x4, starting transfers between devices: 6.28 us -> 4.53 us  [partner(): lax.ppermute(x, axis, [(i, i ^ 1) for i in range(lax.axis_size(axis))])]
    ppermute x16, starting transfers between devices: 17.4 us -> 19 us  [pair_swap(): return lax.ppermute(x, axis, pairs)]
    ppermute x16, waiting for transfers between devices: 15.1 us -> 14.2 us  [pair_swap(): return lax.ppermute(x, axis, pairs)]
    pallas_call x22 -> x25, Pallas kernels: 25.1 us -> 25.4 us  [call(): pl.pallas_call(kernel, out_shape=shapes, in_specs=specs, out_specs=[pl.Bl...]
  transfers between devices with their start and end apart: 20 -> 20, of which waited for: 14 -> 12; matrix products, arithmetic and copies ran while one was open for 0% -> 0% of each run, Pallas kernels for 15% -> 19%
where the time goes in v4:
time: 70.8 us; the launch traced here: 70.6 us
  Pallas kernels  25.4 us (36%)
  starting transfers between devices  23.5 us (33%)
  waiting for transfers between devices  19.3 us (27%)
  local copies, waits for them, and re-layouts  1.43 us (2%)
  between operations  0.98 us (1%)
    pallas_call x25, Pallas kernels, call(): pl.pallas_call(kernel, out_shape=shapes, in_specs=specs, out_specs=[pl.Bl...  25.4 us
    ppermute x16, starting transfers between devices, pair_swap(): return lax.ppermute(x, axis, pairs)  19 us
    ppermute x16, waiting for transfers between devices, pair_swap(): return lax.ppermute(x, axis, pairs)  14.2 us
    ppermute x4, waiting for transfers between devices, partner(): lax.ppermute(x, axis, [(i, i ^ 1) for i in range(lax.axis_size(axis))])  5.1 us
    ppermute x4, starting transfers between devices, partner(): lax.ppermute(x, axis, [(i, i ^ 1) for i in range(lax.axis_size(axis))])  4.53 us
    unnamed x32, local copies, waits for them, and re-layouts  1.43 us
  transfers between devices with their start and end apart: 20, of which 12 were waited for; matrix products, arithmetic and copies ran while one was open for 0% of the time, Pallas kernels for 19%

profile of v4, /device:TPU:0, one launch (start us, length us, event | category | flops | bytes accessed | tf_op | source)
XLA Modules:
  0.0 70.6 jit_solution(8364263676353146246)
XLA Ops:
  2.2 3.1 %collective-permute-start = (f32[8,128]{1,0:T(8,128)S(1)}, f32[8,128]{1,0:T(8,128)S(1)}, u32[]{:S(2)}, u32[]{:S(2)}) collective-permute-start(f32[8,128]{1,0:T(8,128)S(1)} %get-tuple-element.61), channel_id=1, source_target_pairs={{0,8},{8,0},{16,24},{24,16},{1,9},{9,1},{17,25},{25,17},{2,10},{10... | collective-permute-start | bytes 12296 | tf_op jit(solution)/shard_map/ppermute | solution.py:773
  5.2 2.5 %collective-permute-start.1 = (f32[8,128]{1,0:T(8,128)S(1)}, f32[8,128]{1,0:T(8,128)S(1)}, u32[]{:S(2)}, u32[]{:S(2)}) collective-permute-start(f32[8,128]{1,0:T(8,128)S(1)} %get-tuple-element.61), channel_id=1, source_target_pairs={{0,24},{8,16},{16,8},{24,0},{1,25},{9,17},{17,9},{25,1},{2,26},{10... | collective-permute-start | bytes 12296 | tf_op jit(solution)/shard_map/ppermute | solution.py:773
  7.7 2.9 %collective-permute-done.1.far_ref = f32[8,128]{1,0:T(8,128)S(1)} collective-permute-done((f32[8,128]{1,0:T(8,128)S(1)}, f32[8,128]{1,0:T(8,128)S(1)}, u32[]{:S(2)}, u32[]{:S(2)}) %collective-permute-start.1) | collective-permute-done | bytes 4128 | tf_op jit(solution)/shard_map/ppermute | solution.py:773
  10.8 1.6 %collective-permute-start.3 = (f32[8,128]{1,0:T(8,128)S(1)}, f32[8,128]{1,0:T(8,128)S(1)}, u32[]{:S(2)}, u32[]{:S(2)}) collective-permute-start(f32[8,128]{1,0:T(8,128)S(1)} %get-tuple-element.64), channel_id=1, source_target_pairs={{0,6},{2,4},{4,2},{6,0},{1,7},{3,5},{5,3},{7,1},{8,14},{10,12},{12... | collective-permute-start | bytes 12296 | tf_op jit(solution)/shard_map/ppermute | solution.py:773
  12.4 1.4 %collective-permute-done.3.far_ref = f32[8,128]{1,0:T(8,128)S(1)} collective-permute-done((f32[8,128]{1,0:T(8,128)S(1)}, f32[8,128]{1,0:T(8,128)S(1)}, u32[]{:S(2)}, u32[]{:S(2)}) %collective-permute-start.3) | collective-permute-done | bytes 4128 | tf_op jit(solution)/shard_map/ppermute | solution.py:773
  13.9 1.5 %collective-permute-start.4 = (f32[8,128]{1,0:T(8,128)S(1)}, f32[8,128]{1,0:T(8,128)S(1)}, u32[]{:S(2)}, u32[]{:S(2)}) collective-permute-start(f32[8,128]{1,0:T(8,128)S(1)} %get-tuple-element.67), channel_id=1, source_target_pairs={{0,1},{1,0},{2,3},{3,2},{4,5},{5,4},{6,7},{7,6},{8,9},{9,8},{10,11... | collective-permute-start | bytes 12296 | tf_op jit(solution)/shard_map/ppermute | solution.py:778
  15.5 2.3 %shard_map.159 = (bf16[14,640,512]{2,1,0:T(8,128)(2,1)S(1)}, bf16[14,128,512]{2,1,0:T(8,128)(2,1)S(1)}, f32[128,128]{1,0:T(8,128)S(1)}) custom-call(s32[56,128]{1,0:T(8,128)S(1)} %bitcast.17, s32[56,128]{1,0:T(8,128)S(1)} %bitcast.15), custom_call_target="tpu_custom_call" | custom-call | flops 1000000000 | bytes 1000000 | tf_op jit(solution)/shard_map/pallas_call | solution.py:751
  17.9 1.1 %shard_map.162 = (f32[168,128]{1,0:T(8,128)S(1)}, f32[56,128]{1,0:T(8,128)S(1)}, f32[448,128]{1,0:T(8,128)S(1)}, f32[448,128]{1,0:T(8,128)S(1)}, f32[128,1152]{1...) custom-call(s32[8,128]{1,0:T(8,128)S(1)} %get-tuple-element.58.side_, ...), custom_call_target="tpu_custom_call" | custom-call | flops 1000000000 | bytes 1000000 | tf_op jit(solution)/shard_map/pallas_call | solution.py:751
  19.1 2.5 %collective-permute-start.6 = (bf16[64,128]{1,0:T(8,128)(2,1)S(1)}, bf16[64,128]{1,0:T(8,128)(2,1)S(1)}, u32[]{:S(2)}, u32[]{:S(2)}) collective-permute-start(bf16[64,128]{1,0:T(8,128)(2,1)S(1)} %get-tuple-element.70), channel_id=1, source_target_pairs={{0,24},{8,16},{16,8},{24,0},{1,25},{9,17},{17,9},{25,1},{2,26},{10... | collective-permute-start | bytes 49160 | tf_op jit(solution)/shard_map/ppermute | solution.py:773
  21.6 1.0 %shard_map.169 = (bf16[1024,1152]{1,0:T(8,128)(2,1)S(1)}, f32[128,1024]{1,0:T(8,128)S(1)}) custom-call(f32[8,128]{1,0:T(8,128)S(1)} %get-tuple-element.60.pos_ref, f32[8,128]{1,0:T(8,128)S(1)} %get-tuple-element.82.last_ref, f32[128,128]{1,0:T(8,128)S(1)} %get-tuple-element.83.count_ref, f32[8,128]{1,0:T(8,128)S(1)} %copy-done.5), custom_call_target="tpu_custom_call" | custom-call | flops 1000000000 | bytes 1000000 | tf_op jit(solution)/shard_map/pallas_call | solution.py:751
  22.6 1.2 %shard_map.167 = (f32[14,128,512]{2,1,0:T(8,128)S(1)}, f32[14,128,512]{2,1,0:T(8,128)S(1)}, f32[448,128]{1,0:T(8,128)S(1)}) custom-call(f32[448,128]{1,0:T(8,128)S(1)} %get-tuple-element.77.basis_ref, f32[448,128]{1,0:T(8,128)S(1)} %get-tuple-element.78.slope_ref, f32[168,128]{1,0:T(8,128)S(1)} %get-tuple-element.79.unit_ref, f32[8,128]{1,0:T(8,128)S(1)} %copy-done.5), custom_call_target="tpu_custom_call" | custom-call | flops 1000000000 | bytes 1000000 | tf_op jit(solution)/shard_map/pallas_call | solution.py:751
  23.8 0.9 %collective-permute-done.6.far_ref = bf16[64,128]{1,0:T(8,128)(2,1)S(1)} collective-permute-done((bf16[64,128]{1,0:T(8,128)(2,1)S(1)}, bf16[64,128]{1,0:T(8,128)(2,1)S(1)}, u32[]{:S(2)}, u32[]{:S(2)}) %collective-permute-start.6) | collective-permute-done | bytes 16416 | tf_op jit(solution)/shard_map/ppermute | solution.py:773
  25.0 1.6 %collective-permute-start.8 = (bf16[128,128]{1,0:T(8,128)(2,1)S(1)}, bf16[128,128]{1,0:T(8,128)(2,1)S(1)}, u32[]{:S(2)}, u32[]{:S(2)}) collective-permute-start(bf16[128,128]{1,0:T(8,128)(2,1)S(1)} %get-tuple-element.73), channel_id=1, source_target_pairs={{0,6},{2,4},{4,2},{6,0},{1,7},{3,5},{5,3},{7,1},{8,14},{10,12},{12... | collective-permute-start | bytes 98312 | tf_op jit(solution)/shard_map/ppermute | solution.py:773
  27.2 1.1 %collective-permute-done.8.far_ref = bf16[128,128]{1,0:T(8,128)(2,1)S(1)} collective-permute-done((bf16[128,128]{1,0:T(8,128)(2,1)S(1)}, bf16[128,128]{1,0:T(8,128)(2,1)S(1)}, u32[]{:S(2)}, u32[]{:S(2)}) %collective-permute-start.8) | collective-permute-done | bytes 32800 | tf_op jit(solution)/shard_map/ppermute | solution.py:773
  28.6 1.3 %collective-permute-start.9 = (bf16[128,128]{1,0:T(8,128)(2,1)S(1)}, bf16[128,128]{1,0:T(8,128)(2,1)S(1)}, u32[]{:S(2)}, u32[]{:S(2)}) collective-permute-start(bf16[128,128]{1,0:T(8,128)(2,1)S(1)} %get-tuple-element.74), channel_id=1, source_target_pairs={{0,1},{1,0},{2,3},{3,2},{4,5},{5,4},{6,7},{7,6},{8,9},{9,8},{10,11... | collective-permute-start | bytes 98312 | tf_op jit(solution)/shard_map/ppermute | solution.py:778
  29.9 1.1 %shard_map.166.hg_ref.old_ref = f32[14,128,512]{2,1,0:T(8,128)S(1)} custom-call(bf16[128,128]{1,0:T(8,128)(2,1)S(1)} %get-tuple-element.75.h2_ref, bf16[128,128]{1,0:T(8,128)(2,1)S(1)} %get-tuple-element.76.h3_ref, bf16[14,640,512]{2,1,0:T(8,128)(2,1)S(1)} %get-tuple-element.59.hot_ref, ...), custom_call_target="tpu_custom_call", output_to_operand_aliasing={{}: (3, {})} | custom-call | flops 1000000000 | bytes 1000000 | tf_op jit(solution)/shard_map/pallas_call | solution.py:751
  31.1 2.4 %shard_map.168.acc_ref = f32[9,128,128]{2,1,0:T(8,128)S(1)} custom-call(f32[14,128,512]{2,1,0:T(8,128)S(1)} %shard_map.166.hg_ref.old_ref, f32[14,128,512]{2,1,0:T(8,128)S(1)} %get-tuple-element.80.rad_ref, f32[448,128]{1,0:T(8,128)S(1)} %get-tuple-element.81.y_ref), custom_call_target="tpu_custom_call" | custom-call | flops 1000000000 | bytes 1000000 | tf_op jit(solution)/shard_map/pallas_call | solution.py:751
  33.5 2.0 %shard_map.170 = (f32[1,128]{1,0:T(1,128)S(1)}, f32[9,128,128]{2,1,0:T(8,128)S(1)}, f32[128,128]{1,0:T(8,128)S(1)}, bf16[128,128]{1,0:T(8,128)(2,1)S(1)}) custom-call(bf16[128,128]{1,0:T(8,128)(2,1)S(1)} %get-tuple-element.68.h0_ref, bf16[128,128]{1,0:T(8,128)(2,1)S(1)} %collective-permute-done.9.h4_ref, f32[9,128,128]{2,1,0:T(8,128)S(1)} %shard_map.168.acc_ref, ...), custom_call_target="tpu_custom_call" | custom-call | flops 1000000000 | bytes 1000000 | tf_op jit(solution)/shard_map/pallas_call | solution.py:751
  35.6 2.4 %shard_map.171 = (bf16[14,128,512]{2,1,0:T(8,128)(2,1)S(1)}, f32[14,128,512]{2,1,0:T(8,128)S(1)}) custom-call(f32[9,128,128]{2,1,0:T(8,128)S(1)} %get-tuple-element.86.raw_ref.d_ref, f32[14,128,512]{2,1,0:T(8,128)S(1)} %get-tuple-element.80.rad_ref, f32[448,128]{1,0:T(8,128)S(1)} %get-tuple-element.81.y_ref), custom_call_target="tpu_custom_call" | custom-call | flops 1000000000 | bytes 1000000 | tf_op jit(solution)/shard_map/pallas_call | solution.py:751
  38.0 1.1 %shard_map.174.gx_ref = f32[256,128]{1,0:T(8,128)S(1)} custom-call(bf16[14,640,512]{2,1,0:T(8,128)(2,1)S(1)} %get-tuple-element.59.hot_ref, bf16[14,128,512]{2,1,0:T(8,128)(2,1)S(1)} %get-tuple-element.87.rq_ref), custom_call_target="tpu_custom_call" | custom-call | flops 1000000000 | bytes 1000000 | tf_op jit(solution)/shard_map/pallas_call | solution.py:751
  39.1 1.1 %shard_map.172.gy_ref = f32[256,128]{1,0:T(8,128)S(1)} custom-call(bf16[14,640,512]{2,1,0:T(8,128)(2,1)S(1)} %get-tuple-element.59.hot_ref, bf16[14,128,512]{2,1,0:T(8,128)(2,1)S(1)} %get-tuple-element.87.rq_ref), custom_call_target="tpu_custom_call" | custom-call | flops 1000000000 | bytes 1000000 | tf_op jit(solution)/shard_map/pallas_call | solution.py:751
  41.9 2.3 %collective-permute-done.10.az_ref = bf16[128,128]{1,0:T(8,128)(2,1)S(1)} collective-permute-done((bf16[128,128]{1,0:T(8,128)(2,1)S(1)}, bf16[128,128]{1,0:T(8,128)(2,1)S(1)}, u32[]{:S(2)}, u32[]{:S(2)}) %collective-permute-start.10) | collective-permute-done | bytes 32800 | tf_op jit(solution)/shard_map/ppermute | solution.py:778
  44.4 1.6 %collective-permute-start.12 = (bf16[128,128]{1,0:T(8,128)(2,1)S(1)}, bf16[128,128]{1,0:T(8,128)(2,1)S(1)}, u32[]{:S(2)}, u32[]{:S(2)}) collective-permute-start(bf16[128,128]{1,0:T(8,128)(2,1)S(1)} %get-tuple-element.92), channel_id=1, source_target_pairs={{0,6},{2,4},{4,2},{6,0},{1,7},{3,5},{5,3},{7,1},{8,14},{10,12},{12... | collective-permute-start | bytes 98312 | tf_op jit(solution)/shard_map/ppermute | solution.py:773
  46.0 3.6 %shard_map.178.gc_ref = f32[192,128]{1,0:T(8,128)S(1)} custom-call(f32[14,128,512]{2,1,0:T(8,128)S(1)} %shard_map.176.hg_ref, f32[14,128,512]{2,1,0:T(8,128)S(1)} %get-tuple-element.80.rad_ref, f32[14,128,512]{2,1,0:T(8,128)S(1)} %get-tuple-element.98.slo_ref, f32[14,128,512]{2,1,0:T(8,128)S(1)} %get-tuple-element.99.q_ref, ...), custom_call_target="tpu_custom_call" | custom-call | flops 1000000000 | bytes 1000000 | tf_op jit(solution)/shard_map/pallas_call | solution.py:751
  50.1 2.5 %collective-permute-start.14 = (bf16[64,128]{1,0:T(8,128)(2,1)S(1)}, bf16[64,128]{1,0:T(8,128)(2,1)S(1)}, u32[]{:S(2)}, u32[]{:S(2)}) collective-permute-start(bf16[64,128]{1,0:T(8,128)(2,1)S(1)} %get-tuple-element.95), channel_id=1, source_target_pairs={{0,24},{8,16},{16,8},{24,0},{1,25},{9,17},{17,9},{25,1},{2,26},{10... | collective-permute-start | bytes 49160 | tf_op jit(solution)/shard_map/ppermute | solution.py:773
  53.7 2.0 %collective-permute-done.14.far_ref = bf16[64,128]{1,0:T(8,128)(2,1)S(1)} collective-permute-done((bf16[64,128]{1,0:T(8,128)(2,1)S(1)}, bf16[64,128]{1,0:T(8,128)(2,1)S(1)}, u32[]{:S(2)}, u32[]{:S(2)}) %collective-permute-start.14) | collective-permute-done | bytes 16416 | tf_op jit(solution)/shard_map/ppermute | solution.py:773
  55.6 1.6 %shard_map.179 = (f32[8,128]{1,0:T(8,128)S(1)}, f32[8,128]{1,0:T(8,128)S(1)}, f32[8,128]{1,0:T(8,128)S(1)}, f32[8,128]{1,0:T(8,128)S(1)}, f32[8,128]{1,0:T(8,128)S(1)}) custom-call(s32[8,128]{1,0:T(8,128)S(1)} %get-tuple-element.58.side_ref, f32[128,128]{1,0:T(8,128)S(1)} %get-tuple-element.93.own_ref, bf16[64,128]{1,0:T(8,128)(2,1)S(1)} %collective-permute-done.13.near_ref, ...), custom_call_target="tpu_custom_call" | custom-call | flops 1000000000 | bytes 1000000 | tf_op jit(solution)/shard_map/pallas_call | solution.py:751
  58.0 2.8 %collective-permute-done.15.az_ref = f32[8,128]{1,0:T(8,128)S(1)} collective-permute-done((f32[8,128]{1,0:T(8,128)S(1)}, f32[8,128]{1,0:T(8,128)S(1)}, u32[]{:S(2)}, u32[]{:S(2)}) %collective-permute-start.15) | collective-permute-done | bytes 4128 | tf_op jit(solution)/shard_map/ppermute | solution.py:778
  62.2 1.9 %collective-permute-done.17.far_ref = f32[8,128]{1,0:T(8,128)S(1)} collective-permute-done((f32[8,128]{1,0:T(8,128)S(1)}, f32[8,128]{1,0:T(8,128)S(1)}, u32[]{:S(2)}, u32[]{:S(2)}) %collective-permute-start.17) | collective-permute-done | bytes 4128 | tf_op jit(solution)/shard_map/ppermute | solution.py:773
  64.4 2.5 %collective-permute-start.19 = (f32[8,128]{1,0:T(8,128)S(1)}, f32[8,128]{1,0:T(8,128)S(1)}, u32[]{:S(2)}, u32[]{:S(2)}) collective-permute-start(f32[8,128]{1,0:T(8,128)S(1)} %get-tuple-element.110), channel_id=1, source_target_pairs={{0,24},{8,16},{16,8},{24,0},{1,25},{9,17},{17,9},{25,1},{2,26},{10... | collective-permute-start | bytes 12296 | tf_op jit(solution)/shard_map/ppermute | solution.py:773
  66.9 1.1 %collective-permute-done.18.near_ref = f32[8,128]{1,0:T(8,128)S(1)} collective-permute-done((f32[8,128]{1,0:T(8,128)S(1)}, f32[8,128]{1,0:T(8,128)S(1)}, u32[]{:S(2)}, u32[]{:S(2)}) %collective-permute-start.18) | collective-permute-done | bytes 4128 | tf_op jit(solution)/shard_map/ppermute | solution.py:773
  68.0 1.9 %collective-permute-done.19.far_ref = f32[8,128]{1,0:T(8,128)S(1)} collective-permute-done((f32[8,128]{1,0:T(8,128)S(1)}, f32[8,128]{1,0:T(8,128)S(1)}, u32[]{:S(2)}, u32[]{:S(2)}) %collective-permute-start.19) | collective-permute-done | bytes 4128 | tf_op jit(solution)/shard_map/ppermute | solution.py:773
  (65 shorter events, 9.7 us)
Async XLA Ops:
  0.6 10.0 %copy-start.8 = (s32[1,1,1,2,128]{4,3,2,1,0:T(2,128)S(1)}, s32[1,1,1,2,128]{4,3,2,1,0:T(2,128)}, u32[]{:S(2)}) copy-start(s32[1,1,1,2,128]{4,3,2,1,0:T(2,128)} %param.20) | copy-start | bytes 3076
  2.0 11.8 %copy-start.15 = (s32[1,1,1,128]{3,2,1,0:T(1,128)S(1)}, s32[1,1,1,128]{3,2,1,0:T(1,128)}, u32[]{:S(2)}) copy-start(s32[1,1,1,128]{3,2,1,0:T(1,128)} %param.21) | copy-start | bytes 1540
  2.2 5.5 %collective-permute-start = (f32[8,128]{1,0:T(8,128)S(1)}, f32[8,128]{1,0:T(8,128)S(1)}, u32[]{:S(2)}, u32[]{:S(2)}) collective-permute-start(f32[8,128]{1,0:T(8,128)S(1)} %get-tuple-element.61), channel_id=1, source_target_pairs={{0,8},{8,0},{16,24},{24,16},{1,9},{9,1},{17,25},{25,17},{2,10},{10... | collective-permute-start | bytes 12296 | tf_op jit(solution)/shard_map/ppermute | solution.py:773
  5.2 5.4 %collective-permute-start.1 = (f32[8,128]{1,0:T(8,128)S(1)}, f32[8,128]{1,0:T(8,128)S(1)}, u32[]{:S(2)}, u32[]{:S(2)}) collective-permute-start(f32[8,128]{1,0:T(8,128)S(1)} %get-tuple-element.61), channel_id=1, source_target_pairs={{0,24},{8,16},{16,8},{24,0},{1,25},{9,17},{17,9},{25,1},{2,26},{10... | collective-permute-start | bytes 12296 | tf_op jit(solution)/shard_map/ppermute | solution.py:773
  10.6 4.8 %copy-start.2 = (s32[56,1,1,1,128]{4,3,2,1,0:T(1,128)S(1)}, s32[56,1,1,1,128]{4,3,2,1,0:T(1,128)}, u32[]{:S(2)}) copy-start(s32[56,1,1,1,128]{4,3,2,1,0:T(1,128)} %param.18) | copy-start | bytes 86020
  10.6 4.8 %copy-start.3 = (s32[56,1,1,1,128]{4,3,2,1,0:T(1,128)S(1)}, s32[56,1,1,1,128]{4,3,2,1,0:T(1,128)}, u32[]{:S(2)}) copy-start(s32[56,1,1,1,128]{4,3,2,1,0:T(1,128)} %param.17) | copy-start | bytes 86020
  10.8 1.6 %collective-permute-start.2 = (f32[8,128]{1,0:T(8,128)S(1)}, f32[8,128]{1,0:T(8,128)S(1)}, u32[]{:S(2)}, u32[]{:S(2)}) collective-permute-start(f32[8,128]{1,0:T(8,128)S(1)} %get-tuple-element.63), channel_id=1, source_target_pairs={{0,2},{2,0},{4,6},{6,4},{1,3},{3,1},{5,7},{7,5},{8,10},{10,8},{12,... | collective-permute-start | bytes 12296 | tf_op jit(solution)/shard_map/ppermute | solution.py:773
  10.8 3.1 %collective-permute-start.3 = (f32[8,128]{1,0:T(8,128)S(1)}, f32[8,128]{1,0:T(8,128)S(1)}, u32[]{:S(2)}, u32[]{:S(2)}) collective-permute-start(f32[8,128]{1,0:T(8,128)S(1)} %get-tuple-element.64), channel_id=1, source_target_pairs={{0,6},{2,4},{4,2},{6,0},{1,7},{3,5},{5,3},{7,1},{8,14},{10,12},{12... | collective-permute-start | bytes 12296 | tf_op jit(solution)/shard_map/ppermute | solution.py:773
  13.8 4.0 %copy-start.1 = (bf16[384,128]{1,0:T(8,128)(2,1)S(1)}, bf16[384,128]{1,0:T(8,128)(2,1)}, u32[]{:S(2)}) copy-start(bf16[384,128]{1,0:T(8,128)(2,1)} %mix_ref.5) | copy-start | bytes 294916
  13.8 4.0 %copy-start.6 = (f32[8,128]{1,0:T(8,128)S(1)}, f32[8,128]{1,0:T(8,128)}, u32[]{:S(2)}) copy-start(f32[8,128]{1,0:T(8,128)} %radial_ref.9) | copy-start | bytes 12292
  13.8 4.0 %copy-start.10 = (s32[1,1,1,2,64]{4,3,2,1,0:T(2,128)S(1)}, s32[1,1,1,2,64]{4,3,2,1,0:T(2,128)}, u32[]{:S(2)}) copy-start(s32[1,1,1,2,64]{4,3,2,1,0:T(2,128)} %param.19) | copy-start | bytes 1540
  13.8 4.0 %copy-start.11 = (f32[128]{0:T(128)S(1)}, f32[128]{0:T(128)}, u32[]{:S(2)}) copy-start(f32[128]{0:T(128)} %param.24) | copy-start | bytes 1540
  13.9 3.9 %collective-permute-start.4 = (f32[8,128]{1,0:T(8,128)S(1)}, f32[8,128]{1,0:T(8,128)S(1)}, u32[]{:S(2)}, u32[]{:S(2)}) collective-permute-start(f32[8,128]{1,0:T(8,128)S(1)} %get-tuple-element.67), channel_id=1, source_target_pairs={{0,1},{1,0},{2,3},{3,2},{4,5},{5,4},{6,7},{7,6},{8,9},{9,8},{10,11... | collective-permute-start | bytes 12296 | tf_op jit(solution)/shard_map/ppermute | solution.py:778
  15.5 6.1 %copy-start.5 = (f32[8,128]{1,0:T(8,128)S(1)}, f32[8,128]{1,0:T(8,128)}, u32[]{:S(2)}) copy-start(f32[8,128]{1,0:T(8,128)} %radial_ref.8) | copy-start | bytes 12292
  19.0 4.8 %collective-permute-start.5 = (bf16[64,128]{1,0:T(8,128)(2,1)S(1)}, bf16[64,128]{1,0:T(8,128)(2,1)S(1)}, u32[]{:S(2)}, u32[]{:S(2)}) collective-permute-start(bf16[64,128]{1,0:T(8,128)(2,1)S(1)} %get-tuple-element.69), channel_id=1, source_target_pairs={{0,8},{8,0},{16,24},{24,16},{1,9},{9,1},{17,25},{25,17},{2,10},{10... | collective-permute-start | bytes 49160 | tf_op jit(solution)/shard_map/ppermute | solution.py:773
  19.1 5.6 %collective-permute-start.6 = (bf16[64,128]{1,0:T(8,128)(2,1)S(1)}, bf16[64,128]{1,0:T(8,128)(2,1)S(1)}, u32[]{:S(2)}, u32[]{:S(2)}) collective-permute-start(bf16[64,128]{1,0:T(8,128)(2,1)S(1)} %get-tuple-element.70), channel_id=1, source_target_pairs={{0,24},{8,16},{16,8},{24,0},{1,25},{9,17},{17,9},{25,1},{2,26},{10... | collective-permute-start | bytes 49160 | tf_op jit(solution)/shard_map/ppermute | solution.py:773
  24.9 2.3 %collective-permute-start.7 = (bf16[128,128]{1,0:T(8,128)(2,1)S(1)}, bf16[128,128]{1,0:T(8,128)(2,1)S(1)}, u32[]{:S(2)}, u32[]{:S(2)}) collective-permute-start(bf16[128,128]{1,0:T(8,128)(2,1)S(1)} %get-tuple-element.72), channel_id=1, source_target_pairs={{0,2},{2,0},{4,6},{6,4},{1,3},{3,1},{5,7},{7,5},{8,10},{10,8},{12,... | collective-permute-start | bytes 98312 | tf_op jit(solution)/shard_map/ppermute | solution.py:773
  25.0 3.4 %collective-permute-start.8 = (bf16[128,128]{1,0:T(8,128)(2,1)S(1)}, bf16[128,128]{1,0:T(8,128)(2,1)S(1)}, u32[]{:S(2)}, u32[]{:S(2)}) collective-permute-start(bf16[128,128]{1,0:T(8,128)(2,1)S(1)} %get-tuple-element.73), channel_id=1, source_target_pairs={{0,6},{2,4},{4,2},{6,0},{1,7},{3,5},{5,3},{7,1},{8,14},{10,12},{12... | collective-permute-start | bytes 98312 | tf_op jit(solution)/shard_map/ppermute | solution.py:773
  28.6 4.9 %collective-permute-start.9 = (bf16[128,128]{1,0:T(8,128)(2,1)S(1)}, bf16[128,128]{1,0:T(8,128)(2,1)S(1)}, u32[]{:S(2)}, u32[]{:S(2)}) collective-permute-start(bf16[128,128]{1,0:T(8,128)(2,1)S(1)} %get-tuple-element.74), channel_id=1, source_target_pairs={{0,1},{1,0},{2,3},{3,2},{4,5},{5,4},{6,7},{7,6},{8,9},{9,8},{10,11... | collective-permute-start | bytes 98312 | tf_op jit(solution)/shard_map/ppermute | solution.py:778
  31.0 2.5 %copy-start = (bf16[384,128]{1,0:T(8,128)(2,1)S(1)}, bf16[384,128]{1,0:T(8,128)(2,1)}, u32[]{:S(2)}) copy-start(bf16[384,128]{1,0:T(8,128)(2,1)} %mix_ref.4) | copy-start | bytes 294916
  31.0 2.5 %copy-start.4 = (f32[128,16]{0,1:T(8,128)S(1)}, f32[128,16]{0,1:T(8,128)}, u32[]{:S(2)}) copy-start(f32[128,16]{0,1:T(8,128)} %param.28) | copy-start | bytes 24580
  31.0 2.5 %copy-start.12 = (s32[1,1,1,128]{3,2,1,0:T(1,128)S(1)}, s32[1,1,1,128]{3,2,1,0:T(1,128)}, u32[]{:S(2)}) copy-start(s32[1,1,1,128]{3,2,1,0:T(1,128)} %param.16) | copy-start | bytes 1540
  40.2 4.0 %collective-permute-start.10 = (bf16[128,128]{1,0:T(8,128)(2,1)S(1)}, bf16[128,128]{1,0:T(8,128)(2,1)S(1)}, u32[]{:S(2)}, u32[]{:S(2)}) collective-permute-start(bf16[128,128]{1,0:T(8,128)(2,1)S(1)} %get-tuple-element.88), channel_id=1, source_target_pairs={{0,1},{1,0},{2,3},{3,2},{4,5},{5,4},{6,7},{7,6},{8,9},{9,8},{10,11... | collective-permute-start | bytes 98312 | tf_op jit(solution)/shard_map/ppermute | solution.py:778
  44.3 5.3 %collective-permute-start.11 = (bf16[128,128]{1,0:T(8,128)(2,1)S(1)}, bf16[128,128]{1,0:T(8,128)(2,1)S(1)}, u32[]{:S(2)}, u32[]{:S(2)}) collective-permute-start(bf16[128,128]{1,0:T(8,128)(2,1)S(1)} %get-tuple-element.91), channel_id=1, source_target_pairs={{0,2},{2,0},{4,6},{6,4},{1,3},{3,1},{5,7},{7,5},{8,10},{10,8},{12,... | collective-permute-start | bytes 98312 | tf_op jit(solution)/shard_map/ppermute | solution.py:773
  44.4 5.2 %collective-permute-start.12 = (bf16[128,128]{1,0:T(8,128)(2,1)S(1)}, bf16[128,128]{1,0:T(8,128)(2,1)S(1)}, u32[]{:S(2)}, u32[]{:S(2)}) collective-permute-start(bf16[128,128]{1,0:T(8,128)(2,1)S(1)} %get-tuple-element.92), channel_id=1, source_target_pairs={{0,6},{2,4},{4,2},{6,0},{1,7},{3,5},{5,3},{7,1},{8,14},{10,12},{12... | collective-permute-start | bytes 98312 | tf_op jit(solution)/shard_map/ppermute | solution.py:773
  49.9 3.8 %collective-permute-start.13 = (bf16[64,128]{1,0:T(8,128)(2,1)S(1)}, bf16[64,128]{1,0:T(8,128)(2,1)S(1)}, u32[]{:S(2)}, u32[]{:S(2)}) collective-permute-start(bf16[64,128]{1,0:T(8,128)(2,1)S(1)} %get-tuple-element.94), channel_id=1, source_target_pairs={{0,8},{8,0},{16,24},{24,16},{1,9},{9,1},{17,25},{25,17},{2,10},{10... | collective-permute-start | bytes 49160 | tf_op jit(solution)/shard_map/ppermute | solution.py:773
  50.1 5.5 %collective-permute-start.14 = (bf16[64,128]{1,0:T(8,128)(2,1)S(1)}, bf16[64,128]{1,0:T(8,128)(2,1)S(1)}, u32[]{:S(2)}, u32[]{:S(2)}) collective-permute-start(bf16[64,128]{1,0:T(8,128)(2,1)S(1)} %get-tuple-element.95), channel_id=1, source_target_pairs={{0,24},{8,16},{16,8},{24,0},{1,25},{9,17},{17,9},{25,1},{2,26},{10... | collective-permute-start | bytes 49160 | tf_op jit(solution)/shard_map/ppermute | solution.py:773
  57.2 3.7 %collective-permute-start.15 = (f32[8,128]{1,0:T(8,128)S(1)}, f32[8,128]{1,0:T(8,128)S(1)}, u32[]{:S(2)}, u32[]{:S(2)}) collective-permute-start(f32[8,128]{1,0:T(8,128)S(1)} %get-tuple-element.105), channel_id=1, source_target_pairs={{0,1},{1,0},{2,3},{3,2},{4,5},{5,4},{6,7},{7,6},{8,9},{9,8},{10,11... | collective-permute-start | bytes 12296 | tf_op jit(solution)/shard_map/ppermute | solution.py:778
  61.0 1.2 %collective-permute-start.16 = (f32[8,128]{1,0:T(8,128)S(1)}, f32[8,128]{1,0:T(8,128)S(1)}, u32[]{:S(2)}, u32[]{:S(2)}) collective-permute-start(f32[8,128]{1,0:T(8,128)S(1)} %get-tuple-element.107), channel_id=1, source_target_pairs={{0,2},{2,0},{4,6},{6,4},{1,3},{3,1},{5,7},{7,5},{8,10},{10,8},{12,... | collective-permute-start | bytes 12296 | tf_op jit(solution)/shard_map/ppermute | solution.py:773
  61.0 3.1 %collective-permute-start.17 = (f32[8,128]{1,0:T(8,128)S(1)}, f32[8,128]{1,0:T(8,128)S(1)}, u32[]{:S(2)}, u32[]{:S(2)}) collective-permute-start(f32[8,128]{1,0:T(8,128)S(1)} %get-tuple-element.108), channel_id=1, source_target_pairs={{0,6},{2,4},{4,2},{6,0},{1,7},{3,5},{5,3},{7,1},{8,14},{10,12},{12... | collective-permute-start | bytes 12296 | tf_op jit(solution)/shard_map/ppermute | solution.py:773
  64.3 3.6 %collective-permute-start.18 = (f32[8,128]{1,0:T(8,128)S(1)}, f32[8,128]{1,0:T(8,128)S(1)}, u32[]{:S(2)}, u32[]{:S(2)}) collective-permute-start(f32[8,128]{1,0:T(8,128)S(1)} %get-tuple-element.110), channel_id=1, source_target_pairs={{0,8},{8,0},{16,24},{24,16},{1,9},{9,1},{17,25},{25,17},{2,10},{10... | collective-permute-start | bytes 12296 | tf_op jit(solution)/shard_map/ppermute | solution.py:773
  64.4 5.4 %collective-permute-start.19 = (f32[8,128]{1,0:T(8,128)S(1)}, f32[8,128]{1,0:T(8,128)S(1)}, u32[]{:S(2)}, u32[]{:S(2)}) collective-permute-start(f32[8,128]{1,0:T(8,128)S(1)} %get-tuple-element.110), channel_id=1, source_target_pairs={{0,24},{8,16},{16,8},{24,0},{1,25},{9,17},{17,9},{25,1},{2,26},{10... | collective-permute-start | bytes 12296 | tf_op jit(solution)/shard_map/ppermute | solution.py:773
  (4 other events, 6.3 us)

commit v5 on v4

--- a/solution.py
+++ b/solution.py
@@ -105,11 +105,14 @@
     return jnp.where(ids == axis, amount, 0.0)
 
 
-def pos_x_kernel(pos_ref, fx_ref, side_ref, coords_ref, send_ref):
+def side_kernel(side_ref):
     ids = lax.broadcasted_iota(jnp.int32, side_ref.shape, 0)
     first, second = lax.axis_index("gx") % 2, lax.axis_index("gy") % 2
     value = jnp.where(ids == 0, first, jnp.where(ids == 1, second, lax.axis_index("gz")))
     side_ref[...] = value
+
+
+def pos_x_kernel(side_ref, pos_ref, fx_ref, coords_ref, send_ref):
     rows = [pos_ref[i] for i in range(3)]
     coords = jnp.concatenate(rows + [jnp.zeros_like(rows[0])] * 5, axis=0)
     coords_ref[...] = coords
@@ -209,11 +212,21 @@
     to_near_ref[...], to_far_ref[...] = pack_halves(both)
 
 
+def sine_cosine(turn):
+    angle = (turn - 0.5) * math.pi
+    sq = angle * angle
+    even = jnp.full_like(sq, 1.0 / math.factorial(12))
+    odd = jnp.full_like(sq, 1.0 / math.factorial(13))
+    for order in range(5, -1, -1):
+        sign = 1.0 if order % 2 == 0 else -1.0
+        even = even * sq + sign / math.factorial(2 * order)
+        odd = odd * sq + sign / math.factorial(2 * order + 1)
+    return even, -(angle * odd)
+
+
 def radial_parts(dist, rinv, weight, with_slope):
     scaled = jnp.minimum(dist * (1.0 / CUTOFF), 1.0)
-    phase = scaled * math.pi
-    sine = jnp.sin(phase)
-    cosine = jnp.cos(phase)
+    sine, cosine = sine_cosine(scaled)
     inner = 1.0 - scaled * scaled
     weight = weight * (2.0 / CUTOFF) ** 0.5
     env = weight * inner * inner * rinv
@@ -384,12 +397,6 @@
     for step in range(hot_ref.shape[0]):
         more = dot(table_ref[...], hot_ref[step, 2 * atoms : 4 * atoms, :])
         hg_ref[step] = old_ref[step] + more
-
-
-def gather_last_kernel(h4_ref, hot_ref, old_ref, hg_ref):
-    atoms = h4_ref.shape[1]
-    for step in range(hot_ref.shape[0]):
-        hg_ref[step] = old_ref[step] + dot(h4_ref[...], hot_ref[step, 4 * atoms :, :])
 
 
 def partial_kernel(hg_ref, rad_ref, y_ref, acc_ref):
@@ -486,7 +493,7 @@
     gz_ref[...] = total.astype(BF16)
 
 
-def reverse_kernel(raw_ref, rad_ref, y_ref, rq_ref, q_ref):
+def reverse_kernel(raw_ref, rad_ref, y_ref, hot_ref, rq_ref, q_ref, gy_ref):
     steps, channels, width = rad_ref.shape
     atoms = width // GROUP
     entries = steps * GROUP
@@ -512,12 +519,24 @@
                 value = jnp.concatenate(parts, axis=0).astype(BF16)
                 rq_ref[step, pair * 16 : pair * 16 + 16, cols] = value
 
+    def scatter(step):
+        parts = []
+        for at in (step, step + 1):
+            parts.append(dot(hot_ref[at, 2 * atoms : 4 * atoms, :], rq_ref[at], 1, 1))
+        return parts[0] + parts[1]
+
+    gy_ref[...] = jnp.zeros_like(gy_ref)
+    reverse(0)
+    reverse(1)
+
     def body(trip, carry):
+        gy_ref[...] += scatter(2 * trip)
         for part in range(2):
-            reverse(2 * trip + part)
+            reverse(2 * trip + 2 + part)
         return carry
 
-    lax.fori_loop(0, steps // 2, body, 0)
+    lax.fori_loop(0, steps // 2 - 1, body, 0)
+    gy_ref[...] += scatter(steps - 2)
 
 
 def scatter_kernel(first, hot_ref, rq_ref, out_ref):
@@ -529,9 +548,23 @@
     out_ref[...] = total
 
 
-def edge_kernel(start, hg_ref, rad_ref, slo_ref, q_ref, d_ref, unit_ref, grad_ref, dd_ref):
+def edge_kernel(
+    start,
+    h4_ref,
+    hot_ref,
+    old_ref,
+    rad_ref,
+    slo_ref,
+    q_ref,
+    d_ref,
+    unit_ref,
+    grad_ref,
+    dd_ref,
+    hg_ref,
+):
     channels, atoms = d_ref.shape[1:]
-    entries = hg_ref.shape[0] * GROUP
+    steps = old_ref.shape[0]
+    entries = steps * GROUP
     count = grad_ref.shape[0] // (4 * GROUP)
     for m in range(1, 9):
         if m < 4:
@@ -539,7 +572,10 @@
         else:
             dd_ref[m] = (3.0 * ROOT5 if m == 6 else ROOT15) * d_ref[m]
 
-    def body(step, carry):
+    def prepare(step, slot):
+        hg_ref[slot] = old_ref[step] + dot(h4_ref[...], hot_ref[step, 4 * atoms :, :])
+
+    def edges(step, slot):
         first = step * GROUP
         units = []
         for jj in range(GROUP):
@@ -550,7 +586,7 @@
             d = [None] + [dd_ref[m, rows, :] for m in range(1, 9)]
             for jj in range(GROUP):
                 cols = slice(jj * atoms, (jj + 1) * atoms)
-                hg = hg_ref[step, rows, cols]
+                hg = hg_ref[slot, rows, cols]
                 vx, vy, vz = units[jj]
                 msg = hg * rad_ref[step, rows, cols]
                 parts = [
@@ -566,9 +602,19 @@
             for i in range(4):
                 row = pl.ds(i * count * GROUP + first - start * GROUP + jj, 1)
                 grad_ref[row, :] = jnp.sum(sums[jj][i], axis=0, keepdims=True)
+
+    prepare(start, 0)
+    prepare(start + 1, 1)
+
+    def body(trip, carry):
+        step = start + 2 * trip
+        for part in range(2):
+            edges(step + part, part)
+        for part in range(2):
+            prepare(jnp.minimum(step + 2 + part, steps - 1), part)
         return carry
 
-    lax.fori_loop(start, start + count, body, 0)
+    lax.fori_loop(0, count // 2, body, 0)
 
 
 def fold_z_kernel(side_ref, gy_ref, az_ref, fz_ref, acc_ref, to_near_ref, to_far_ref):
@@ -824,7 +870,8 @@
 
     small = f32(8, atoms)
     side = jax.ShapeDtypeStruct((8, atoms), jnp.int32)
-    side, pos, sent = call(pos_x_kernel, [side, small, small], pos, fx)
+    side = call(side_kernel, side)
+    pos, sent = call(pos_x_kernel, [small, small], side, pos, fx)
     steps = entries // GROUP
     width = GROUP * atoms
     hot, lanes, count = call(
@@ -916,16 +963,16 @@
         ],
     )
     rows = f32(2 * atoms, channels)
-    rq, quad = call(reverse_kernel, [b16(steps, channels, width), big], raw, rad, ylm)
-    gy = call(functools.partial(scatter_kernel, 2 * atoms), rows, hot, rq)
-    hg = call(gather_last_kernel, big, h4, hot, hg, aliases={2: 0})
+    rq, quad, gy = call(
+        reverse_kernel, [b16(steps, channels, width), big, rows], raw, rad, ylm, hot
+    )
     az = partner(gz)
 
     def edges(start, count):
         out = f32(4 * count * GROUP, atoms)
-        scaled = [pltpu.VMEM((9, channels, atoms), F32)]
+        room = [pltpu.VMEM((9, channels, atoms), F32), pltpu.VMEM((2, channels, width), F32)]
         kernel = functools.partial(edge_kernel, start)
-        return call(kernel, out, hg, rad, slo, quad, raw, unit, scratch=scaled)
+        return call(kernel, out, h4, hot, hg, rad, slo, quad, raw, unit, scratch=room)
 
     cut = steps // 7
     acc, near, far = call(

time: 70.8 us -> 69.3 us (0.979)
  local copies, waits for them, and re-layouts: 1.43 us -> 0.7 us
    unnamed x32 -> x30, local copies, waits for them, and re-layouts: 1.43 us -> 0.7 us
    pallas_call x25 -> x24, Pallas kernels: 25.4 us -> 24.9 us  [call(): pl.pallas_call(kernel, out_shape=shapes, in_specs=specs, out_specs=[pl.Bl...]
  transfers between devices with their start and end apart: 20 -> 20, of which waited for: 12 -> 12; matrix products, arithmetic and copies ran while one was open for 0% -> 0% of each run, Pallas kernels for 19% -> 21%
where the time goes in v5:
time: 69.3 us; the launch traced here: 69.2 us
  Pallas kernels  24.9 us (36%)
  starting transfers between devices  23.5 us (34%)
  waiting for transfers between devices  19.1 us (28%)
  between operations  0.98 us (1%)
  local copies, waits for them, and re-layouts  0.7 us (1%)
    pallas_call x24, Pallas kernels, call(): pl.pallas_call(kernel, out_shape=shapes, in_specs=specs, out_specs=[pl.Bl...  24.9 us
    ppermute x16, starting transfers between devices, pair_swap(): return lax.ppermute(x, axis, pairs)  19 us
    ppermute x16, waiting for transfers between devices, pair_swap(): return lax.ppermute(x, axis, pairs)  14.2 us
    ppermute x4, waiting for transfers between devices, partner(): lax.ppermute(x, axis, [(i, i ^ 1) for i in range(lax.axis_size(axis))])  4.83 us
    ppermute x4, starting transfers between devices, partner(): lax.ppermute(x, axis, [(i, i ^ 1) for i in range(lax.axis_size(axis))])  4.55 us
  transfers between devices with their start and end apart: 20, of which 12 were waited for; matrix products, arithmetic and copies ran while one was open for 0% of the time, Pallas kernels for 21%

profile of v5, /device:TPU:0, one launch (start us, length us, event | category | flops | bytes accessed | tf_op | source)
XLA Modules:
  0.0 69.2 jit_solution(2795624217094738890)
XLA Ops:
  1.5 3.1 %collective-permute-start = (f32[8,128]{1,0:T(8,128)S(1)}, f32[8,128]{1,0:T(8,128)S(1)}, u32[]{:S(2)}, u32[]{:S(2)}) collective-permute-start(f32[8,128]{1,0:T(8,128)S(1)} %get-tuple-element.59), channel_id=1, source_target_pairs={{0,8},{8,0},{16,24},{24,16},{1,9},{9,1},{17,25},{25,17},{2,10},{10... | collective-permute-start | bytes 12296 | tf_op jit(solution)/shard_map/ppermute | solution.py:819
  4.5 2.5 %collective-permute-start.1 = (f32[8,128]{1,0:T(8,128)S(1)}, f32[8,128]{1,0:T(8,128)S(1)}, u32[]{:S(2)}, u32[]{:S(2)}) collective-permute-start(f32[8,128]{1,0:T(8,128)S(1)} %get-tuple-element.59), channel_id=1, source_target_pairs={{0,24},{8,16},{16,8},{24,0},{1,25},{9,17},{17,9},{25,1},{2,26},{10... | collective-permute-start | bytes 12296 | tf_op jit(solution)/shard_map/ppermute | solution.py:819
  7.0 2.9 %collective-permute-done.1.far_ref = f32[8,128]{1,0:T(8,128)S(1)} collective-permute-done((f32[8,128]{1,0:T(8,128)S(1)}, f32[8,128]{1,0:T(8,128)S(1)}, u32[]{:S(2)}, u32[]{:S(2)}) %collective-permute-start.1) | collective-permute-done | bytes 4128 | tf_op jit(solution)/shard_map/ppermute | solution.py:819
  10.1 1.6 %collective-permute-start.3 = (f32[8,128]{1,0:T(8,128)S(1)}, f32[8,128]{1,0:T(8,128)S(1)}, u32[]{:S(2)}, u32[]{:S(2)}) collective-permute-start(f32[8,128]{1,0:T(8,128)S(1)} %get-tuple-element.62), channel_id=1, source_target_pairs={{0,6},{2,4},{4,2},{6,0},{1,7},{3,5},{5,3},{7,1},{8,14},{10,12},{12... | collective-permute-start | bytes 12296 | tf_op jit(solution)/shard_map/ppermute | solution.py:819
  11.7 1.4 %collective-permute-done.3.far_ref = f32[8,128]{1,0:T(8,128)S(1)} collective-permute-done((f32[8,128]{1,0:T(8,128)S(1)}, f32[8,128]{1,0:T(8,128)S(1)}, u32[]{:S(2)}, u32[]{:S(2)}) %collective-permute-start.3) | collective-permute-done | bytes 4128 | tf_op jit(solution)/shard_map/ppermute | solution.py:819
  13.2 1.5 %collective-permute-start.4 = (f32[8,128]{1,0:T(8,128)S(1)}, f32[8,128]{1,0:T(8,128)S(1)}, u32[]{:S(2)}, u32[]{:S(2)}) collective-permute-start(f32[8,128]{1,0:T(8,128)S(1)} %get-tuple-element.65), channel_id=1, source_target_pairs={{0,1},{1,0},{2,3},{3,2},{4,5},{5,4},{6,7},{7,6},{8,9},{9,8},{10,11... | collective-permute-start | bytes 12296 | tf_op jit(solution)/shard_map/ppermute | solution.py:824
  14.8 2.3 %shard_map.165 = (bf16[14,640,512]{2,1,0:T(8,128)(2,1)S(1)}, bf16[14,128,512]{2,1,0:T(8,128)(2,1)S(1)}, f32[128,128]{1,0:T(8,128)S(1)}) custom-call(s32[56,128]{1,0:T(8,128)S(1)} %bitcast.17, s32[56,128]{1,0:T(8,128)S(1)} %bitcast.15), custom_call_target="tpu_custom_call" | custom-call | flops 1000000000 | bytes 1000000 | tf_op jit(solution)/shard_map/pallas_call | solution.py:797
  17.1 1.0 %shard_map.162 = (f32[168,128]{1,0:T(8,128)S(1)}, f32[56,128]{1,0:T(8,128)S(1)}, f32[448,128]{1,0:T(8,128)S(1)}, f32[448,128]{1,0:T(8,128)S(1)}, f32[128,1152]{1...) custom-call(s32[8,128]{1,0:T(8,128)S(1)} %shard_map.158.side_ref, ...), custom_call_target="tpu_custom_call" | custom-call | flops 1000000000 | bytes 1000000 | tf_op jit(solution)/shard_map/pallas_call | solution.py:797
  18.3 2.5 %collective-permute-start.6 = (bf16[64,128]{1,0:T(8,128)(2,1)S(1)}, bf16[64,128]{1,0:T(8,128)(2,1)S(1)}, u32[]{:S(2)}, u32[]{:S(2)}) collective-permute-start(bf16[64,128]{1,0:T(8,128)(2,1)S(1)} %get-tuple-element.68), channel_id=1, source_target_pairs={{0,24},{8,16},{16,8},{24,0},{1,25},{9,17},{17,9},{25,1},{2,26},{10... | collective-permute-start | bytes 49160 | tf_op jit(solution)/shard_map/ppermute | solution.py:819
  21.6 1.2 %shard_map.168 = (f32[14,128,512]{2,1,0:T(8,128)S(1)}, f32[14,128,512]{2,1,0:T(8,128)S(1)}, f32[448,128]{1,0:T(8,128)S(1)}) custom-call(f32[448,128]{1,0:T(8,128)S(1)} %get-tuple-element.76.basis_ref, f32[448,128]{1,0:T(8,128)S(1)} %get-tuple-element.77.slope_ref, f32[168,128]{1,0:T(8,128)S(1)} %get-tuple-element.78.unit_ref, f32[8,128]{1,0:T(8,128)S(1)} %copy-done.5), custom_call_target="tpu_custom_call" | custom-call | flops 1000000000 | bytes 1000000 | tf_op jit(solution)/shard_map/pallas_call | solution.py:797
  22.8 1.1 %collective-permute-done.6.far_ref = bf16[64,128]{1,0:T(8,128)(2,1)S(1)} collective-permute-done((bf16[64,128]{1,0:T(8,128)(2,1)S(1)}, bf16[64,128]{1,0:T(8,128)(2,1)S(1)}, u32[]{:S(2)}, u32[]{:S(2)}) %collective-permute-start.6) | collective-permute-done | bytes 16416 | tf_op jit(solution)/shard_map/ppermute | solution.py:819
  24.2 1.6 %collective-permute-start.8 = (bf16[128,128]{1,0:T(8,128)(2,1)S(1)}, bf16[128,128]{1,0:T(8,128)(2,1)S(1)}, u32[]{:S(2)}, u32[]{:S(2)}) collective-permute-start(bf16[128,128]{1,0:T(8,128)(2,1)S(1)} %get-tuple-element.71), channel_id=1, source_target_pairs={{0,6},{2,4},{4,2},{6,0},{1,7},{3,5},{5,3},{7,1},{8,14},{10,12},{12... | collective-permute-start | bytes 98312 | tf_op jit(solution)/shard_map/ppermute | solution.py:819
  26.4 1.2 %collective-permute-done.8.far_ref = bf16[128,128]{1,0:T(8,128)(2,1)S(1)} collective-permute-done((bf16[128,128]{1,0:T(8,128)(2,1)S(1)}, bf16[128,128]{1,0:T(8,128)(2,1)S(1)}, u32[]{:S(2)}, u32[]{:S(2)}) %collective-permute-start.8) | collective-permute-done | bytes 32800 | tf_op jit(solution)/shard_map/ppermute | solution.py:819
  27.8 1.3 %collective-permute-start.9 = (bf16[128,128]{1,0:T(8,128)(2,1)S(1)}, bf16[128,128]{1,0:T(8,128)(2,1)S(1)}, u32[]{:S(2)}, u32[]{:S(2)}) collective-permute-start(bf16[128,128]{1,0:T(8,128)(2,1)S(1)} %get-tuple-element.72), channel_id=1, source_target_pairs={{0,1},{1,0},{2,3},{3,2},{4,5},{5,4},{6,7},{7,6},{8,9},{9,8},{10,11... | collective-permute-start | bytes 98312 | tf_op jit(solution)/shard_map/ppermute | solution.py:824
  29.1 1.1 %shard_map.167.hg_ref.old_ref = f32[14,128,512]{2,1,0:T(8,128)S(1)} custom-call(bf16[128,128]{1,0:T(8,128)(2,1)S(1)} %get-tuple-element.73.h2_ref, bf16[128,128]{1,0:T(8,128)(2,1)S(1)} %get-tuple-element.74.h3_ref, bf16[14,640,512]{2,1,0:T(8,128)(2,1)S(1)} %get-tuple-element.75.hot_ref, ...), custom_call_target="tpu_custom_call", output_to_operand_aliasing={{}: (3, {})} | custom-call | flops 1000000000 | bytes 1000000 | tf_op jit(solution)/shard_map/pallas_call | solution.py:797
  30.3 2.4 %shard_map.169.acc_ref = f32[9,128,128]{2,1,0:T(8,128)S(1)} custom-call(f32[14,128,512]{2,1,0:T(8,128)S(1)} %shard_map.167.hg_ref.old_ref, f32[14,128,512]{2,1,0:T(8,128)S(1)} %get-tuple-element.79.rad_ref, f32[448,128]{1,0:T(8,128)S(1)} %get-tuple-element.80.y_ref), custom_call_target="tpu_custom_call" | custom-call | flops 1000000000 | bytes 1000000 | tf_op jit(solution)/shard_map/pallas_call | solution.py:797
  32.7 2.0 %shard_map.171 = (f32[1,128]{1,0:T(1,128)S(1)}, f32[9,128,128]{2,1,0:T(8,128)S(1)}, f32[128,128]{1,0:T(8,128)S(1)}, bf16[128,128]{1,0:T(8,128)(2,1)S(1)}) custom-call(bf16[128,128]{1,0:T(8,128)(2,1)S(1)} %get-tuple-element.66.h0_ref, bf16[128,128]{1,0:T(8,128)(2,1)S(1)} %collective-permute-done.9.h4_ref, f32[9,128,128]{2,1,0:T(8,128)S(1)} %shard_map.169.acc_ref, ...), custom_call_target="tpu_custom_call" | custom-call | flops 1000000000 | bytes 1000000 | tf_op jit(solution)/shard_map/pallas_call | solution.py:797
  34.7 3.4 %shard_map.172 = (bf16[14,128,512]{2,1,0:T(8,128)(2,1)S(1)}, f32[14,128,512]{2,1,0:T(8,128)S(1)}, f32[256,128]{1,0:T(8,128)S(1)}) custom-call(f32[9,128,128]{2,1,0:T(8,128)S(1)} %get-tuple-element.85.raw_ref.d_ref, f32[14,128,512]{2,1,0:T(8,128)S(1)} %get-tuple-element.79.rad_ref, f32[448,128]{1,0:T(8,128)S(1)} %get-tuple-element.80.y_ref, ...), custom_call_target="tpu_custom_call" | custom-call | flops 1000000000 | bytes 1000000 | tf_op jit(solution)/shard_map/pallas_call | solution.py:797
  38.1 0.9 %collective-permute-start.10 = (bf16[128,128]{1,0:T(8,128)(2,1)S(1)}, bf16[128,128]{1,0:T(8,128)(2,1)S(1)}, u32[]{:S(2)}, u32[]{:S(2)}) collective-permute-start(bf16[128,128]{1,0:T(8,128)(2,1)S(1)} %get-tuple-element.87), channel_id=1, source_target_pairs={{0,1},{1,0},{2,3},{3,2},{4,5},{5,4},{6,7},{7,6},{8,9},{9,8},{10,11... | collective-permute-start | bytes 98312 | tf_op jit(solution)/shard_map/ppermute | solution.py:824
  39.0 1.1 %shard_map.174.gx_ref = f32[256,128]{1,0:T(8,128)S(1)} custom-call(bf16[14,640,512]{2,1,0:T(8,128)(2,1)S(1)} %get-tuple-element.75.hot_ref, bf16[14,128,512]{2,1,0:T(8,128)(2,1)S(1)} %get-tuple-element.89.rq_ref), custom_call_target="tpu_custom_call" | custom-call | flops 1000000000 | bytes 1000000 | tf_op jit(solution)/shard_map/pallas_call | solution.py:797
  40.1 2.0 %collective-permute-done.10.az_ref = bf16[128,128]{1,0:T(8,128)(2,1)S(1)} collective-permute-done((bf16[128,128]{1,0:T(8,128)(2,1)S(1)}, bf16[128,128]{1,0:T(8,128)(2,1)S(1)}, u32[]{:S(2)}, u32[]{:S(2)}) %collective-permute-start.10) | collective-permute-done | bytes 32800 | tf_op jit(solution)/shard_map/ppermute | solution.py:824
  42.4 1.6 %collective-permute-start.12 = (bf16[128,128]{1,0:T(8,128)(2,1)S(1)}, bf16[128,128]{1,0:T(8,128)(2,1)S(1)}, u32[]{:S(2)}, u32[]{:S(2)}) collective-permute-start(bf16[128,128]{1,0:T(8,128)(2,1)S(1)} %get-tuple-element.92), channel_id=1, source_target_pairs={{0,6},{2,4},{4,2},{6,0},{1,7},{3,5},{5,3},{7,1},{8,14},{10,12},{12... | collective-permute-start | bytes 98312 | tf_op jit(solution)/shard_map/ppermute | solution.py:819
  44.0 4.3 %shard_map.177.gc_ref = f32[192,128]{1,0:T(8,128)S(1)} custom-call(bf16[128,128]{1,0:T(8,128)(2,1)S(1)} %collective-permute-done.9.h4_ref, bf16[14,640,512]{2,1,0:T(8,128)(2,1)S(1)} %get-tuple-element.75.hot_ref, f32[14,128,512]{2,1,0:T(8,128)S(1)} %shard_map.167.hg_ref.old_ref, f32[14,128,512]{2,1,0:T(8,128)S(1)} %get-tuple-element.79.rad_ref, ...), custom_call_target="tpu_custom_call" | custom-call | flops 1000000000 | bytes 1000000 | tf_op jit(solution)/shard_map/pallas_call | solution.py:797
  48.7 2.5 %collective-permute-start.14 = (bf16[64,128]{1,0:T(8,128)(2,1)S(1)}, bf16[64,128]{1,0:T(8,128)(2,1)S(1)}, u32[]{:S(2)}, u32[]{:S(2)}) collective-permute-start(bf16[64,128]{1,0:T(8,128)(2,1)S(1)} %get-tuple-element.95), channel_id=1, source_target_pairs={{0,24},{8,16},{16,8},{24,0},{1,25},{9,17},{17,9},{25,1},{2,26},{10... | collective-permute-start | bytes 49160 | tf_op jit(solution)/shard_map/ppermute | solution.py:819
  52.3 1.9 %collective-permute-done.14.far_ref = bf16[64,128]{1,0:T(8,128)(2,1)S(1)} collective-permute-done((bf16[64,128]{1,0:T(8,128)(2,1)S(1)}, bf16[64,128]{1,0:T(8,128)(2,1)S(1)}, u32[]{:S(2)}, u32[]{:S(2)}) %collective-permute-start.14) | collective-permute-done | bytes 16416 | tf_op jit(solution)/shard_map/ppermute | solution.py:819
  54.2 1.5 %shard_map.178 = (f32[8,128]{1,0:T(8,128)S(1)}, f32[8,128]{1,0:T(8,128)S(1)}, f32[8,128]{1,0:T(8,128)S(1)}, f32[8,128]{1,0:T(8,128)S(1)}, f32[8,128]{1,0:T(8,128)S(1)}) custom-call(s32[8,128]{1,0:T(8,128)S(1)} %shard_map.158.side_ref, f32[128,128]{1,0:T(8,128)S(1)} %get-tuple-element.93.own_ref, bf16[64,128]{1,0:T(8,128)(2,1)S(1)} %collective-permute-done.13.near_ref, ...), custom_call_target="tpu_custom_call" | custom-call | flops 1000000000 | bytes 1000000 | tf_op jit(solution)/shard_map/pallas_call | solution.py:797
  55.7 0.9 %collective-permute-start.15 = (f32[8,128]{1,0:T(8,128)S(1)}, f32[8,128]{1,0:T(8,128)S(1)}, u32[]{:S(2)}, u32[]{:S(2)}) collective-permute-start(f32[8,128]{1,0:T(8,128)S(1)} %get-tuple-element.105), channel_id=1, source_target_pairs={{0,1},{1,0},{2,3},{3,2},{4,5},{5,4},{6,7},{7,6},{8,9},{9,8},{10,11... | collective-permute-start | bytes 12296 | tf_op jit(solution)/shard_map/ppermute | solution.py:824
  56.6 2.8 %collective-permute-done.15.az_ref = f32[8,128]{1,0:T(8,128)S(1)} collective-permute-done((f32[8,128]{1,0:T(8,128)S(1)}, f32[8,128]{1,0:T(8,128)S(1)}, u32[]{:S(2)}, u32[]{:S(2)}) %collective-permute-start.15) | collective-permute-done | bytes 4128 | tf_op jit(solution)/shard_map/ppermute | solution.py:824
  60.7 1.9 %collective-permute-done.17.far_ref = f32[8,128]{1,0:T(8,128)S(1)} collective-permute-done((f32[8,128]{1,0:T(8,128)S(1)}, f32[8,128]{1,0:T(8,128)S(1)}, u32[]{:S(2)}, u32[]{:S(2)}) %collective-permute-start.17) | collective-permute-done | bytes 4128 | tf_op jit(solution)/shard_map/ppermute | solution.py:819
  63.0 2.5 %collective-permute-start.19 = (f32[8,128]{1,0:T(8,128)S(1)}, f32[8,128]{1,0:T(8,128)S(1)}, u32[]{:S(2)}, u32[]{:S(2)}) collective-permute-start(f32[8,128]{1,0:T(8,128)S(1)} %get-tuple-element.110), channel_id=1, source_target_pairs={{0,24},{8,16},{16,8},{24,0},{1,25},{9,17},{17,9},{25,1},{2,26},{10... | collective-permute-start | bytes 12296 | tf_op jit(solution)/shard_map/ppermute | solution.py:819
  65.5 1.0 %collective-permute-done.18.near_ref = f32[8,128]{1,0:T(8,128)S(1)} collective-permute-done((f32[8,128]{1,0:T(8,128)S(1)}, f32[8,128]{1,0:T(8,128)S(1)}, u32[]{:S(2)}, u32[]{:S(2)}) %collective-permute-start.18) | collective-permute-done | bytes 4128 | tf_op jit(solution)/shard_map/ppermute | solution.py:819
  66.5 1.9 %collective-permute-done.19.far_ref = f32[8,128]{1,0:T(8,128)S(1)} collective-permute-done((f32[8,128]{1,0:T(8,128)S(1)}, f32[8,128]{1,0:T(8,128)S(1)}, u32[]{:S(2)}, u32[]{:S(2)}) %collective-permute-start.19) | collective-permute-done | bytes 4128 | tf_op jit(solution)/shard_map/ppermute | solution.py:819
  (62 shorter events, 7.3 us)
Async XLA Ops:
  0.6 9.3 %copy-start.8 = (s32[1,1,1,2,128]{4,3,2,1,0:T(2,128)S(1)}, s32[1,1,1,2,128]{4,3,2,1,0:T(2,128)}, u32[]{:S(2)}) copy-start(s32[1,1,1,2,128]{4,3,2,1,0:T(2,128)} %param.20) | copy-start | bytes 3076
  1.3 11.8 %copy-start.14 = (s32[1,1,1,128]{3,2,1,0:T(1,128)S(1)}, s32[1,1,1,128]{3,2,1,0:T(1,128)}, u32[]{:S(2)}) copy-start(s32[1,1,1,128]{3,2,1,0:T(1,128)} %param.21) | copy-start | bytes 1540
  1.5 5.5 %collective-permute-start = (f32[8,128]{1,0:T(8,128)S(1)}, f32[8,128]{1,0:T(8,128)S(1)}, u32[]{:S(2)}, u32[]{:S(2)}) collective-permute-start(f32[8,128]{1,0:T(8,128)S(1)} %get-tuple-element.59), channel_id=1, source_target_pairs={{0,8},{8,0},{16,24},{24,16},{1,9},{9,1},{17,25},{25,17},{2,10},{10... | collective-permute-start | bytes 12296 | tf_op jit(solution)/shard_map/ppermute | solution.py:819
  4.5 5.4 %collective-permute-start.1 = (f32[8,128]{1,0:T(8,128)S(1)}, f32[8,128]{1,0:T(8,128)S(1)}, u32[]{:S(2)}, u32[]{:S(2)}) collective-permute-start(f32[8,128]{1,0:T(8,128)S(1)} %get-tuple-element.59), channel_id=1, source_target_pairs={{0,24},{8,16},{16,8},{24,0},{1,25},{9,17},{17,9},{25,1},{2,26},{10... | collective-permute-start | bytes 12296 | tf_op jit(solution)/shard_map/ppermute | solution.py:819
  9.9 4.8 %copy-start.2 = (s32[56,1,1,1,128]{4,3,2,1,0:T(1,128)S(1)}, s32[56,1,1,1,128]{4,3,2,1,0:T(1,128)}, u32[]{:S(2)}) copy-start(s32[56,1,1,1,128]{4,3,2,1,0:T(1,128)} %param.18) | copy-start | bytes 86020
  9.9 4.8 %copy-start.3 = (s32[56,1,1,1,128]{4,3,2,1,0:T(1,128)S(1)}, s32[56,1,1,1,128]{4,3,2,1,0:T(1,128)}, u32[]{:S(2)}) copy-start(s32[56,1,1,1,128]{4,3,2,1,0:T(1,128)} %param.17) | copy-start | bytes 86020
  10.1 1.6 %collective-permute-start.2 = (f32[8,128]{1,0:T(8,128)S(1)}, f32[8,128]{1,0:T(8,128)S(1)}, u32[]{:S(2)}, u32[]{:S(2)}) collective-permute-start(f32[8,128]{1,0:T(8,128)S(1)} %get-tuple-element.61), channel_id=1, source_target_pairs={{0,2},{2,0},{4,6},{6,4},{1,3},{3,1},{5,7},{7,5},{8,10},{10,8},{12,... | collective-permute-start | bytes 12296 | tf_op jit(solution)/shard_map/ppermute | solution.py:819
  10.1 3.1 %collective-permute-start.3 = (f32[8,128]{1,0:T(8,128)S(1)}, f32[8,128]{1,0:T(8,128)S(1)}, u32[]{:S(2)}, u32[]{:S(2)}) collective-permute-start(f32[8,128]{1,0:T(8,128)S(1)} %get-tuple-element.62), channel_id=1, source_target_pairs={{0,6},{2,4},{4,2},{6,0},{1,7},{3,5},{5,3},{7,1},{8,14},{10,12},{12... | collective-permute-start | bytes 12296 | tf_op jit(solution)/shard_map/ppermute | solution.py:819
  13.1 4.0 %copy-start.1 = (bf16[384,128]{1,0:T(8,128)(2,1)S(1)}, bf16[384,128]{1,0:T(8,128)(2,1)}, u32[]{:S(2)}) copy-start(bf16[384,128]{1,0:T(8,128)(2,1)} %mix_ref.5) | copy-start | bytes 294916
  13.1 4.0 %copy-start.6 = (f32[8,128]{1,0:T(8,128)S(1)}, f32[8,128]{1,0:T(8,128)}, u32[]{:S(2)}) copy-start(f32[8,128]{1,0:T(8,128)} %radial_ref.9) | copy-start | bytes 12292
  13.1 4.0 %copy-start.10 = (f32[128]{0:T(128)S(1)}, f32[128]{0:T(128)}, u32[]{:S(2)}) copy-start(f32[128]{0:T(128)} %param.24) | copy-start | bytes 1540
  13.2 3.9 %collective-permute-start.4 = (f32[8,128]{1,0:T(8,128)S(1)}, f32[8,128]{1,0:T(8,128)S(1)}, u32[]{:S(2)}, u32[]{:S(2)}) collective-permute-start(f32[8,128]{1,0:T(8,128)S(1)} %get-tuple-element.65), channel_id=1, source_target_pairs={{0,1},{1,0},{2,3},{3,2},{4,5},{5,4},{6,7},{7,6},{8,9},{9,8},{10,11... | collective-permute-start | bytes 12296 | tf_op jit(solution)/shard_map/ppermute | solution.py:824
  14.8 6.1 %copy-start.5 = (f32[8,128]{1,0:T(8,128)S(1)}, f32[8,128]{1,0:T(8,128)}, u32[]{:S(2)}) copy-start(f32[8,128]{1,0:T(8,128)} %radial_ref.8) | copy-start | bytes 12292
  18.2 4.6 %collective-permute-start.5 = (bf16[64,128]{1,0:T(8,128)(2,1)S(1)}, bf16[64,128]{1,0:T(8,128)(2,1)S(1)}, u32[]{:S(2)}, u32[]{:S(2)}) collective-permute-start(bf16[64,128]{1,0:T(8,128)(2,1)S(1)} %get-tuple-element.67), channel_id=1, source_target_pairs={{0,8},{8,0},{16,24},{24,16},{1,9},{9,1},{17,25},{25,17},{2,10},{10... | collective-permute-start | bytes 49160 | tf_op jit(solution)/shard_map/ppermute | solution.py:819
  18.3 5.6 %collective-permute-start.6 = (bf16[64,128]{1,0:T(8,128)(2,1)S(1)}, bf16[64,128]{1,0:T(8,128)(2,1)S(1)}, u32[]{:S(2)}, u32[]{:S(2)}) collective-permute-start(bf16[64,128]{1,0:T(8,128)(2,1)S(1)} %get-tuple-element.68), channel_id=1, source_target_pairs={{0,24},{8,16},{16,8},{24,0},{1,25},{9,17},{17,9},{25,1},{2,26},{10... | collective-permute-start | bytes 49160 | tf_op jit(solution)/shard_map/ppermute | solution.py:819
  24.1 2.3 %collective-permute-start.7 = (bf16[128,128]{1,0:T(8,128)(2,1)S(1)}, bf16[128,128]{1,0:T(8,128)(2,1)S(1)}, u32[]{:S(2)}, u32[]{:S(2)}) collective-permute-start(bf16[128,128]{1,0:T(8,128)(2,1)S(1)} %get-tuple-element.70), channel_id=1, source_target_pairs={{0,2},{2,0},{4,6},{6,4},{1,3},{3,1},{5,7},{7,5},{8,10},{10,8},{12,... | collective-permute-start | bytes 98312 | tf_op jit(solution)/shard_map/ppermute | solution.py:819
  24.2 3.4 %collective-permute-start.8 = (bf16[128,128]{1,0:T(8,128)(2,1)S(1)}, bf16[128,128]{1,0:T(8,128)(2,1)S(1)}, u32[]{:S(2)}, u32[]{:S(2)}) collective-permute-start(bf16[128,128]{1,0:T(8,128)(2,1)S(1)} %get-tuple-element.71), channel_id=1, source_target_pairs={{0,6},{2,4},{4,2},{6,0},{1,7},{3,5},{5,3},{7,1},{8,14},{10,12},{12... | collective-permute-start | bytes 98312 | tf_op jit(solution)/shard_map/ppermute | solution.py:819
  27.8 4.9 %collective-permute-start.9 = (bf16[128,128]{1,0:T(8,128)(2,1)S(1)}, bf16[128,128]{1,0:T(8,128)(2,1)S(1)}, u32[]{:S(2)}, u32[]{:S(2)}) collective-permute-start(bf16[128,128]{1,0:T(8,128)(2,1)S(1)} %get-tuple-element.72), channel_id=1, source_target_pairs={{0,1},{1,0},{2,3},{3,2},{4,5},{5,4},{6,7},{7,6},{8,9},{9,8},{10,11... | collective-permute-start | bytes 98312 | tf_op jit(solution)/shard_map/ppermute | solution.py:824
  30.2 2.4 %copy-start = (bf16[384,128]{1,0:T(8,128)(2,1)S(1)}, bf16[384,128]{1,0:T(8,128)(2,1)}, u32[]{:S(2)}) copy-start(bf16[384,128]{1,0:T(8,128)(2,1)} %mix_ref.4) | copy-start | bytes 294916
  30.2 2.4 %copy-start.4 = (f32[128,16]{0,1:T(8,128)S(1)}, f32[128,16]{0,1:T(8,128)}, u32[]{:S(2)}) copy-start(f32[128,16]{0,1:T(8,128)} %param.28) | copy-start | bytes 24580
  30.2 2.4 %copy-start.11 = (s32[1,1,1,128]{3,2,1,0:T(1,128)S(1)}, s32[1,1,1,128]{3,2,1,0:T(1,128)}, u32[]{:S(2)}) copy-start(s32[1,1,1,128]{3,2,1,0:T(1,128)} %param.16) | copy-start | bytes 1540
  30.3 2.4 %copy-start.12 = (f32[128]{0:T(128)S(1)}, f32[128]{0:T(128)}, u32[]{:S(2)}) copy-start(f32[128]{0:T(128)} %param.27) | copy-start | bytes 1540
  38.1 4.0 %collective-permute-start.10 = (bf16[128,128]{1,0:T(8,128)(2,1)S(1)}, bf16[128,128]{1,0:T(8,128)(2,1)S(1)}, u32[]{:S(2)}, u32[]{:S(2)}) collective-permute-start(bf16[128,128]{1,0:T(8,128)(2,1)S(1)} %get-tuple-element.87), channel_id=1, source_target_pairs={{0,1},{1,0},{2,3},{3,2},{4,5},{5,4},{6,7},{7,6},{8,9},{9,8},{10,11... | collective-permute-start | bytes 98312 | tf_op jit(solution)/shard_map/ppermute | solution.py:824
  42.3 6.0 %collective-permute-start.11 = (bf16[128,128]{1,0:T(8,128)(2,1)S(1)}, bf16[128,128]{1,0:T(8,128)(2,1)S(1)}, u32[]{:S(2)}, u32[]{:S(2)}) collective-permute-start(bf16[128,128]{1,0:T(8,128)(2,1)S(1)} %get-tuple-element.91), channel_id=1, source_target_pairs={{0,2},{2,0},{4,6},{6,4},{1,3},{3,1},{5,7},{7,5},{8,10},{10,8},{12,... | collective-permute-start | bytes 98312 | tf_op jit(solution)/shard_map/ppermute | solution.py:819
  42.4 5.9 %collective-permute-start.12 = (bf16[128,128]{1,0:T(8,128)(2,1)S(1)}, bf16[128,128]{1,0:T(8,128)(2,1)S(1)}, u32[]{:S(2)}, u32[]{:S(2)}) collective-permute-start(bf16[128,128]{1,0:T(8,128)(2,1)S(1)} %get-tuple-element.92), channel_id=1, source_target_pairs={{0,6},{2,4},{4,2},{6,0},{1,7},{3,5},{5,3},{7,1},{8,14},{10,12},{12... | collective-permute-start | bytes 98312 | tf_op jit(solution)/shard_map/ppermute | solution.py:819
  48.4 3.8 %collective-permute-start.13 = (bf16[64,128]{1,0:T(8,128)(2,1)S(1)}, bf16[64,128]{1,0:T(8,128)(2,1)S(1)}, u32[]{:S(2)}, u32[]{:S(2)}) collective-permute-start(bf16[64,128]{1,0:T(8,128)(2,1)S(1)} %get-tuple-element.94), channel_id=1, source_target_pairs={{0,8},{8,0},{16,24},{24,16},{1,9},{9,1},{17,25},{25,17},{2,10},{10... | collective-permute-start | bytes 49160 | tf_op jit(solution)/shard_map/ppermute | solution.py:819
  48.7 5.5 %collective-permute-start.14 = (bf16[64,128]{1,0:T(8,128)(2,1)S(1)}, bf16[64,128]{1,0:T(8,128)(2,1)S(1)}, u32[]{:S(2)}, u32[]{:S(2)}) collective-permute-start(bf16[64,128]{1,0:T(8,128)(2,1)S(1)} %get-tuple-element.95), channel_id=1, source_target_pairs={{0,24},{8,16},{16,8},{24,0},{1,25},{9,17},{17,9},{25,1},{2,26},{10... | collective-permute-start | bytes 49160 | tf_op jit(solution)/shard_map/ppermute | solution.py:819
  55.7 3.7 %collective-permute-start.15 = (f32[8,128]{1,0:T(8,128)S(1)}, f32[8,128]{1,0:T(8,128)S(1)}, u32[]{:S(2)}, u32[]{:S(2)}) collective-permute-start(f32[8,128]{1,0:T(8,128)S(1)} %get-tuple-element.105), channel_id=1, source_target_pairs={{0,1},{1,0},{2,3},{3,2},{4,5},{5,4},{6,7},{7,6},{8,9},{9,8},{10,11... | collective-permute-start | bytes 12296 | tf_op jit(solution)/shard_map/ppermute | solution.py:824
  59.5 1.2 %collective-permute-start.16 = (f32[8,128]{1,0:T(8,128)S(1)}, f32[8,128]{1,0:T(8,128)S(1)}, u32[]{:S(2)}, u32[]{:S(2)}) collective-permute-start(f32[8,128]{1,0:T(8,128)S(1)} %get-tuple-element.107), channel_id=1, source_target_pairs={{0,2},{2,0},{4,6},{6,4},{1,3},{3,1},{5,7},{7,5},{8,10},{10,8},{12,... | collective-permute-start | bytes 12296 | tf_op jit(solution)/shard_map/ppermute | solution.py:819
  59.6 3.1 %collective-permute-start.17 = (f32[8,128]{1,0:T(8,128)S(1)}, f32[8,128]{1,0:T(8,128)S(1)}, u32[]{:S(2)}, u32[]{:S(2)}) collective-permute-start(f32[8,128]{1,0:T(8,128)S(1)} %get-tuple-element.108), channel_id=1, source_target_pairs={{0,6},{2,4},{4,2},{6,0},{1,7},{3,5},{5,3},{7,1},{8,14},{10,12},{12... | collective-permute-start | bytes 12296 | tf_op jit(solution)/shard_map/ppermute | solution.py:819
  62.9 3.6 %collective-permute-start.18 = (f32[8,128]{1,0:T(8,128)S(1)}, f32[8,128]{1,0:T(8,128)S(1)}, u32[]{:S(2)}, u32[]{:S(2)}) collective-permute-start(f32[8,128]{1,0:T(8,128)S(1)} %get-tuple-element.110), channel_id=1, source_target_pairs={{0,8},{8,0},{16,24},{24,16},{1,9},{9,1},{17,25},{25,17},{2,10},{10... | collective-permute-start | bytes 12296 | tf_op jit(solution)/shard_map/ppermute | solution.py:819
  63.0 5.4 %collective-permute-start.19 = (f32[8,128]{1,0:T(8,128)S(1)}, f32[8,128]{1,0:T(8,128)S(1)}, u32[]{:S(2)}, u32[]{:S(2)}) collective-permute-start(f32[8,128]{1,0:T(8,128)S(1)} %get-tuple-element.110), channel_id=1, source_target_pairs={{0,24},{8,16},{16,8},{24,0},{1,25},{9,17},{17,9},{25,1},{2,26},{10... | collective-permute-start | bytes 12296 | tf_op jit(solution)/shard_map/ppermute | solution.py:819
  (3 other events, 3.8 us)

commit v6 on v5

--- a/solution.py
+++ b/solution.py
@@ -525,18 +525,13 @@
             parts.append(dot(hot_ref[at, 2 * atoms : 4 * atoms, :], rq_ref[at], 1, 1))
         return parts[0] + parts[1]
 
-    gy_ref[...] = jnp.zeros_like(gy_ref)
-    reverse(0)
-    reverse(1)
-
-    def body(trip, carry):
-        gy_ref[...] += scatter(2 * trip)
-        for part in range(2):
-            reverse(2 * trip + 2 + part)
-        return carry
-
-    lax.fori_loop(0, steps // 2 - 1, body, 0)
-    gy_ref[...] += scatter(steps - 2)
+    total = None
+    for step in range(0, steps, 2):
+        reverse(step)
+        reverse(step + 1)
+        part = scatter(step)
+        total = part if total is None else total + part
+    gy_ref[...] = total
 
 
 def scatter_kernel(first, hot_ref, rq_ref, out_ref):

time: 69.3 us -> 69.3 us (level)
  no operation moved by 1% of the time
where the time goes in v6:
time: 69.3 us; the launch traced here: 69.1 us
  Pallas kernels  24.8 us (36%)
  starting transfers between devices  23.5 us (34%)
  waiting for transfers between devices  19.1 us (28%)
  between operations  0.98 us (1%)
  local copies, waits for them, and re-layouts  0.7 us (1%)
    pallas_call x24, Pallas kernels, call(): pl.pallas_call(kernel, out_shape=shapes, in_specs=specs, out_specs=[pl.Bl...  24.8 us
    ppermute x16, starting transfers between devices, pair_swap(): return lax.ppermute(x, axis, pairs)  19 us
    ppermute x16, waiting for transfers between devices, pair_swap(): return lax.ppermute(x, axis, pairs)  14.3 us
    ppermute x4, waiting for transfers between devices, partner(): lax.ppermute(x, axis, [(i, i ^ 1) for i in range(lax.axis_size(axis))])  4.85 us
    ppermute x4, starting transfers between devices, partner(): lax.ppermute(x, axis, [(i, i ^ 1) for i in range(lax.axis_size(axis))])  4.53 us
  transfers between devices with their start and end apart: 20, of which 12 were waited for; matrix products, arithmetic and copies ran while one was open for 0% of the time, Pallas kernels for 21%

profile of v6, /device:TPU:0, one launch (start us, length us, event | category | flops | bytes accessed | tf_op | source)
XLA Modules:
  0.0 69.1 jit_solution(17566117971151855870)
XLA Ops:
  1.5 3.1 %collective-permute-start = (f32[8,128]{1,0:T(8,128)S(1)}, f32[8,128]{1,0:T(8,128)S(1)}, u32[]{:S(2)}, u32[]{:S(2)}) collective-permute-start(f32[8,128]{1,0:T(8,128)S(1)} %get-tuple-element.59), channel_id=1, source_target_pairs={{0,8},{8,0},{16,24},{24,16},{1,9},{9,1},{17,25},{25,17},{2,10},{10... | collective-permute-start | bytes 12296 | tf_op jit(solution)/shard_map/ppermute | solution.py:814
  4.5 2.5 %collective-permute-start.1 = (f32[8,128]{1,0:T(8,128)S(1)}, f32[8,128]{1,0:T(8,128)S(1)}, u32[]{:S(2)}, u32[]{:S(2)}) collective-permute-start(f32[8,128]{1,0:T(8,128)S(1)} %get-tuple-element.59), channel_id=1, source_target_pairs={{0,24},{8,16},{16,8},{24,0},{1,25},{9,17},{17,9},{25,1},{2,26},{10... | collective-permute-start | bytes 12296 | tf_op jit(solution)/shard_map/ppermute | solution.py:814
  7.0 2.9 %collective-permute-done.1.far_ref = f32[8,128]{1,0:T(8,128)S(1)} collective-permute-done((f32[8,128]{1,0:T(8,128)S(1)}, f32[8,128]{1,0:T(8,128)S(1)}, u32[]{:S(2)}, u32[]{:S(2)}) %collective-permute-start.1) | collective-permute-done | bytes 4128 | tf_op jit(solution)/shard_map/ppermute | solution.py:814
  10.1 1.6 %collective-permute-start.3 = (f32[8,128]{1,0:T(8,128)S(1)}, f32[8,128]{1,0:T(8,128)S(1)}, u32[]{:S(2)}, u32[]{:S(2)}) collective-permute-start(f32[8,128]{1,0:T(8,128)S(1)} %get-tuple-element.62), channel_id=1, source_target_pairs={{0,6},{2,4},{4,2},{6,0},{1,7},{3,5},{5,3},{7,1},{8,14},{10,12},{12... | collective-permute-start | bytes 12296 | tf_op jit(solution)/shard_map/ppermute | solution.py:814
  11.7 1.4 %collective-permute-done.3.far_ref = f32[8,128]{1,0:T(8,128)S(1)} collective-permute-done((f32[8,128]{1,0:T(8,128)S(1)}, f32[8,128]{1,0:T(8,128)S(1)}, u32[]{:S(2)}, u32[]{:S(2)}) %collective-permute-start.3) | collective-permute-done | bytes 4128 | tf_op jit(solution)/shard_map/ppermute | solution.py:814
  13.2 1.5 %collective-permute-start.4 = (f32[8,128]{1,0:T(8,128)S(1)}, f32[8,128]{1,0:T(8,128)S(1)}, u32[]{:S(2)}, u32[]{:S(2)}) collective-permute-start(f32[8,128]{1,0:T(8,128)S(1)} %get-tuple-element.65), channel_id=1, source_target_pairs={{0,1},{1,0},{2,3},{3,2},{4,5},{5,4},{6,7},{7,6},{8,9},{9,8},{10,11... | collective-permute-start | bytes 12296 | tf_op jit(solution)/shard_map/ppermute | solution.py:819
  14.8 2.3 %shard_map.165 = (bf16[14,640,512]{2,1,0:T(8,128)(2,1)S(1)}, bf16[14,128,512]{2,1,0:T(8,128)(2,1)S(1)}, f32[128,128]{1,0:T(8,128)S(1)}) custom-call(s32[56,128]{1,0:T(8,128)S(1)} %bitcast.17, s32[56,128]{1,0:T(8,128)S(1)} %bitcast.15), custom_call_target="tpu_custom_call" | custom-call | flops 1000000000 | bytes 1000000 | tf_op jit(solution)/shard_map/pallas_call | solution.py:792
  17.1 1.0 %shard_map.162 = (f32[168,128]{1,0:T(8,128)S(1)}, f32[56,128]{1,0:T(8,128)S(1)}, f32[448,128]{1,0:T(8,128)S(1)}, f32[448,128]{1,0:T(8,128)S(1)}, f32[128,1152]{1...) custom-call(s32[8,128]{1,0:T(8,128)S(1)} %shard_map.158.side_ref, ...), custom_call_target="tpu_custom_call" | custom-call | flops 1000000000 | bytes 1000000 | tf_op jit(solution)/shard_map/pallas_call | solution.py:792
  18.3 2.5 %collective-permute-start.6 = (bf16[64,128]{1,0:T(8,128)(2,1)S(1)}, bf16[64,128]{1,0:T(8,128)(2,1)S(1)}, u32[]{:S(2)}, u32[]{:S(2)}) collective-permute-start(bf16[64,128]{1,0:T(8,128)(2,1)S(1)} %get-tuple-element.68), channel_id=1, source_target_pairs={{0,24},{8,16},{16,8},{24,0},{1,25},{9,17},{17,9},{25,1},{2,26},{10... | collective-permute-start | bytes 49160 | tf_op jit(solution)/shard_map/ppermute | solution.py:814
  21.6 1.2 %shard_map.168 = (f32[14,128,512]{2,1,0:T(8,128)S(1)}, f32[14,128,512]{2,1,0:T(8,128)S(1)}, f32[448,128]{1,0:T(8,128)S(1)}) custom-call(f32[448,128]{1,0:T(8,128)S(1)} %get-tuple-element.76.basis_ref, f32[448,128]{1,0:T(8,128)S(1)} %get-tuple-element.77.slope_ref, f32[168,128]{1,0:T(8,128)S(1)} %get-tuple-element.78.unit_ref, f32[8,128]{1,0:T(8,128)S(1)} %copy-done.5), custom_call_target="tpu_custom_call" | custom-call | flops 1000000000 | bytes 1000000 | tf_op jit(solution)/shard_map/pallas_call | solution.py:792
  22.8 1.1 %collective-permute-done.6.far_ref = bf16[64,128]{1,0:T(8,128)(2,1)S(1)} collective-permute-done((bf16[64,128]{1,0:T(8,128)(2,1)S(1)}, bf16[64,128]{1,0:T(8,128)(2,1)S(1)}, u32[]{:S(2)}, u32[]{:S(2)}) %collective-permute-start.6) | collective-permute-done | bytes 16416 | tf_op jit(solution)/shard_map/ppermute | solution.py:814
  24.2 1.6 %collective-permute-start.8 = (bf16[128,128]{1,0:T(8,128)(2,1)S(1)}, bf16[128,128]{1,0:T(8,128)(2,1)S(1)}, u32[]{:S(2)}, u32[]{:S(2)}) collective-permute-start(bf16[128,128]{1,0:T(8,128)(2,1)S(1)} %get-tuple-element.71), channel_id=1, source_target_pairs={{0,6},{2,4},{4,2},{6,0},{1,7},{3,5},{5,3},{7,1},{8,14},{10,12},{12... | collective-permute-start | bytes 98312 | tf_op jit(solution)/shard_map/ppermute | solution.py:814
  26.5 1.1 %collective-permute-done.8.far_ref = bf16[128,128]{1,0:T(8,128)(2,1)S(1)} collective-permute-done((bf16[128,128]{1,0:T(8,128)(2,1)S(1)}, bf16[128,128]{1,0:T(8,128)(2,1)S(1)}, u32[]{:S(2)}, u32[]{:S(2)}) %collective-permute-start.8) | collective-permute-done | bytes 32800 | tf_op jit(solution)/shard_map/ppermute | solution.py:814
  27.8 1.3 %collective-permute-start.9 = (bf16[128,128]{1,0:T(8,128)(2,1)S(1)}, bf16[128,128]{1,0:T(8,128)(2,1)S(1)}, u32[]{:S(2)}, u32[]{:S(2)}) collective-permute-start(bf16[128,128]{1,0:T(8,128)(2,1)S(1)} %get-tuple-element.72), channel_id=1, source_target_pairs={{0,1},{1,0},{2,3},{3,2},{4,5},{5,4},{6,7},{7,6},{8,9},{9,8},{10,11... | collective-permute-start | bytes 98312 | tf_op jit(solution)/shard_map/ppermute | solution.py:819
  29.1 1.1 %shard_map.167.hg_ref.old_ref = f32[14,128,512]{2,1,0:T(8,128)S(1)} custom-call(bf16[128,128]{1,0:T(8,128)(2,1)S(1)} %get-tuple-element.73.h2_ref, bf16[128,128]{1,0:T(8,128)(2,1)S(1)} %get-tuple-element.74.h3_ref, bf16[14,640,512]{2,1,0:T(8,128)(2,1)S(1)} %get-tuple-element.75.hot_ref, ...), custom_call_target="tpu_custom_call", output_to_operand_aliasing={{}: (3, {})} | custom-call | flops 1000000000 | bytes 1000000 | tf_op jit(solution)/shard_map/pallas_call | solution.py:792
  30.3 2.4 %shard_map.169.acc_ref = f32[9,128,128]{2,1,0:T(8,128)S(1)} custom-call(f32[14,128,512]{2,1,0:T(8,128)S(1)} %shard_map.167.hg_ref.old_ref, f32[14,128,512]{2,1,0:T(8,128)S(1)} %get-tuple-element.79.rad_ref, f32[448,128]{1,0:T(8,128)S(1)} %get-tuple-element.80.y_ref), custom_call_target="tpu_custom_call" | custom-call | flops 1000000000 | bytes 1000000 | tf_op jit(solution)/shard_map/pallas_call | solution.py:792
  32.7 2.0 %shard_map.171 = (f32[1,128]{1,0:T(1,128)S(1)}, f32[9,128,128]{2,1,0:T(8,128)S(1)}, f32[128,128]{1,0:T(8,128)S(1)}, bf16[128,128]{1,0:T(8,128)(2,1)S(1)}) custom-call(bf16[128,128]{1,0:T(8,128)(2,1)S(1)} %get-tuple-element.66.h0_ref, bf16[128,128]{1,0:T(8,128)(2,1)S(1)} %collective-permute-done.9.h4_ref, f32[9,128,128]{2,1,0:T(8,128)S(1)} %shard_map.169.acc_ref, ...), custom_call_target="tpu_custom_call" | custom-call | flops 1000000000 | bytes 1000000 | tf_op jit(solution)/shard_map/pallas_call | solution.py:792
  34.7 3.2 %shard_map.172 = (bf16[14,128,512]{2,1,0:T(8,128)(2,1)S(1)}, f32[14,128,512]{2,1,0:T(8,128)S(1)}, f32[256,128]{1,0:T(8,128)S(1)}) custom-call(f32[9,128,128]{2,1,0:T(8,128)S(1)} %get-tuple-element.85.raw_ref.d_ref, f32[14,128,512]{2,1,0:T(8,128)S(1)} %get-tuple-element.79.rad_ref, f32[448,128]{1,0:T(8,128)S(1)} %get-tuple-element.80.y_ref, ...), custom_call_target="tpu_custom_call" | custom-call | flops 1000000000 | bytes 1000000 | tf_op jit(solution)/shard_map/pallas_call | solution.py:792
  37.9 0.9 %collective-permute-start.10 = (bf16[128,128]{1,0:T(8,128)(2,1)S(1)}, bf16[128,128]{1,0:T(8,128)(2,1)S(1)}, u32[]{:S(2)}, u32[]{:S(2)}) collective-permute-start(bf16[128,128]{1,0:T(8,128)(2,1)S(1)} %get-tuple-element.87), channel_id=1, source_target_pairs={{0,1},{1,0},{2,3},{3,2},{4,5},{5,4},{6,7},{7,6},{8,9},{9,8},{10,11... | collective-permute-start | bytes 98312 | tf_op jit(solution)/shard_map/ppermute | solution.py:819
  38.7 1.1 %shard_map.174.gx_ref = f32[256,128]{1,0:T(8,128)S(1)} custom-call(bf16[14,640,512]{2,1,0:T(8,128)(2,1)S(1)} %get-tuple-element.75.hot_ref, bf16[14,128,512]{2,1,0:T(8,128)(2,1)S(1)} %get-tuple-element.89.rq_ref), custom_call_target="tpu_custom_call" | custom-call | flops 1000000000 | bytes 1000000 | tf_op jit(solution)/shard_map/pallas_call | solution.py:792
  39.8 2.0 %collective-permute-done.10.az_ref = bf16[128,128]{1,0:T(8,128)(2,1)S(1)} collective-permute-done((bf16[128,128]{1,0:T(8,128)(2,1)S(1)}, bf16[128,128]{1,0:T(8,128)(2,1)S(1)}, u32[]{:S(2)}, u32[]{:S(2)}) %collective-permute-start.10) | collective-permute-done | bytes 32800 | tf_op jit(solution)/shard_map/ppermute | solution.py:819
  42.1 1.6 %collective-permute-start.12 = (bf16[128,128]{1,0:T(8,128)(2,1)S(1)}, bf16[128,128]{1,0:T(8,128)(2,1)S(1)}, u32[]{:S(2)}, u32[]{:S(2)}) collective-permute-start(bf16[128,128]{1,0:T(8,128)(2,1)S(1)} %get-tuple-element.92), channel_id=1, source_target_pairs={{0,6},{2,4},{4,2},{6,0},{1,7},{3,5},{5,3},{7,1},{8,14},{10,12},{12... | collective-permute-start | bytes 98312 | tf_op jit(solution)/shard_map/ppermute | solution.py:814
  43.7 4.5 %shard_map.177.gc_ref = f32[192,128]{1,0:T(8,128)S(1)} custom-call(bf16[128,128]{1,0:T(8,128)(2,1)S(1)} %collective-permute-done.9.h4_ref, bf16[14,640,512]{2,1,0:T(8,128)(2,1)S(1)} %get-tuple-element.75.hot_ref, f32[14,128,512]{2,1,0:T(8,128)S(1)} %shard_map.167.hg_ref.old_ref, f32[14,128,512]{2,1,0:T(8,128)S(1)} %get-tuple-element.79.rad_ref, ...), custom_call_target="tpu_custom_call" | custom-call | flops 1000000000 | bytes 1000000 | tf_op jit(solution)/shard_map/pallas_call | solution.py:792
  48.6 2.5 %collective-permute-start.14 = (bf16[64,128]{1,0:T(8,128)(2,1)S(1)}, bf16[64,128]{1,0:T(8,128)(2,1)S(1)}, u32[]{:S(2)}, u32[]{:S(2)}) collective-permute-start(bf16[64,128]{1,0:T(8,128)(2,1)S(1)} %get-tuple-element.95), channel_id=1, source_target_pairs={{0,24},{8,16},{16,8},{24,0},{1,25},{9,17},{17,9},{25,1},{2,26},{10... | collective-permute-start | bytes 49160 | tf_op jit(solution)/shard_map/ppermute | solution.py:814
  52.2 2.0 %collective-permute-done.14.far_ref = bf16[64,128]{1,0:T(8,128)(2,1)S(1)} collective-permute-done((bf16[64,128]{1,0:T(8,128)(2,1)S(1)}, bf16[64,128]{1,0:T(8,128)(2,1)S(1)}, u32[]{:S(2)}, u32[]{:S(2)}) %collective-permute-start.14) | collective-permute-done | bytes 16416 | tf_op jit(solution)/shard_map/ppermute | solution.py:814
  54.2 1.5 %shard_map.178 = (f32[8,128]{1,0:T(8,128)S(1)}, f32[8,128]{1,0:T(8,128)S(1)}, f32[8,128]{1,0:T(8,128)S(1)}, f32[8,128]{1,0:T(8,128)S(1)}, f32[8,128]{1,0:T(8,128)S(1)}) custom-call(s32[8,128]{1,0:T(8,128)S(1)} %shard_map.158.side_ref, f32[128,128]{1,0:T(8,128)S(1)} %get-tuple-element.93.own_ref, bf16[64,128]{1,0:T(8,128)(2,1)S(1)} %collective-permute-done.13.near_ref, ...), custom_call_target="tpu_custom_call" | custom-call | flops 1000000000 | bytes 1000000 | tf_op jit(solution)/shard_map/pallas_call | solution.py:792
  55.7 0.8 %collective-permute-start.15 = (f32[8,128]{1,0:T(8,128)S(1)}, f32[8,128]{1,0:T(8,128)S(1)}, u32[]{:S(2)}, u32[]{:S(2)}) collective-permute-start(f32[8,128]{1,0:T(8,128)S(1)} %get-tuple-element.105), channel_id=1, source_target_pairs={{0,1},{1,0},{2,3},{3,2},{4,5},{5,4},{6,7},{7,6},{8,9},{9,8},{10,11... | collective-permute-start | bytes 12296 | tf_op jit(solution)/shard_map/ppermute | solution.py:819
  56.5 2.8 %collective-permute-done.15.az_ref = f32[8,128]{1,0:T(8,128)S(1)} collective-permute-done((f32[8,128]{1,0:T(8,128)S(1)}, f32[8,128]{1,0:T(8,128)S(1)}, u32[]{:S(2)}, u32[]{:S(2)}) %collective-permute-start.15) | collective-permute-done | bytes 4128 | tf_op jit(solution)/shard_map/ppermute | solution.py:819
  60.7 1.9 %collective-permute-done.17.far_ref = f32[8,128]{1,0:T(8,128)S(1)} collective-permute-done((f32[8,128]{1,0:T(8,128)S(1)}, f32[8,128]{1,0:T(8,128)S(1)}, u32[]{:S(2)}, u32[]{:S(2)}) %collective-permute-start.17) | collective-permute-done | bytes 4128 | tf_op jit(solution)/shard_map/ppermute | solution.py:814
  62.9 2.5 %collective-permute-start.19 = (f32[8,128]{1,0:T(8,128)S(1)}, f32[8,128]{1,0:T(8,128)S(1)}, u32[]{:S(2)}, u32[]{:S(2)}) collective-permute-start(f32[8,128]{1,0:T(8,128)S(1)} %get-tuple-element.110), channel_id=1, source_target_pairs={{0,24},{8,16},{16,8},{24,0},{1,25},{9,17},{17,9},{25,1},{2,26},{10... | collective-permute-start | bytes 12296 | tf_op jit(solution)/shard_map/ppermute | solution.py:814
  65.4 1.1 %collective-permute-done.18.near_ref = f32[8,128]{1,0:T(8,128)S(1)} collective-permute-done((f32[8,128]{1,0:T(8,128)S(1)}, f32[8,128]{1,0:T(8,128)S(1)}, u32[]{:S(2)}, u32[]{:S(2)}) %collective-permute-start.18) | collective-permute-done | bytes 4128 | tf_op jit(solution)/shard_map/ppermute | solution.py:814
  66.5 1.9 %collective-permute-done.19.far_ref = f32[8,128]{1,0:T(8,128)S(1)} collective-permute-done((f32[8,128]{1,0:T(8,128)S(1)}, f32[8,128]{1,0:T(8,128)S(1)}, u32[]{:S(2)}, u32[]{:S(2)}) %collective-permute-start.19) | collective-permute-done | bytes 4128 | tf_op jit(solution)/shard_map/ppermute | solution.py:814
  (62 shorter events, 7.2 us)
Async XLA Ops:
  0.6 9.3 %copy-start.8 = (s32[1,1,1,2,128]{4,3,2,1,0:T(2,128)S(1)}, s32[1,1,1,2,128]{4,3,2,1,0:T(2,128)}, u32[]{:S(2)}) copy-start(s32[1,1,1,2,128]{4,3,2,1,0:T(2,128)} %param.20) | copy-start | bytes 3076
  1.3 11.8 %copy-start.14 = (s32[1,1,1,128]{3,2,1,0:T(1,128)S(1)}, s32[1,1,1,128]{3,2,1,0:T(1,128)}, u32[]{:S(2)}) copy-start(s32[1,1,1,128]{3,2,1,0:T(1,128)} %param.21) | copy-start | bytes 1540
  1.5 5.5 %collective-permute-start = (f32[8,128]{1,0:T(8,128)S(1)}, f32[8,128]{1,0:T(8,128)S(1)}, u32[]{:S(2)}, u32[]{:S(2)}) collective-permute-start(f32[8,128]{1,0:T(8,128)S(1)} %get-tuple-element.59), channel_id=1, source_target_pairs={{0,8},{8,0},{16,24},{24,16},{1,9},{9,1},{17,25},{25,17},{2,10},{10... | collective-permute-start | bytes 12296 | tf_op jit(solution)/shard_map/ppermute | solution.py:814
  4.5 5.4 %collective-permute-start.1 = (f32[8,128]{1,0:T(8,128)S(1)}, f32[8,128]{1,0:T(8,128)S(1)}, u32[]{:S(2)}, u32[]{:S(2)}) collective-permute-start(f32[8,128]{1,0:T(8,128)S(1)} %get-tuple-element.59), channel_id=1, source_target_pairs={{0,24},{8,16},{16,8},{24,0},{1,25},{9,17},{17,9},{25,1},{2,26},{10... | collective-permute-start | bytes 12296 | tf_op jit(solution)/shard_map/ppermute | solution.py:814
  9.9 4.8 %copy-start.2 = (s32[56,1,1,1,128]{4,3,2,1,0:T(1,128)S(1)}, s32[56,1,1,1,128]{4,3,2,1,0:T(1,128)}, u32[]{:S(2)}) copy-start(s32[56,1,1,1,128]{4,3,2,1,0:T(1,128)} %param.18) | copy-start | bytes 86020
  9.9 4.8 %copy-start.3 = (s32[56,1,1,1,128]{4,3,2,1,0:T(1,128)S(1)}, s32[56,1,1,1,128]{4,3,2,1,0:T(1,128)}, u32[]{:S(2)}) copy-start(s32[56,1,1,1,128]{4,3,2,1,0:T(1,128)} %param.17) | copy-start | bytes 86020
  10.1 1.6 %collective-permute-start.2 = (f32[8,128]{1,0:T(8,128)S(1)}, f32[8,128]{1,0:T(8,128)S(1)}, u32[]{:S(2)}, u32[]{:S(2)}) collective-permute-start(f32[8,128]{1,0:T(8,128)S(1)} %get-tuple-element.61), channel_id=1, source_target_pairs={{0,2},{2,0},{4,6},{6,4},{1,3},{3,1},{5,7},{7,5},{8,10},{10,8},{12,... | collective-permute-start | bytes 12296 | tf_op jit(solution)/shard_map/ppermute | solution.py:814
  10.1 3.1 %collective-permute-start.3 = (f32[8,128]{1,0:T(8,128)S(1)}, f32[8,128]{1,0:T(8,128)S(1)}, u32[]{:S(2)}, u32[]{:S(2)}) collective-permute-start(f32[8,128]{1,0:T(8,128)S(1)} %get-tuple-element.62), channel_id=1, source_target_pairs={{0,6},{2,4},{4,2},{6,0},{1,7},{3,5},{5,3},{7,1},{8,14},{10,12},{12... | collective-permute-start | bytes 12296 | tf_op jit(solution)/shard_map/ppermute | solution.py:814
  13.1 4.0 %copy-start.1 = (bf16[384,128]{1,0:T(8,128)(2,1)S(1)}, bf16[384,128]{1,0:T(8,128)(2,1)}, u32[]{:S(2)}) copy-start(bf16[384,128]{1,0:T(8,128)(2,1)} %mix_ref.5) | copy-start | bytes 294916
  13.1 4.0 %copy-start.6 = (f32[8,128]{1,0:T(8,128)S(1)}, f32[8,128]{1,0:T(8,128)}, u32[]{:S(2)}) copy-start(f32[8,128]{1,0:T(8,128)} %radial_ref.9) | copy-start | bytes 12292
  13.1 4.0 %copy-start.10 = (f32[128]{0:T(128)S(1)}, f32[128]{0:T(128)}, u32[]{:S(2)}) copy-start(f32[128]{0:T(128)} %param.24) | copy-start | bytes 1540
  13.2 3.9 %collective-permute-start.4 = (f32[8,128]{1,0:T(8,128)S(1)}, f32[8,128]{1,0:T(8,128)S(1)}, u32[]{:S(2)}, u32[]{:S(2)}) collective-permute-start(f32[8,128]{1,0:T(8,128)S(1)} %get-tuple-element.65), channel_id=1, source_target_pairs={{0,1},{1,0},{2,3},{3,2},{4,5},{5,4},{6,7},{7,6},{8,9},{9,8},{10,11... | collective-permute-start | bytes 12296 | tf_op jit(solution)/shard_map/ppermute | solution.py:819
  14.8 6.1 %copy-start.5 = (f32[8,128]{1,0:T(8,128)S(1)}, f32[8,128]{1,0:T(8,128)}, u32[]{:S(2)}) copy-start(f32[8,128]{1,0:T(8,128)} %radial_ref.8) | copy-start | bytes 12292
  18.2 4.6 %collective-permute-start.5 = (bf16[64,128]{1,0:T(8,128)(2,1)S(1)}, bf16[64,128]{1,0:T(8,128)(2,1)S(1)}, u32[]{:S(2)}, u32[]{:S(2)}) collective-permute-start(bf16[64,128]{1,0:T(8,128)(2,1)S(1)} %get-tuple-element.67), channel_id=1, source_target_pairs={{0,8},{8,0},{16,24},{24,16},{1,9},{9,1},{17,25},{25,17},{2,10},{10... | collective-permute-start | bytes 49160 | tf_op jit(solution)/shard_map/ppermute | solution.py:814
  18.3 5.6 %collective-permute-start.6 = (bf16[64,128]{1,0:T(8,128)(2,1)S(1)}, bf16[64,128]{1,0:T(8,128)(2,1)S(1)}, u32[]{:S(2)}, u32[]{:S(2)}) collective-permute-start(bf16[64,128]{1,0:T(8,128)(2,1)S(1)} %get-tuple-element.68), channel_id=1, source_target_pairs={{0,24},{8,16},{16,8},{24,0},{1,25},{9,17},{17,9},{25,1},{2,26},{10... | collective-permute-start | bytes 49160 | tf_op jit(solution)/shard_map/ppermute | solution.py:814
  24.1 2.3 %collective-permute-start.7 = (bf16[128,128]{1,0:T(8,128)(2,1)S(1)}, bf16[128,128]{1,0:T(8,128)(2,1)S(1)}, u32[]{:S(2)}, u32[]{:S(2)}) collective-permute-start(bf16[128,128]{1,0:T(8,128)(2,1)S(1)} %get-tuple-element.70), channel_id=1, source_target_pairs={{0,2},{2,0},{4,6},{6,4},{1,3},{3,1},{5,7},{7,5},{8,10},{10,8},{12,... | collective-permute-start | bytes 98312 | tf_op jit(solution)/shard_map/ppermute | solution.py:814
  24.2 3.4 %collective-permute-start.8 = (bf16[128,128]{1,0:T(8,128)(2,1)S(1)}, bf16[128,128]{1,0:T(8,128)(2,1)S(1)}, u32[]{:S(2)}, u32[]{:S(2)}) collective-permute-start(bf16[128,128]{1,0:T(8,128)(2,1)S(1)} %get-tuple-element.71), channel_id=1, source_target_pairs={{0,6},{2,4},{4,2},{6,0},{1,7},{3,5},{5,3},{7,1},{8,14},{10,12},{12... | collective-permute-start | bytes 98312 | tf_op jit(solution)/shard_map/ppermute | solution.py:814
  27.8 4.9 %collective-permute-start.9 = (bf16[128,128]{1,0:T(8,128)(2,1)S(1)}, bf16[128,128]{1,0:T(8,128)(2,1)S(1)}, u32[]{:S(2)}, u32[]{:S(2)}) collective-permute-start(bf16[128,128]{1,0:T(8,128)(2,1)S(1)} %get-tuple-element.72), channel_id=1, source_target_pairs={{0,1},{1,0},{2,3},{3,2},{4,5},{5,4},{6,7},{7,6},{8,9},{9,8},{10,11... | collective-permute-start | bytes 98312 | tf_op jit(solution)/shard_map/ppermute | solution.py:819
  30.2 2.4 %copy-start = (bf16[384,128]{1,0:T(8,128)(2,1)S(1)}, bf16[384,128]{1,0:T(8,128)(2,1)}, u32[]{:S(2)}) copy-start(bf16[384,128]{1,0:T(8,128)(2,1)} %mix_ref.4) | copy-start | bytes 294916
  30.2 2.4 %copy-start.4 = (f32[128,16]{0,1:T(8,128)S(1)}, f32[128,16]{0,1:T(8,128)}, u32[]{:S(2)}) copy-start(f32[128,16]{0,1:T(8,128)} %param.28) | copy-start | bytes 24580
  30.2 2.4 %copy-start.11 = (s32[1,1,1,128]{3,2,1,0:T(1,128)S(1)}, s32[1,1,1,128]{3,2,1,0:T(1,128)}, u32[]{:S(2)}) copy-start(s32[1,1,1,128]{3,2,1,0:T(1,128)} %param.16) | copy-start | bytes 1540
  30.3 2.4 %copy-start.12 = (f32[128]{0:T(128)S(1)}, f32[128]{0:T(128)}, u32[]{:S(2)}) copy-start(f32[128]{0:T(128)} %param.27) | copy-start | bytes 1540
  37.9 4.0 %collective-permute-start.10 = (bf16[128,128]{1,0:T(8,128)(2,1)S(1)}, bf16[128,128]{1,0:T(8,128)(2,1)S(1)}, u32[]{:S(2)}, u32[]{:S(2)}) collective-permute-start(bf16[128,128]{1,0:T(8,128)(2,1)S(1)} %get-tuple-element.87), channel_id=1, source_target_pairs={{0,1},{1,0},{2,3},{3,2},{4,5},{5,4},{6,7},{7,6},{8,9},{9,8},{10,11... | collective-permute-start | bytes 98312 | tf_op jit(solution)/shard_map/ppermute | solution.py:819
  42.1 6.1 %collective-permute-start.11 = (bf16[128,128]{1,0:T(8,128)(2,1)S(1)}, bf16[128,128]{1,0:T(8,128)(2,1)S(1)}, u32[]{:S(2)}, u32[]{:S(2)}) collective-permute-start(bf16[128,128]{1,0:T(8,128)(2,1)S(1)} %get-tuple-element.91), channel_id=1, source_target_pairs={{0,2},{2,0},{4,6},{6,4},{1,3},{3,1},{5,7},{7,5},{8,10},{10,8},{12,... | collective-permute-start | bytes 98312 | tf_op jit(solution)/shard_map/ppermute | solution.py:814
  42.1 6.1 %collective-permute-start.12 = (bf16[128,128]{1,0:T(8,128)(2,1)S(1)}, bf16[128,128]{1,0:T(8,128)(2,1)S(1)}, u32[]{:S(2)}, u32[]{:S(2)}) collective-permute-start(bf16[128,128]{1,0:T(8,128)(2,1)S(1)} %get-tuple-element.92), channel_id=1, source_target_pairs={{0,6},{2,4},{4,2},{6,0},{1,7},{3,5},{5,3},{7,1},{8,14},{10,12},{12... | collective-permute-start | bytes 98312 | tf_op jit(solution)/shard_map/ppermute | solution.py:814
  48.4 3.8 %collective-permute-start.13 = (bf16[64,128]{1,0:T(8,128)(2,1)S(1)}, bf16[64,128]{1,0:T(8,128)(2,1)S(1)}, u32[]{:S(2)}, u32[]{:S(2)}) collective-permute-start(bf16[64,128]{1,0:T(8,128)(2,1)S(1)} %get-tuple-element.94), channel_id=1, source_target_pairs={{0,8},{8,0},{16,24},{24,16},{1,9},{9,1},{17,25},{25,17},{2,10},{10... | collective-permute-start | bytes 49160 | tf_op jit(solution)/shard_map/ppermute | solution.py:814
  48.6 5.5 %collective-permute-start.14 = (bf16[64,128]{1,0:T(8,128)(2,1)S(1)}, bf16[64,128]{1,0:T(8,128)(2,1)S(1)}, u32[]{:S(2)}, u32[]{:S(2)}) collective-permute-start(bf16[64,128]{1,0:T(8,128)(2,1)S(1)} %get-tuple-element.95), channel_id=1, source_target_pairs={{0,24},{8,16},{16,8},{24,0},{1,25},{9,17},{17,9},{25,1},{2,26},{10... | collective-permute-start | bytes 49160 | tf_op jit(solution)/shard_map/ppermute | solution.py:814
  55.7 3.7 %collective-permute-start.15 = (f32[8,128]{1,0:T(8,128)S(1)}, f32[8,128]{1,0:T(8,128)S(1)}, u32[]{:S(2)}, u32[]{:S(2)}) collective-permute-start(f32[8,128]{1,0:T(8,128)S(1)} %get-tuple-element.105), channel_id=1, source_target_pairs={{0,1},{1,0},{2,3},{3,2},{4,5},{5,4},{6,7},{7,6},{8,9},{9,8},{10,11... | collective-permute-start | bytes 12296 | tf_op jit(solution)/shard_map/ppermute | solution.py:819
  59.5 1.2 %collective-permute-start.16 = (f32[8,128]{1,0:T(8,128)S(1)}, f32[8,128]{1,0:T(8,128)S(1)}, u32[]{:S(2)}, u32[]{:S(2)}) collective-permute-start(f32[8,128]{1,0:T(8,128)S(1)} %get-tuple-element.107), channel_id=1, source_target_pairs={{0,2},{2,0},{4,6},{6,4},{1,3},{3,1},{5,7},{7,5},{8,10},{10,8},{12,... | collective-permute-start | bytes 12296 | tf_op jit(solution)/shard_map/ppermute | solution.py:814
  59.5 3.1 %collective-permute-start.17 = (f32[8,128]{1,0:T(8,128)S(1)}, f32[8,128]{1,0:T(8,128)S(1)}, u32[]{:S(2)}, u32[]{:S(2)}) collective-permute-start(f32[8,128]{1,0:T(8,128)S(1)} %get-tuple-element.108), channel_id=1, source_target_pairs={{0,6},{2,4},{4,2},{6,0},{1,7},{3,5},{5,3},{7,1},{8,14},{10,12},{12... | collective-permute-start | bytes 12296 | tf_op jit(solution)/shard_map/ppermute | solution.py:814
  62.9 3.6 %collective-permute-start.18 = (f32[8,128]{1,0:T(8,128)S(1)}, f32[8,128]{1,0:T(8,128)S(1)}, u32[]{:S(2)}, u32[]{:S(2)}) collective-permute-start(f32[8,128]{1,0:T(8,128)S(1)} %get-tuple-element.110), channel_id=1, source_target_pairs={{0,8},{8,0},{16,24},{24,16},{1,9},{9,1},{17,25},{25,17},{2,10},{10... | collective-permute-start | bytes 12296 | tf_op jit(solution)/shard_map/ppermute | solution.py:814
  62.9 5.4 %collective-permute-start.19 = (f32[8,128]{1,0:T(8,128)S(1)}, f32[8,128]{1,0:T(8,128)S(1)}, u32[]{:S(2)}, u32[]{:S(2)}) collective-permute-start(f32[8,128]{1,0:T(8,128)S(1)} %get-tuple-element.110), channel_id=1, source_target_pairs={{0,24},{8,16},{16,8},{24,0},{1,25},{9,17},{17,9},{25,1},{2,26},{10... | collective-permute-start | bytes 12296 | tf_op jit(solution)/shard_map/ppermute | solution.py:814
  (3 other events, 3.8 us)
